TPU v7x, 32 devices: a whole 2x2x4 slice. The times are simulated.
32 devices in a mesh: dp: 4 (over z), row: 2 (over y), col: 4 (over x, core).
Axes of the slice: x: 2, y: 2, z: 4, core: 2. Of those that a mesh axis runs over, the one named last changes fastest.
Arguments:
- tokens: bfloat16 [4096, 2048], P(('dp', 'row'), 'col'), may hold values from -6 to 6
- w_query: bfloat16 [2048, 2048], P(('dp', 'row'), 'col'), may hold values from -0.125 to 0.125
- key_matrix: bfloat16 [2048, 1024], P(('dp', 'row'), 'col'), may hold values from -0.125 to 0.125
- value_matrix: bfloat16 [2048, 1024], P(('dp', 'row'), 'col'), may hold values from -0.125 to 0.125
- w_output: bfloat16 [2048, 2048], P('col', ('dp', 'row')), may hold values from -1 to 1
- w_gate: bfloat16 [2048, 8192], P(('dp', 'row'), 'col'), may hold values from -0.125 to 0.125
- w_up: bfloat16 [2048, 8192], P(('dp', 'row'), 'col'), may hold values from -0.125 to 0.125
- w_down: bfloat16 [8192, 2048], P('col', ('dp', 'row')), may hold values from -0.0625 to 0.0625
- gain_attn: bfloat16 [2048], P(('dp', 'row')), may hold values from 0.5 to 1.5
- gain_ffn: bfloat16 [2048], P(('dp', 'row')), may hold values from 0.5 to 1.5
- lengths: int32 [4], P('dp'), may hold values from 256 to 1024, as said below
- cotangent: bfloat16 [4096, 2048], P(('dp', 'row'), 'col'), may hold values from -6 to 6
Outputs:
- layer_out: bfloat16 [4096, 2048], P(('dp', 'row'), 'col')
- grad_tokens: bfloat16 [4096, 2048], P(('dp', 'row'), 'col')
- grad_gain_attn: float32 [2048], P(('dp', 'row'))
- grad_gain_ffn: float32 [2048], P(('dp', 'row'))
- grad_query: float32 [2048, 2048], P(('dp', 'row'), 'col')
- grad_key: float32 [2048, 1024], P(('dp', 'row'), 'col')
- grad_value: float32 [2048, 1024], P(('dp', 'row'), 'col')
- grad_output: float32 [2048, 2048], P('col', ('dp', 'row'))
- grad_gate: float32 [2048, 8192], P(('dp', 'row'), 'col')
- grad_up: float32 [2048, 8192], P(('dp', 'row'), 'col')
- grad_down: float32 [8192, 2048], P('col', ('dp', 'row'))
Inputs may be any that keep to these rules, and one draw needn't show every extreme that they name: lengths[s] counts the valid leading positions of sequence s; in every draw some sequence fills all 1024 positions.
All inputs are finite; a program needn't handle non-finite values.
Results may differ from a plain program's by a relative error of at most 0.025.
Values may be sent and summed in bfloat16 or wider, within the bound.
A program may use at most 192 MiB of HBM per device.

v0:
```python
import math

import jax
import jax.numpy as jnp
from jax import lax
from jax.sharding import PartitionSpec as P

QUERY_HEADS = 8
KEY_VALUE_HEADS = 4
HEAD_SIZE = 256


EPSILON = 1e-06
ROPE_BASE = 1000042.0


def rope_tables(positions):
    half = HEAD_SIZE // 2
    freq = ROPE_BASE ** (-jnp.arange(half, dtype=jnp.float32) * 2.0 / HEAD_SIZE)
    angle = positions[:, None] * freq[None, :]
    return (jnp.cos(angle), jnp.sin(angle))


def rotary_apply(values, cosine_table, sine_table):
    half = values.shape[-1] // 2
    first = values[..., :half]
    second = values[..., half:]
    cos_part = cosine_table[:, None, :]
    sin_part = sine_table[:, None, :]
    return jnp.concatenate(
        [first * cos_part - second * sin_part, second * cos_part + first * sin_part], axis=-1
    )


def rotate_back(grads, cosine_table, sine_table):
    half = grads.shape[-1] // 2
    first = grads[..., :half]
    second = grads[..., half:]
    cos_part = cosine_table[:, None, :]
    sin_part = sine_table[:, None, :]
    return jnp.concatenate(
        [first * cos_part + second * sin_part, second * cos_part - first * sin_part], axis=-1
    )


def norm_rows(full, gain):
    factor = lax.rsqrt(jnp.mean(full * full, axis=1, keepdims=True) + EPSILON)
    return (factor, (full * factor * gain).astype(jnp.bfloat16))


def norm_back(full, factor, gain, grad):
    inner = jnp.mean(gain * grad * full, axis=1, keepdims=True)
    back = factor * gain * grad - full * factor * factor * factor * inner
    gain_grad = jnp.sum(grad * full * factor, axis=0)
    return (back, gain_grad)


def contract_rows(left, right):
    return lax.dot_general(
        left, right, (((0,), (0,)), ((), ())), preferred_element_type=jnp.float32
    )


def times_transposed(left, right):
    return lax.dot_general(
        left, right, (((1,), (1,)), ((), ())), preferred_element_type=jnp.float32
    )


def masked_scores(query_rows, key_part, query_pos, index, key_block, score_scale):
    scores = (
        jnp.einsum("hgqd,khd->hgqk", query_rows, key_part, preferred_element_type=jnp.float32)
        * score_scale
    )
    key_pos = index * key_block + jnp.arange(key_block, dtype=jnp.int32)
    return jnp.where(key_pos[None, :] <= query_pos[:, None], scores, -1e30)


def attend(query_rows, keys, values, query_pos, key_block, score_scale):
    heads, query_group, token_count, size = query_rows.shape
    blocks = keys.shape[0] // key_block
    key_parts = keys.reshape(blocks, key_block, heads, size)
    value_parts = values.reshape(blocks, key_block, heads, size)
    indices = jnp.arange(blocks, dtype=jnp.int32)

    def totals(carry, item):
        top, total = carry
        key_part, index = item
        scores = masked_scores(query_rows, key_part, query_pos, index, key_block, score_scale)
        new_top = jnp.maximum(top, jnp.max(scores, axis=-1))
        total = total * jnp.exp(top - new_top) + jnp.sum(
            jnp.exp(scores - new_top[..., None]), axis=-1
        )
        return ((new_top, total), None)

    start = (
        jnp.full((heads, query_group, token_count), -1e30, jnp.float32),
        jnp.zeros((heads, query_group, token_count), jnp.float32),
    )
    (top, total), unused = lax.scan(totals, start, (key_parts, indices))
    log_total = top + jnp.log(total)

    def mixing(accum, item):
        key_part, value_part, index = item
        scores = masked_scores(query_rows, key_part, query_pos, index, key_block, score_scale)
        probs = jnp.exp(scores - log_total[..., None]).astype(jnp.bfloat16)
        return (
            accum
            + jnp.einsum("hgqk,khd->hgqd", probs, value_part, preferred_element_type=jnp.float32),
            None,
        )

    accum, unused = lax.scan(
        mixing,
        jnp.zeros((heads, query_group, token_count, size), jnp.float32),
        (key_parts, value_parts, indices),
    )
    return (accum, log_total)


def attend_back(
    query_rows, keys, values, query_pos, key_block, score_scale, log_total, delta, grad_out
):
    heads, query_group, token_count, size = query_rows.shape
    blocks = keys.shape[0] // key_block
    key_parts = keys.reshape(blocks, key_block, heads, size)
    value_parts = values.reshape(blocks, key_block, heads, size)

    def step(grad_query, item):
        key_part, value_part, index = item
        scores = masked_scores(query_rows, key_part, query_pos, index, key_block, score_scale)
        probs = jnp.exp(scores - log_total[..., None])
        probs_low = probs.astype(jnp.bfloat16)
        grad_probs = jnp.einsum(
            "hgqd,khd->hgqk", grad_out, value_part, preferred_element_type=jnp.float32
        )
        grad_scores = (probs * (grad_probs - delta[..., None]) * score_scale).astype(jnp.bfloat16)
        grad_query = grad_query + jnp.einsum(
            "hgqk,khd->hgqd", grad_scores, key_part, preferred_element_type=jnp.float32
        )
        grad_key = jnp.einsum(
            "hgqk,hgqd->khd", grad_scores, query_rows, preferred_element_type=jnp.float32
        )
        grad_value = jnp.einsum(
            "hgqk,hgqd->khd", probs_low, grad_out, preferred_element_type=jnp.float32
        )
        return (grad_query, (grad_key, grad_value))

    grad_query, (grad_keys, grad_values) = lax.scan(
        step,
        jnp.zeros((heads, query_group, token_count, size), jnp.float32),
        (key_parts, value_parts, jnp.arange(blocks, dtype=jnp.int32)),
    )
    return (
        grad_query,
        grad_keys.reshape(blocks * key_block, heads * size),
        grad_values.reshape(blocks * key_block, heads * size),
    )


def row_grads(value):
    return lax.all_gather(value, "col", axis=1, tiled=True)


def col_total(value):
    return lax.psum(value.astype(jnp.bfloat16), "col").astype(jnp.float32)


def per_device(
    tokens,
    w_query,
    key_matrix,
    value_matrix,
    w_output,
    w_gate,
    w_up,
    w_down,
    gain_attn,
    gain_ffn,
    lengths,
    cotangent,
):
    row_count = tokens.shape[0]
    slot_size = row_count * lax.axis_size("row")
    key_block = min(512, slot_size)
    col_width = tokens.shape[1]
    col_start = lax.axis_index("col") * col_width
    query_group = QUERY_HEADS // KEY_VALUE_HEADS
    score_scale = 1.0 / math.sqrt(HEAD_SIZE)
    query_pos = lax.axis_index("row") * row_count + jnp.arange(row_count, dtype=jnp.int32)
    valid = (query_pos < lengths[0]).astype(jnp.float32)[:, None]
    cosine_table, sine_table = rope_tables(query_pos.astype(jnp.float32))
    x_full = lax.all_gather(tokens, "col", axis=1, tiled=True).astype(jnp.float32)
    full_query, full_key, full_value, full_gate, full_up, full_gain_attn, full_gain_ffn = (
        lax.all_gather(w_query, ("dp", "row"), axis=0, tiled=True),
        lax.all_gather(key_matrix, ("dp", "row"), axis=0, tiled=True),
        lax.all_gather(value_matrix, ("dp", "row"), axis=0, tiled=True),
        lax.all_gather(w_gate, ("dp", "row"), axis=0, tiled=True),
        lax.all_gather(w_up, ("dp", "row"), axis=0, tiled=True),
        lax.all_gather(gain_attn, ("dp", "row"), axis=0, tiled=True),
        lax.all_gather(gain_ffn, ("dp", "row"), axis=0, tiled=True),
    )
    full_output, full_down = (
        lax.all_gather(w_output, ("dp", "row"), axis=1, tiled=True),
        lax.all_gather(w_down, ("dp", "row"), axis=1, tiled=True),
    )
    gain_one = full_gain_attn.astype(jnp.float32)
    gain_two = full_gain_ffn.astype(jnp.float32)
    factor_one, normed = norm_rows(x_full, gain_one)
    query_raw = jnp.dot(normed, full_query, preferred_element_type=jnp.float32)
    unrotated_key = jnp.dot(normed, full_key, preferred_element_type=jnp.float32)
    value_local = jnp.dot(normed, full_value, preferred_element_type=jnp.float32).astype(
        jnp.bfloat16
    )
    kv_heads = full_key.shape[1] // HEAD_SIZE
    query_rot = rotary_apply(
        query_raw.reshape(row_count, kv_heads * query_group, HEAD_SIZE), cosine_table, sine_table
    ).astype(jnp.bfloat16)
    key_rot = rotary_apply(
        unrotated_key.reshape(row_count, kv_heads, HEAD_SIZE), cosine_table, sine_table
    ).astype(jnp.bfloat16)
    keys_all, values_all = (
        lax.all_gather(key_rot.reshape(row_count, kv_heads * HEAD_SIZE), "row", axis=0, tiled=True),
        lax.all_gather(value_local, "row", axis=0, tiled=True),
    )
    keys_all = keys_all.reshape(slot_size, kv_heads, HEAD_SIZE)
    values_all = values_all.reshape(slot_size, kv_heads, HEAD_SIZE)
    query_rows = query_rot.reshape(row_count, kv_heads, query_group, HEAD_SIZE).transpose(
        1, 2, 0, 3
    )
    attended, log_total = attend(
        query_rows, keys_all, values_all, query_pos, key_block, score_scale
    )
    mixed_heads = (
        attended.transpose(2, 0, 1, 3).reshape(row_count, kv_heads * query_group * HEAD_SIZE)
        * valid
    ).astype(jnp.bfloat16)
    attn_part = lax.psum_scatter(
        jnp.dot(mixed_heads, full_output, preferred_element_type=jnp.float32).astype(jnp.bfloat16),
        "col",
        scatter_dimension=1,
        tiled=True,
    ).astype(jnp.float32)
    residual = tokens.astype(jnp.float32) + attn_part
    residual_full = lax.all_gather(residual.astype(jnp.bfloat16), "col", axis=1, tiled=True).astype(
        residual.dtype
    )
    factor_two, normed_two = norm_rows(residual_full, gain_two)
    gate = jnp.dot(normed_two, full_gate, preferred_element_type=jnp.float32)
    upward = jnp.dot(normed_two, full_up, preferred_element_type=jnp.float32)
    sigmoid_gate = jax.nn.sigmoid(gate)
    silu_gate = gate * sigmoid_gate
    hidden = (silu_gate * upward).astype(jnp.bfloat16)
    ffn_part = lax.psum_scatter(
        jnp.dot(hidden, full_down, preferred_element_type=jnp.float32).astype(jnp.bfloat16),
        "col",
        scatter_dimension=1,
        tiled=True,
    ).astype(jnp.float32)
    layer_out = (residual + ffn_part).astype(jnp.bfloat16)
    full_query, full_key, full_value, full_gate, full_up, full_gain_attn, full_gain_ffn = (
        lax.all_gather(w_query, ("dp", "row"), axis=0, tiled=True),
        lax.all_gather(key_matrix, ("dp", "row"), axis=0, tiled=True),
        lax.all_gather(value_matrix, ("dp", "row"), axis=0, tiled=True),
        lax.all_gather(w_gate, ("dp", "row"), axis=0, tiled=True),
        lax.all_gather(w_up, ("dp", "row"), axis=0, tiled=True),
        lax.all_gather(gain_attn, ("dp", "row"), axis=0, tiled=True),
        lax.all_gather(gain_ffn, ("dp", "row"), axis=0, tiled=True),
    )
    full_output, full_down = (
        lax.all_gather(w_output, ("dp", "row"), axis=1, tiled=True),
        lax.all_gather(w_down, ("dp", "row"), axis=1, tiled=True),
    )
    gain_one = full_gain_attn.astype(jnp.float32)
    gain_two = full_gain_ffn.astype(jnp.float32)
    grad_out = cotangent.astype(jnp.float32) * valid
    grad_out_full = row_grads(grad_out.astype(jnp.bfloat16))
    grad_hidden = times_transposed(grad_out_full, full_down)
    grad_gate_act = (
        grad_hidden * upward * sigmoid_gate * (1.0 + gate * (1.0 - sigmoid_gate))
    ).astype(jnp.bfloat16)
    grad_up_act = (grad_hidden * silu_gate).astype(jnp.bfloat16)
    grad_down_part = contract_rows(grad_out_full, hidden)
    grad_gate_part = contract_rows(normed_two, grad_gate_act)
    grad_up_part = contract_rows(normed_two, grad_up_act)
    grad_normed_two = col_total(
        times_transposed(grad_gate_act, full_gate) + times_transposed(grad_up_act, full_up)
    )
    back_two, gain_two_grad = norm_back(residual_full, factor_two, gain_two, grad_normed_two)
    grad_residual = (grad_out + lax.dynamic_slice_in_dim(back_two, col_start, col_width, 1)).astype(
        jnp.bfloat16
    )
    grad_residual_full = row_grads(grad_residual)
    grad_output_part = contract_rows(grad_residual_full, mixed_heads)
    grad_mixed = (times_transposed(grad_residual_full, full_output) * valid).astype(jnp.bfloat16)
    grad_heads = grad_mixed.reshape(row_count, kv_heads, query_group, HEAD_SIZE).transpose(
        1, 2, 0, 3
    )
    delta = jnp.sum(grad_heads.astype(jnp.float32) * attended, axis=-1)
    grad_query_rot, grad_keys_all, grad_values_all = attend_back(
        query_rows,
        keys_all,
        values_all,
        query_pos,
        key_block,
        score_scale,
        log_total,
        delta,
        grad_heads,
    )
    grad_keys_own, grad_values_own = (
        lax.psum_scatter(
            grad_keys_all.astype(jnp.bfloat16), "row", scatter_dimension=0, tiled=True
        ).astype(jnp.float32),
        lax.psum_scatter(
            grad_values_all.astype(jnp.bfloat16), "row", scatter_dimension=0, tiled=True
        ).astype(jnp.float32),
    )
    grad_query_raw = (
        rotate_back(
            grad_query_rot.transpose(2, 0, 1, 3).reshape(
                row_count, kv_heads * query_group, HEAD_SIZE
            ),
            cosine_table,
            sine_table,
        )
        .reshape(row_count, kv_heads * query_group * HEAD_SIZE)
        .astype(jnp.bfloat16)
    )
    grad_key_raw = (
        rotate_back(grad_keys_own.reshape(row_count, kv_heads, HEAD_SIZE), cosine_table, sine_table)
        .reshape(row_count, kv_heads * HEAD_SIZE)
        .astype(jnp.bfloat16)
    )
    grad_value_raw = grad_values_own.astype(jnp.bfloat16)
    grad_query_part = contract_rows(normed, grad_query_raw)
    grad_key_part = contract_rows(normed, grad_key_raw)
    grad_value_part = contract_rows(normed, grad_value_raw)
    grad_normed = col_total(
        times_transposed(grad_query_raw, full_query)
        + times_transposed(grad_key_raw, full_key)
        + times_transposed(grad_value_raw, full_value)
    )
    back_one, gain_one_grad = norm_back(x_full, factor_one, gain_one, grad_normed)
    grad_tokens = (
        grad_residual.astype(jnp.float32)
        + lax.dynamic_slice_in_dim(back_one, col_start, col_width, 1)
    ).astype(jnp.bfloat16)
    summed = (
        lax.psum_scatter(
            grad_query_part.astype(jnp.bfloat16), ("dp", "row"), scatter_dimension=0, tiled=True
        ).astype(jnp.float32),
        lax.psum_scatter(
            grad_key_part.astype(jnp.bfloat16), ("dp", "row"), scatter_dimension=0, tiled=True
        ).astype(jnp.float32),
        lax.psum_scatter(
            grad_value_part.astype(jnp.bfloat16), ("dp", "row"), scatter_dimension=0, tiled=True
        ).astype(jnp.float32),
        lax.psum_scatter(
            grad_output_part.astype(jnp.bfloat16), ("dp", "row"), scatter_dimension=0, tiled=True
        ).astype(jnp.float32),
        lax.psum_scatter(
            grad_gate_part.astype(jnp.bfloat16), ("dp", "row"), scatter_dimension=0, tiled=True
        ).astype(jnp.float32),
        lax.psum_scatter(
            grad_up_part.astype(jnp.bfloat16), ("dp", "row"), scatter_dimension=0, tiled=True
        ).astype(jnp.float32),
        lax.psum_scatter(
            grad_down_part.astype(jnp.bfloat16), ("dp", "row"), scatter_dimension=0, tiled=True
        ).astype(jnp.float32),
        lax.psum_scatter(
            gain_one_grad.astype(jnp.bfloat16), ("dp", "row"), scatter_dimension=0, tiled=True
        ).astype(jnp.float32),
        lax.psum_scatter(
            gain_two_grad.astype(jnp.bfloat16), ("dp", "row"), scatter_dimension=0, tiled=True
        ).astype(jnp.float32),
    )
    return (
        layer_out,
        grad_tokens,
        summed[7],
        summed[8],
        summed[0],
        summed[1],
        summed[2],
        summed[3].T,
        summed[4],
        summed[5],
        summed[6].T,
    )


def solution(mesh):
    in_specs = (
        P(("dp", "row"), "col"),
        P(("dp", "row"), "col"),
        P(("dp", "row"), "col"),
        P(("dp", "row"), "col"),
        P("col", ("dp", "row")),
        P(("dp", "row"), "col"),
        P(("dp", "row"), "col"),
        P("col", ("dp", "row")),
        P(("dp", "row")),
        P(("dp", "row")),
        P("dp"),
        P(("dp", "row"), "col"),
    )
    out_specs = (
        P(("dp", "row"), "col"),
        P(("dp", "row"), "col"),
        P(("dp", "row")),
        P(("dp", "row")),
        P(("dp", "row"), "col"),
        P(("dp", "row"), "col"),
        P(("dp", "row"), "col"),
        P("col", ("dp", "row")),
        P(("dp", "row"), "col"),
        P(("dp", "row"), "col"),
        P("col", ("dp", "row")),
    )
    return jax.shard_map(
        per_device, mesh=mesh, in_specs=in_specs, out_specs=out_specs, check_vma=False
    )
```

profile of v0, /device:TPU:0, one launch (start us, length us, event | category | flops | bytes accessed | tf_op | source)
XLA Modules:
  0.0 1670.9 jit_solution(14932956478151561862)
XLA Ops:
  11.3 22.3 %all-gather = bf16[8,1,256]{2,1,0:T(2,128)(2,1)S(1)} all-gather(bf16[1,1,256]{2,1,0:T(2,128)(2,1)S(1)} %reshape.346), channel_id=1, replica_groups=mesh['dp'=4,'row'=2,'col'=4] {'dp','row'}, dimensions={0}, use_global_device_ids=true | all-gather | bytes 4608 | tf_op jit(solution)/shard_map/all_gather | solution.py:200
  35.4 2.3 fusion.55
  37.6 39.7 %all-gather.16.cloned.1.call-done = bf16[2048,256]{1,0:T(8,128)(2,1)} async-done(((bf16[256,256]{1,0:T(8,128)(2,1)}), bf16[2048,256]{1,0:T(8,128)(2,1)}) %all-gather.16.cloned.1.call-update) | async-done | bytes 1048592 | tf_op jit(solution)/shard_map/all_gather | solution.py:196
  77.3 2.1 convolution_bitcast_fusion.3
  80.7 7.1 all_gather.57
  89.1 29.4 %all-gather.20.cloned.1.call-done = bf16[2048,256]{1,0:T(8,128)(2,1)} async-done(((bf16[256,256]{1,0:T(8,128)(2,1)}), bf16[2048,256]{1,0:T(8,128)(2,1)}) %all-gather.20.cloned.1.call-update) | async-done | bytes 1048592 | tf_op jit(solution)/shard_map/all_gather | solution.py:197
  118.5 2.0 convolution_convert_fusion.9
  120.4 7.1 all_gather.60
  127.6 40.7 %all-gather.18.cloned.1.call-done = bf16[2048,512]{1,0:T(8,128)(2,1)} async-done(((bf16[256,512]{1,0:T(8,128)(2,1)}), bf16[2048,512]{1,0:T(8,128)(2,1)}) %all-gather.18.cloned.1.call-update) | async-done | bytes 2097168 | tf_op jit(solution)/shard_map/all_gather | solution.py:195
  168.3 3.0 fusion.105
  171.7 5.3 while.39
  177.0 9.4 while.40
  178.5 3.0 fusion.162
  183.0 3.4 fusion.162
  186.4 2.0 copy.60
  188.5 30.5 %all-gather.22.cloned.1.call-done = bf16[512,2048]{1,0:T(8,128)(2,1)} async-done(((bf16[512,256]{1,0:T(8,128)(2,1)}), bf16[512,2048]{1,0:T(8,128)(2,1)}) %all-gather.22.cloned.1.call-update) | async-done | bytes 2097168 | tf_op jit(solution)/shard_map/all_gather | solution.py:204
  219.1 4.2 convolution_convert_fusion.6
  223.4 29.4 %reduce-scatter.12.cloned.1.call-done = bf16[512,512]{1,0:T(8,128)(2,1)} async-done(((bf16[512,2048]{1,0:T(8,128)(2,1)}), bf16[512,512]{1,0:T(8,128)(2,1)}) %reduce-scatter.12.cloned.1.call-update) | async-done | bytes 524304 | tf_op jit(solution)/shard_map/reduce_scatter | solution.py:238
  258.1 20.8 %all-gather.1 = bf16[8,1,256]{2,1,0:T(2,128)(2,1)S(1)} all-gather(bf16[1,1,256]{2,1,0:T(2,128)(2,1)S(1)} %reshape.348), channel_id=1, replica_groups=mesh['dp'=4,'row'=2,'col'=4] {'dp','row'}, dimensions={0}, use_global_device_ids=true | all-gather | bytes 4608 | tf_op jit(solution)/shard_map/all_gather | solution.py:201
  279.0 2.2 fusion.59
  281.2 123.0 %all-gather.28.cloned.1.call-done = bf16[2048,2048]{1,0:T(8,128)(2,1)} async-done(((bf16[256,2048]{1,0:T(8,128)(2,1)}), bf16[2048,2048]{1,0:T(8,128)(2,1)}) %all-gather.28.cloned.1.call-update) | async-done | bytes 8388624 | tf_op jit(solution)/shard_map/all_gather | solution.py:199
  404.2 9.5 fusion.103
  413.7 115.3 %all-gather.26.cloned.1.call-done = bf16[2048,2048]{1,0:T(8,128)(2,1)} async-done(((bf16[256,2048]{1,0:T(8,128)(2,1)}), bf16[2048,2048]{1,0:T(8,128)(2,1)}) %all-gather.26.cloned.1.call-update) | async-done | bytes 8388624 | tf_op jit(solution)/shard_map/all_gather | solution.py:198
  529.0 9.7 fusion.104
  538.7 13.1 all-gather.32.cloned.1.call-done
  551.8 127.0 %all-gather.30.cloned.1.call-done = bf16[2048,2048]{1,0:T(8,128)(2,1)} async-done(((bf16[2048,256]{1,0:T(8,128)(2,1)}), bf16[2048,2048]{1,0:T(8,128)(2,1)}) %all-gather.30.cloned.1.call-update) | async-done | bytes 8388624 | tf_op jit(solution)/shard_map/all_gather | solution.py:205
  678.8 13.6 multiply_convert_fusion
  692.4 8.5 fusion.106
  700.9 9.6 add_convert_fusion.1
  710.6 49.6 %all-reduce.6.cloned.1.call-done = bf16[512,2048]{1,0:T(8,128)(2,1)} async-done(((bf16[512,2048]{1,0:T(8,128)(2,1)}), bf16[512,2048]{1,0:T(8,128)(2,1)}) %all-reduce.6.cloned.1.call-update) | async-done | bytes 2097168 | tf_op jit(solution)/shard_map/psum | solution.py:166
  760.2 3.3 fusion.62
  765.9 22.7 %all-gather.34.cloned.1.call-done = bf16[512,2048]{1,0:T(8,128)(2,1)} async-done(((bf16[512,512]{1,0:T(8,128)(2,1)}), bf16[512,2048]{1,0:T(8,128)(2,1)}) %all-gather.34.cloned.1.call-update) | async-done | bytes 2097168 | tf_op jit(solution)/shard_map/all_gather | solution.py:162
  788.6 3.5 fusion.64
  793.3 18.5 %while.41 = (s32[]{:T(128)}, f32[1,2,512,256]{3,2,1,0:T(8,128)}, bf16[2,512,1,256]{3,1,2,0:T(8,128)(2,1)}, bf16[2,512,1,256]{3,1,2,0:T(8,128)(2,1)}, s32[2]{0:T(...) while((s32[]{:T(128)}, f32[1,2,512,256]{3,2,1,0:T(8,128)}, ...), condition=%wide.region_14.15_spmd.clone, body=%wide.region_13.14_spmd.clone.sunk | while | flops 1347159040 | bytes 34883008 | solution.py:149
  796.4 2.5 fusion.175
  805.4 2.9 fusion.175
  811.8 2.2 copy.73
  814.7 9.0 convolution_convert_fusion.5
  825.5 3.3 reduce-scatter.16.cloned.1.call-done
  831.2 4.1 fusion.95
  835.3 10.9 reduce-scatter.18.cloned.1.call-done
  846.1 2.2 fusion.107
  848.7 2.7 add_convert_fusion
  853.1 2.0 convolution_convert_fusion.8
  857.2 4.7 convolution_convert_fusion.3
  861.9 2.9 convolution_convert_fusion.4
  865.1 10.4 convolution_convert_fusion
  875.6 10.2 convolution_convert_fusion.2
  886.1 10.2 convolution_convert_fusion.1
  898.2 2.0 add_convert_fusion.2
  900.3 34.2 %all-reduce.8.cloned.1.call-done = bf16[512,2048]{1,0:T(8,128)(2,1)} async-done(((bf16[512,2048]{1,0:T(8,128)(2,1)}), bf16[512,2048]{1,0:T(8,128)(2,1)}) %all-reduce.8.cloned.1.call-update) | async-done | bytes 2097168 | tf_op jit(solution)/shard_map/psum | solution.py:166
  934.5 4.3 convert_element_type.235
  938.9 3.4 fusion.58
  942.3 21.8 %all-reduce.2 = (bf16[2048]{0:T(1024)(128)(2,1)S(1)}, bf16[2048]{0:T(1024)(128)(2,1)S(1)}) all-reduce(bf16[2048]{0:T(1024)(128)(2,1)S(1)} %get-tuple-element.376, bf16[2048]{0:T(1024)(128)(2,1)S(1)} %get-tuple-element.374), channel_id=6, replica_groups=mesh['dp'=4,'row'=2,'col'=4] {'dp','row'}, use_global_device_ids=true, to_apply=%region_20.21.clone | all-reduce | flops 4096 | bytes 16384
  964.8 2.7 fusion.67
  967.5 34.6 %reduce-scatter.22.cloned.1.call-done = bf16[256,256]{1,0:T(8,128)(2,1)} async-done(((bf16[2048,256]{1,0:T(8,128)(2,1)}), bf16[256,256]{1,0:T(8,128)(2,1)}) %reduce-scatter.22.cloned.1.call-update) | async-done | bytes 131088 | tf_op jit(solution)/shard_map/reduce_scatter | solution.py:353
  1003.7 65.1 %reduce-scatter.24.cloned.1.call-done = bf16[256,256]{1,0:T(8,128)(2,1)} async-done(((bf16[2048,256]{1,0:T(8,128)(2,1)}), bf16[256,256]{1,0:T(8,128)(2,1)}) %reduce-scatter.24.cloned.1.call-update) | async-done | bytes 131088 | tf_op jit(solution)/shard_map/reduce_scatter | solution.py:356
  1070.4 69.1 %reduce-scatter.26.cloned.1.call-done = bf16[256,512]{1,0:T(8,128)(2,1)} async-done(((bf16[2048,512]{1,0:T(8,128)(2,1)}), bf16[256,512]{1,0:T(8,128)(2,1)}) %reduce-scatter.26.cloned.1.call-update) | async-done | bytes 262160 | tf_op jit(solution)/shard_map/reduce_scatter | solution.py:359
  1141.5 68.9 %reduce-scatter.20.cloned.1.call-done = bf16[256,512]{1,0:T(8,128)(2,1)} async-done(((bf16[2048,512]{1,0:T(8,128)(2,1)}), bf16[256,512]{1,0:T(8,128)(2,1)}) %reduce-scatter.20.cloned.1.call-update) | async-done | bytes 262160 | tf_op jit(solution)/shard_map/reduce_scatter | solution.py:350
  1212.2 148.3 %reduce-scatter.32.cloned.1.call-done = bf16[256,2048]{1,0:T(8,128)(2,1)} async-done(((bf16[2048,2048]{1,0:T(8,128)(2,1)}), bf16[256,2048]{1,0:T(8,128)(2,1)}) %reduce-scatter.32.cloned.1.call-update) | async-done | bytes 1048592 | tf_op jit(solution)/shard_map/reduce_scatter | solution.py:368
  1363.8 147.0 %reduce-scatter.28.cloned.1.call-done = bf16[256,2048]{1,0:T(8,128)(2,1)} async-done(((bf16[2048,2048]{1,0:T(8,128)(2,1)}), bf16[256,2048]{1,0:T(8,128)(2,1)}) %reduce-scatter.28.cloned.1.call-update) | async-done | bytes 1048592 | tf_op jit(solution)/shard_map/reduce_scatter | solution.py:362
  1510.8 2.8 convert_element_type.249
  1513.6 147.3 %reduce-scatter.30.cloned.1.call-done = bf16[256,2048]{1,0:T(8,128)(2,1)} async-done(((bf16[2048,2048]{1,0:T(8,128)(2,1)}), bf16[256,2048]{1,0:T(8,128)(2,1)}) %reduce-scatter.30.cloned.1.call-update) | async-done | bytes 1048592 | tf_op jit(solution)/shard_map/reduce_scatter | solution.py:365
  1660.9 2.8 convert_element_type.251
  (228 shorter events, 55.8 us)
Async XLA Ops:
  7.2 28.2 %all-gather.14.cloned.1.call-start = ((), (), s32[]{:S(2)}) async-start(), calls=%async_computation.11 | async-start | bytes 2621440 | tf_op jit(solution)/shard_map/all_gather | solution.py:193
  7.9 69.4 %all-gather.16.cloned.1.call-start = ((), (), s32[]{:S(2)}) async-start(), calls=%async_computation.12 | async-start | bytes 1179648 | tf_op jit(solution)/shard_map/all_gather | solution.py:196
  8.7 109.8 %all-gather.20.cloned.1.call-start = ((), (), s32[]{:S(2)}) async-start(), calls=%async_computation.14 | async-start | bytes 1179648 | tf_op jit(solution)/shard_map/all_gather | solution.py:197
  9.4 158.9 %all-gather.18.cloned.1.call-start = ((), (), s32[]{:S(2)}) async-start(), calls=%async_computation.13 | async-start | bytes 2359296 | tf_op jit(solution)/shard_map/all_gather | solution.py:195
  10.0 209.1 %all-gather.22.cloned.1.call-start = ((), (), s32[]{:S(2)}) async-start(), calls=%async_computation.15 | async-start | bytes 2359296 | tf_op jit(solution)/shard_map/all_gather | solution.py:204
  10.6 242.2 %reduce-scatter.12.cloned.1.call-start = ((), (), s32[]{:S(2)}) async-start(), calls=%async_computation.16 | async-start | bytes 2621440 | tf_op jit(solution)/shard_map/reduce_scatter | solution.py:238
  35.3 136.0 %copy-start.18 = (f32[512,128]{0,1:T(8,128)}, f32[512,128]{0,1:T(8,128)S(1)}, u32[]{:S(2)}) copy-start(f32[512,128]{0,1:T(8,128)S(1)} %get-tuple-element.455) | copy-start | bytes 786436
  35.3 135.9 %copy-start.20 = (f32[512,128]{0,1:T(8,128)}, f32[512,128]{0,1:T(8,128)S(1)}, u32[]{:S(2)}) copy-start(f32[512,128]{0,1:T(8,128)S(1)} %get-tuple-element.456) | copy-start | bytes 786436
  35.3 42.0 %copy-start.8 = (bf16[512,2048]{1,0:T(8,128)(2,1)S(1)}, bf16[512,2048]{1,0:T(8,128)(2,1)}, u32[]{:S(2)}) copy-start(bf16[512,2048]{1,0:T(8,128)(2,1)} %all-gather.14.cloned.1.call-done) | copy-start | bytes 6291460
  188.5 30.5 %copy-start.26 = (f32[64,8,2,256]{3,1,2,0:T(8,128)}, f32[64,8,2,256]{3,1,2,0:T(8,128)S(1)}, u32[]{:S(2)}) copy-start(f32[64,8,2,256]{3,1,2,0:T(8,128)S(1)} %copy.75) | copy-start | bytes 3145732
  223.3 29.5 %copy-start.14 = (bf16[512,512]{1,0:T(8,128)(2,1)S(1)}, bf16[512,512]{1,0:T(8,128)(2,1)}, u32[]{:S(2)}) copy-start(bf16[512,512]{1,0:T(8,128)(2,1)} %param.18) | copy-start | bytes 1572868
  223.3 33.0 %copy-start.24 = (bf16[512,512]{1,0:T(8,128)(2,1)S(1)}, bf16[512,512]{1,0:T(8,128)(2,1)}, u32[]{:S(2)}) copy-start(bf16[512,512]{1,0:T(8,128)(2,1)} %param.29) | copy-start | bytes 1572868
  223.3 55.6 %all-gather.24.cloned.1.call-start = ((), (), s32[]{:S(2)}) async-start(), calls=%async_computation.17 | async-start | bytes 2621440 | tf_op jit(solution)/shard_map/all_gather | solution.py:245
  254.8 149.4 %all-gather.28.cloned.1.call-start = ((), (), s32[]{:S(2)}) async-start(), calls=%async_computation.19 | async-start | bytes 9437184 | tf_op jit(solution)/shard_map/all_gather | solution.py:199
  255.6 2.6 copy-start.30
  255.6 273.4 %all-gather.26.cloned.1.call-start = ((), (), s32[]{:S(2)}) async-start(), calls=%async_computation.18 | async-start | bytes 9437184 | tf_op jit(solution)/shard_map/all_gather | solution.py:198
  256.3 295.5 %all-gather.32.cloned.1.call-start = ((), (), s32[]{:S(2)}) async-start(), calls=%async_computation.22 | async-start | bytes 2621440 | tf_op jit(solution)/shard_map/all_gather | solution.py:162
  257.3 421.4 %all-gather.30.cloned.1.call-start = ((), (), s32[]{:S(2)}) async-start(), calls=%async_computation.20 | async-start | bytes 9437184 | tf_op jit(solution)/shard_map/all_gather | solution.py:205
  258.1 502.1 %all-reduce.6.cloned.1.call-start = ((), (), s32[]{:S(2)}) async-start(), calls=%async_computation.23 | async-start | bytes 4194304 | tf_op jit(solution)/shard_map/psum | solution.py:166
  278.9 125.3 %copy-start.10 = (bf16[512,2048]{1,0:T(8,128)(2,1)S(1)}, bf16[512,2048]{1,0:T(8,128)(2,1)}, u32[]{:S(2)}) copy-start(bf16[512,2048]{1,0:T(8,128)(2,1)} %all-gather.24.cloned.1.call-done) | copy-start | bytes 6291460
  692.4 8.5 copy-start.33
  692.4 8.5 copy-start.32
  710.5 78.1 %all-gather.34.cloned.1.call-start = ((), (), s32[]{:S(2)}) async-start(), calls=%async_computation.24 | async-start | bytes 2621440 | tf_op jit(solution)/shard_map/all_gather | solution.py:162
  760.2 3.3 copy-start.7
  763.5 1.0 copy-start.25
  765.8 63.0 %reduce-scatter.16.cloned.1.call-start = ((), (), s32[]{:S(2)}) async-start(), calls=%async_computation.25 | async-start | bytes 786432 | tf_op jit(solution)/shard_map/reduce_scatter | solution.py:312
  765.9 26.4 %copy-start.17 = (f32[1,2,512,256]{3,2,1,0:T(8,128)S(1)}, f32[1,2,512,256]{3,2,1,0:T(8,128)}, u32[]{:S(2)}) copy-start(f32[1,2,512,256]{3,2,1,0:T(8,128)} %get-tuple-element.157) | copy-start | bytes 3145732
  793.3 2.3 copy-start.3
  793.3 2.3 copy-start.11
  794.7 1.0 copy-start
  794.7 1.2 copy-start.13
  796.4 2.5 copy-start.27
  796.4 4.8 copy-start.1
  801.2 1.2 copy-start.4
  801.2 1.2 copy-start.12
  802.4 2.3 copy-start.3
  802.4 2.3 copy-start.11
  803.7 1.2 copy-start.13
  805.4 2.9 copy-start.27
  805.4 5.2 copy-start.1
  810.6 1.2 copy-start.4
  810.6 1.2 copy-start.12
  811.8 2.9 copy-start.34
  814.0 32.1 %reduce-scatter.18.cloned.1.call-start = ((), (), s32[]{:S(2)}) async-start(), calls=%async_computation.26 | async-start | bytes 786432 | tf_op jit(solution)/shard_map/reduce_scatter | solution.py:315
  814.6 83.6 %reduce-scatter.14.cloned.1.call-start = ((), (), s32[]{:S(2)}) async-start(), calls=%async_computation.21 | async-start | bytes 2621440 | tf_op jit(solution)/shard_map/reduce_scatter | solution.py:254
  823.7 1.2 copy-start.2
  823.7 1.6 copy-start.19
  823.7 1.6 copy-start.21
  823.7 110.8 %all-reduce.8.cloned.1.call-start = ((), (), s32[]{:S(2)}) async-start(), calls=%async_computation.27 | async-start | bytes 4194304 | tf_op jit(solution)/shard_map/psum | solution.py:166
  831.2 17.2 %copy-start.22 = (bf16[2048,512]{1,0:T(8,128)(2,1)S(1)}, bf16[2048,512]{1,0:T(8,128)(2,1)}, u32[]{:S(2)}) copy-start(bf16[2048,512]{1,0:T(8,128)(2,1)} %all-gather.18.cloned.1.call-done) | copy-start | bytes 6291460
  846.1 2.6 copy-start.5
  851.5 1.6 copy-start.9
  851.5 3.6 copy-start.29
  851.5 150.6 %reduce-scatter.22.cloned.1.call-start = ((), (), s32[]{:S(2)}) async-start(), calls=%async_computation.29 | async-start | bytes 1179648 | tf_op jit(solution)/shard_map/reduce_scatter | solution.py:353
  855.1 213.7 %reduce-scatter.24.cloned.1.call-start = ((), (), s32[]{:S(2)}) async-start(), calls=%async_computation.30 | async-start | bytes 1179648 | tf_op jit(solution)/shard_map/reduce_scatter | solution.py:356
  857.1 282.4 %reduce-scatter.26.cloned.1.call-start = ((), (), s32[]{:S(2)}) async-start(), calls=%async_computation.31 | async-start | bytes 2359296 | tf_op jit(solution)/shard_map/reduce_scatter | solution.py:359
  861.9 348.5 %reduce-scatter.20.cloned.1.call-start = ((), (), s32[]{:S(2)}) async-start(), calls=%async_computation.28 | async-start | bytes 2359296 | tf_op jit(solution)/shard_map/reduce_scatter | solution.py:350
  864.8 495.7 %reduce-scatter.32.cloned.1.call-start = ((), (), s32[]{:S(2)}) async-start(), calls=%async_computation.34 | async-start | bytes 9437184 | tf_op jit(solution)/shard_map/reduce_scatter | solution.py:368
  875.5 635.3 %reduce-scatter.28.cloned.1.call-start = ((), (), s32[]{:S(2)}) async-start(), calls=%async_computation.32 | async-start | bytes 9437184 | tf_op jit(solution)/shard_map/reduce_scatter | solution.py:362
  885.8 775.1 %reduce-scatter.30.cloned.1.call-start = ((), (), s32[]{:S(2)}) async-start(), calls=%async_computation.33 | async-start | bytes 9437184 | tf_op jit(solution)/shard_map/reduce_scatter | solution.py:365
  896.3 1.9 copy-start.15
  896.3 1.9 copy-start.23
  934.5 4.3 copy-start.6
  938.9 25.9 %copy-start.16 = (bf16[512,512]{1,0:T(8,128)(2,1)S(1)}, bf16[512,512]{1,0:T(8,128)(2,1)}, u32[]{:S(2)}) copy-start(bf16[512,512]{1,0:T(8,128)(2,1)} %fusion.72) | copy-start | bytes 1572868
  (4 other events, 3.3 us)
Sparse Core Ops, SparseCore 0:
  9.5 25.2 all-gather.13
  37.0 40.2 all-gather.15
  79.4 38.9 all-gather.19
  120.4 47.7 all-gather.17
  170.2 48.8 all-gather.21
  223.4 29.3 reduce-scatter.11
  254.9 22.5 all-gather.23
  279.7 124.4 all-gather.27
  406.3 122.6 all-gather.25
  531.0 20.7 all-gather.31
  553.8 124.9 all-gather.29
  710.6 49.5 all-reduce.5
  765.9 22.6 all-gather.33
  814.1 14.6 reduce-scatter.15
  831.5 14.6 reduce-scatter.17
  849.1 31.1 reduce-scatter.13
  883.1 51.3 all-reduce.7
  937.8 64.2 reduce-scatter.21
  1005.5 63.2 reduce-scatter.23
  1072.2 67.2 reduce-scatter.25
  1143.0 67.3 reduce-scatter.19
  1214.0 146.4 reduce-scatter.31
  1364.2 146.5 reduce-scatter.27
  1514.3 146.5 reduce-scatter.29
where the time goes:
time: 1680 us; the launch traced here: 1670 us
  waiting for transfers between devices  1360 us (81%)
  matrix products  147 us (9%)
  blocking collectives  79.2 us (5%)
  other arithmetic  46.3 us (3%)
  local copies, waits for them, and re-layouts  21.3 us (1%)
    reduce_scatter x1, waiting for transfers between devices, per_device(): lax.psum_scatter(grad_down_part.astype(jnp.bfloat16), ('dp', 'row'), scat...  148 us
    reduce_scatter x1, waiting for transfers between devices, per_device(): lax.psum_scatter(grad_up_part.astype(jnp.bfloat16), ('dp', 'row'), scatte...  147 us
    reduce_scatter x1, waiting for transfers between devices, per_device(): lax.psum_scatter(grad_gate_part.astype(jnp.bfloat16), ('dp', 'row'), scat...  147 us
    all_gather x1, waiting for transfers between devices, per_device(): lax.all_gather(w_down, ('dp', 'row'), axis=1, tiled=True)  127 us
    all_gather x1, waiting for transfers between devices, per_device(): lax.all_gather(w_up, ('dp', 'row'), axis=0, tiled=True)  123 us
    all_gather x1, waiting for transfers between devices, per_device(): lax.all_gather(w_gate, ('dp', 'row'), axis=0, tiled=True)  115 us
    psum x2, waiting for transfers between devices, col_total(): return lax.psum(value.astype(jnp.bfloat16), 'col').astype(jnp.float32)  83.8 us
    reduce_scatter x1, waiting for transfers between devices, per_device(): lax.psum_scatter(grad_output_part.astype(jnp.bfloat16), ('dp', 'row'), sc...  69.1 us
  transfers between devices with their start and end apart: 24, of which 21 were waited for; matrix products, arithmetic and copies ran while one was open for 8% of the time, Pallas kernels for 0%

commit v1 on v0

v1 whole, which is shorter than its diff:
```python
import math

import jax
import jax.numpy as jnp
from jax import lax
from jax.sharding import PartitionSpec as P

QUERY_HEADS = 8
KEY_VALUE_HEADS = 4
HEAD_SIZE = 256


EPSILON = 1e-06
ROPE_BASE = 1000042.0


def rope_tables(positions):
    half = HEAD_SIZE // 2
    freq = ROPE_BASE ** (-jnp.arange(half, dtype=jnp.float32) * 2.0 / HEAD_SIZE)
    angle = positions[:, None] * freq[None, :]
    return (jnp.cos(angle), jnp.sin(angle))


def rotary_apply(values, cosine_table, sine_table):
    half = values.shape[-1] // 2
    first = values[..., :half]
    second = values[..., half:]
    cos_part = cosine_table[:, None, :]
    sin_part = sine_table[:, None, :]
    return jnp.concatenate(
        [first * cos_part - second * sin_part, second * cos_part + first * sin_part], axis=-1
    )


def rotate_back(grads, cosine_table, sine_table):
    half = grads.shape[-1] // 2
    first = grads[..., :half]
    second = grads[..., half:]
    cos_part = cosine_table[:, None, :]
    sin_part = sine_table[:, None, :]
    return jnp.concatenate(
        [first * cos_part + second * sin_part, second * cos_part - first * sin_part], axis=-1
    )


def norm_rows(full, gain):
    factor = lax.rsqrt(jnp.mean(full * full, axis=1, keepdims=True) + EPSILON)
    return (factor, (full * factor * gain).astype(jnp.bfloat16))


def norm_back(full, factor, gain, grad):
    inner = jnp.mean(gain * grad * full, axis=1, keepdims=True)
    back = factor * gain * grad - full * factor * factor * factor * inner
    gain_grad = jnp.sum(grad * full * factor, axis=0)
    return (back, gain_grad)


def contract_rows(left, right):
    return lax.dot_general(
        left, right, (((0,), (0,)), ((), ())), preferred_element_type=jnp.float32
    )


def times_transposed(left, right):
    return lax.dot_general(
        left, right, (((1,), (1,)), ((), ())), preferred_element_type=jnp.float32
    )


def masked_scores(query_rows, key_part, query_pos, index, key_block, score_scale):
    scores = (
        jnp.einsum("hgqd,khd->hgqk", query_rows, key_part, preferred_element_type=jnp.float32)
        * score_scale
    )
    key_pos = index * key_block + jnp.arange(key_block, dtype=jnp.int32)
    return jnp.where(key_pos[None, :] <= query_pos[:, None], scores, -1e30)


def attend(query_rows, keys, values, query_pos, key_block, score_scale):
    heads, query_group, token_count, size = query_rows.shape
    blocks = keys.shape[0] // key_block
    key_parts = keys.reshape(blocks, key_block, heads, size)
    value_parts = values.reshape(blocks, key_block, heads, size)
    indices = jnp.arange(blocks, dtype=jnp.int32)

    def totals(carry, item):
        top, total = carry
        key_part, index = item
        scores = masked_scores(query_rows, key_part, query_pos, index, key_block, score_scale)
        new_top = jnp.maximum(top, jnp.max(scores, axis=-1))
        total = total * jnp.exp(top - new_top) + jnp.sum(
            jnp.exp(scores - new_top[..., None]), axis=-1
        )
        return ((new_top, total), None)

    start = (
        jnp.full((heads, query_group, token_count), -1e30, jnp.float32),
        jnp.zeros((heads, query_group, token_count), jnp.float32),
    )
    (top, total), unused = lax.scan(totals, start, (key_parts, indices))
    log_total = top + jnp.log(total)

    def mixing(accum, item):
        key_part, value_part, index = item
        scores = masked_scores(query_rows, key_part, query_pos, index, key_block, score_scale)
        probs = jnp.exp(scores - log_total[..., None]).astype(jnp.bfloat16)
        return (
            accum
            + jnp.einsum("hgqk,khd->hgqd", probs, value_part, preferred_element_type=jnp.float32),
            None,
        )

    accum, unused = lax.scan(
        mixing,
        jnp.zeros((heads, query_group, token_count, size), jnp.float32),
        (key_parts, value_parts, indices),
    )
    return (accum, log_total)


def attend_back(
    query_rows, keys, values, query_pos, key_block, score_scale, log_total, delta, grad_out
):
    heads, query_group, token_count, size = query_rows.shape
    blocks = keys.shape[0] // key_block
    key_parts = keys.reshape(blocks, key_block, heads, size)
    value_parts = values.reshape(blocks, key_block, heads, size)

    def step(grad_query, item):
        key_part, value_part, index = item
        scores = masked_scores(query_rows, key_part, query_pos, index, key_block, score_scale)
        probs = jnp.exp(scores - log_total[..., None])
        probs_low = probs.astype(jnp.bfloat16)
        grad_probs = jnp.einsum(
            "hgqd,khd->hgqk", grad_out, value_part, preferred_element_type=jnp.float32
        )
        grad_scores = (probs * (grad_probs - delta[..., None]) * score_scale).astype(jnp.bfloat16)
        grad_query = grad_query + jnp.einsum(
            "hgqk,khd->hgqd", grad_scores, key_part, preferred_element_type=jnp.float32
        )
        grad_key = jnp.einsum(
            "hgqk,hgqd->khd", grad_scores, query_rows, preferred_element_type=jnp.float32
        )
        grad_value = jnp.einsum(
            "hgqk,hgqd->khd", probs_low, grad_out, preferred_element_type=jnp.float32
        )
        return (grad_query, (grad_key, grad_value))

    grad_query, (grad_keys, grad_values) = lax.scan(
        step,
        jnp.zeros((heads, query_group, token_count, size), jnp.float32),
        (key_parts, value_parts, jnp.arange(blocks, dtype=jnp.int32)),
    )
    return (
        grad_query,
        grad_keys.reshape(blocks * key_block, heads * size),
        grad_values.reshape(blocks * key_block, heads * size),
    )


def swap(value, axis, bit):
    size = lax.axis_size(axis)
    return lax.ppermute(value, axis, [(i, i ^ bit) for i in range(size)])


def gather_col(value):
    width = value.shape[1]
    far = swap(value, "col", 2)
    near = swap(jnp.concatenate([value, far], axis=1), "col", 1)
    return jnp.concatenate([value, near[:, :width], far, near[:, width:]], axis=1)


def scatter_col(value):
    width = value.shape[1] // 4
    part = [value[:, p * width : (p + 1) * width].astype(jnp.float32) for p in range(4)]
    low = jnp.bfloat16
    got = swap(jnp.concatenate([part[1], part[3]], axis=1).astype(low), "col", 1)
    keep_own = part[0] + got[:, :width].astype(jnp.float32)
    keep_far = part[2] + got[:, width:].astype(jnp.float32)
    return keep_own + swap(keep_far.astype(low), "col", 2).astype(jnp.float32)


def col_sum(value):
    value = value + swap(value, "col", 1)
    return value + swap(value, "col", 2)


def gather_row(value, axis):
    if lax.axis_size("row") == 2:
        other = swap(value, "row", 1)
        first = lax.axis_index("row") == 0
        return jnp.concatenate(
            [jnp.where(first, value, other), jnp.where(first, other, value)], axis=axis
        )
    return lax.all_gather(value, "row", axis=axis, tiled=True)


def scatter_row(value, axis):
    if lax.axis_size("row") == 2:
        me = lax.axis_index("row")
        mine = lax.dynamic_index_in_dim(value, me, axis, keepdims=False)
        theirs = lax.dynamic_index_in_dim(value, 1 - me, axis, keepdims=False)
        got = swap(theirs.astype(jnp.bfloat16), "row", 1)
        return mine.astype(jnp.float32) + got.astype(jnp.float32)
    value = lax.psum_scatter(value.astype(jnp.bfloat16), "row", scatter_dimension=axis, tiled=True)
    return jnp.squeeze(value, axis).astype(jnp.float32)


def reorder(blocks, shift):
    out = []
    for p in range(4):
        pick = blocks[p]
        for s in range(1, 4):
            pick = jnp.where(shift == s, blocks[p ^ s], pick)
        out.append(pick)
    return out


def gather_weight(local, shift):
    got = [local] + [swap(local, "dp", j) for j in range(1, 4)]
    full = gather_row(jnp.stack(reorder(got, shift))[:, None], 1)
    return full.reshape(-1, local.shape[1])


def exchange_weight(local, shift):
    me = lax.axis_index("dp")
    quarter = local.shape[1] // 4

    def part(j):
        return lax.dynamic_slice_in_dim(local, (me ^ j) * quarter, quarter, 1)

    got = [part(0)] + [swap(part(j), "dp", j) for j in range(1, 4)]
    full = gather_row(jnp.stack(reorder(got, shift))[:, None], 1)
    return full.reshape(-1, quarter)


def return_weight(grad, shift):
    rows, quarter = grad.shape
    row_size = lax.axis_size("row")
    own = scatter_row(grad.reshape(4, row_size, rows // (4 * row_size), quarter), 1)
    own = own.astype(jnp.bfloat16)
    sends = reorder([own[p] for p in range(4)], shift)
    got = [sends[0]] + [swap(sends[j], "dp", j) for j in range(1, 4)]
    natural = reorder(got, lax.axis_index("dp"))
    return jnp.concatenate(natural, axis=1).astype(jnp.float32)


def sum_weight(grad, shift):
    rows, width = grad.shape
    row_size = lax.axis_size("row")
    own = scatter_row(grad.reshape(4, row_size, rows // (4 * row_size), width), 1)
    sends = reorder([own[p] for p in range(4)], shift)
    total = sends[0]
    for j in range(1, 4):
        total = total + swap(sends[j].astype(jnp.bfloat16), "dp", j).astype(jnp.float32)
    return total


def gather_tokens(value):
    full = gather_col(
        jnp.concatenate([value] + [swap(value, "dp", j) for j in range(1, 4)], axis=0)
    )
    return full


def scatter_tokens(value):
    own = scatter_col(value)
    rows = own.shape[0] // 4
    total = own[:rows]
    for j in range(1, 4):
        total = total + swap(
            own[j * rows : (j + 1) * rows].astype(jnp.bfloat16), "dp", j
        ).astype(jnp.float32)
    return total


def per_device(
    tokens,
    w_query,
    key_matrix,
    value_matrix,
    w_output,
    w_gate,
    w_up,
    w_down,
    gain_attn,
    gain_ffn,
    lengths,
    cotangent,
):
    low = jnp.bfloat16
    wide = jnp.float32
    row_count, col_width = tokens.shape
    model_width = col_width * 4
    slot_size = row_count * lax.axis_size("row")
    key_block = min(512, slot_size)
    query_group = QUERY_HEADS // KEY_VALUE_HEADS
    score_scale = 1.0 / math.sqrt(HEAD_SIZE)
    me_dp, me_row, me_col = (lax.axis_index(name) for name in ("dp", "row", "col"))
    shift = me_dp ^ me_col
    query_pos = me_row * row_count + jnp.arange(row_count, dtype=jnp.int32)
    valid = (query_pos < lengths[0]).astype(wide)[:, None]
    cosine_table, sine_table = rope_tables(query_pos.astype(wide))

    gains = lax.all_gather(jnp.stack([gain_attn, gain_ffn]), ("dp", "row"), axis=1, tiled=True)
    gains = gains.reshape(2, 4, col_width)
    gains = jnp.concatenate(reorder([gains[:, p] for p in range(4)], me_col), axis=1)
    gain_one, gain_two = gains[0].astype(wide), gains[1].astype(wide)

    x_full = gather_col(tokens)
    q_cols, k_cols = w_query.shape[1], key_matrix.shape[1]
    attn_weight = gather_weight(
        jnp.concatenate([w_query, key_matrix, value_matrix], axis=1), shift
    )
    out_weight = gather_weight(w_output.T, shift)
    down_weight = exchange_weight(w_down.T, shift)
    gate_weight = exchange_weight(w_gate, shift)
    up_weight = exchange_weight(w_up, shift)
    x_wide = x_full.astype(wide)
    factor_one, normed = norm_rows(x_wide, gain_one)
    qkv = jnp.dot(normed, attn_weight, preferred_element_type=wide)
    kv_heads = k_cols // HEAD_SIZE
    query_rot = rotary_apply(
        qkv[:, :q_cols].reshape(row_count, kv_heads * query_group, HEAD_SIZE),
        cosine_table,
        sine_table,
    ).astype(low)
    key_rot = rotary_apply(
        qkv[:, q_cols : q_cols + k_cols].reshape(row_count, kv_heads, HEAD_SIZE),
        cosine_table,
        sine_table,
    ).astype(low)
    kv_all = gather_row(
        jnp.concatenate(
            [key_rot.reshape(row_count, k_cols), qkv[:, q_cols + k_cols :].astype(low)], axis=1
        ),
        0,
    )
    keys_all = kv_all[:, :k_cols].reshape(slot_size, kv_heads, HEAD_SIZE)
    values_all = kv_all[:, k_cols:].reshape(slot_size, kv_heads, HEAD_SIZE)
    query_rows = query_rot.reshape(row_count, kv_heads, query_group, HEAD_SIZE).transpose(
        1, 2, 0, 3
    )
    attended, log_total = attend(
        query_rows, keys_all, values_all, query_pos, key_block, score_scale
    )
    mixed_heads = (
        attended.transpose(2, 0, 1, 3).reshape(row_count, q_cols) * valid
    ).astype(low)
    residual = tokens.astype(wide) + scatter_col(times_transposed(mixed_heads, out_weight))

    grad_out = (cotangent.astype(wide) * valid).astype(low)
    residual_full = gather_tokens(residual.astype(low)).astype(wide)
    grad_out_full = gather_tokens(grad_out)
    factor_two, normed_two = norm_rows(residual_full, gain_two)
    gate = jnp.dot(normed_two, gate_weight, preferred_element_type=wide)
    upward = jnp.dot(normed_two, up_weight, preferred_element_type=wide)
    sigmoid_gate = jax.nn.sigmoid(gate)
    silu_gate = gate * sigmoid_gate
    hidden = (silu_gate * upward).astype(low)
    layer_out = (residual + scatter_tokens(times_transposed(hidden, down_weight))).astype(low)
    grad_hidden = jnp.dot(grad_out_full, down_weight, preferred_element_type=wide)
    grad_gate_act = (
        grad_hidden * upward * sigmoid_gate * (1.0 + gate * (1.0 - sigmoid_gate))
    ).astype(low)
    grad_up_act = (grad_hidden * silu_gate).astype(low)
    grad_down_part = contract_rows(grad_out_full, hidden)
    grad_gate_part = contract_rows(normed_two, grad_gate_act)
    grad_up_part = contract_rows(normed_two, grad_up_act)
    grad_normed_two = scatter_tokens(
        times_transposed(grad_gate_act, gate_weight) + times_transposed(grad_up_act, up_weight)
    )
    own_gain_two = gain_two[:col_width]
    own_factor_two = factor_two[:row_count]
    own_residual = residual_full[:row_count, :col_width]
    scaled = own_gain_two * grad_normed_two
    inner = col_sum(jnp.sum(scaled * own_residual, axis=1)[:, None]) / model_width
    grad_residual = (
        grad_out.astype(wide)
        + own_factor_two * scaled
        - own_residual * own_factor_two * own_factor_two * own_factor_two * inner
    ).astype(low)
    gain_two_grad = jnp.sum(grad_normed_two * own_residual * own_factor_two, axis=0)

    grad_residual_full = gather_col(grad_residual)
    grad_output_part = contract_rows(grad_residual_full, mixed_heads)
    grad_mixed = (
        jnp.dot(grad_residual_full, out_weight, preferred_element_type=wide) * valid
    ).astype(low)
    grad_heads = grad_mixed.reshape(row_count, kv_heads, query_group, HEAD_SIZE).transpose(
        1, 2, 0, 3
    )
    delta = jnp.sum(grad_heads.astype(wide) * attended, axis=-1)
    grad_query_rot, grad_keys_all, grad_values_all = attend_back(
        query_rows,
        keys_all,
        values_all,
        query_pos,
        key_block,
        score_scale,
        log_total,
        delta,
        grad_heads,
    )
    grad_kv = scatter_row(
        jnp.concatenate([grad_keys_all, grad_values_all], axis=1).reshape(
            slot_size // row_count, row_count, 2 * k_cols
        ),
        0,
    )
    grad_query_raw = (
        rotate_back(
            grad_query_rot.transpose(2, 0, 1, 3).reshape(
                row_count, kv_heads * query_group, HEAD_SIZE
            ),
            cosine_table,
            sine_table,
        )
        .reshape(row_count, q_cols)
        .astype(low)
    )
    grad_key_raw = (
        rotate_back(
            grad_kv[:, :k_cols].reshape(row_count, kv_heads, HEAD_SIZE), cosine_table, sine_table
        )
        .reshape(row_count, k_cols)
        .astype(low)
    )
    grad_raw = jnp.concatenate([grad_query_raw, grad_key_raw, grad_kv[:, k_cols:].astype(low)], axis=1)
    grad_attn_part = contract_rows(normed, grad_raw)
    grad_normed = scatter_col(times_transposed(grad_raw, attn_weight))
    own_gain_one = gain_one[:col_width]
    own_tokens = tokens.astype(wide)
    scaled = own_gain_one * grad_normed
    inner = col_sum(jnp.sum(scaled * own_tokens, axis=1)[:, None]) / model_width
    grad_tokens = (
        grad_residual.astype(wide)
        + factor_one * scaled
        - own_tokens * factor_one * factor_one * factor_one * inner
    ).astype(low)
    gain_one_grad = jnp.sum(grad_normed * own_tokens * factor_one, axis=0)

    gain_grads = jnp.zeros((2, model_width), wide)
    gain_grads = lax.dynamic_update_slice(
        gain_grads, jnp.stack([gain_one_grad, gain_two_grad]), (0, me_col * col_width)
    )
    gain_grads = lax.psum(gain_grads, ("dp", "row", "col"))
    own = gain_attn.shape[0]
    gain_grads = lax.dynamic_slice_in_dim(
        gain_grads, (me_dp * lax.axis_size("row") + me_row) * own, own, 1
    )
    grad_attn = sum_weight(grad_attn_part, shift)
    return (
        layer_out,
        grad_tokens,
        gain_grads[0],
        gain_grads[1],
        grad_attn[:, :q_cols],
        grad_attn[:, q_cols : q_cols + k_cols],
        grad_attn[:, q_cols + k_cols :],
        sum_weight(grad_output_part, shift).T,
        return_weight(grad_gate_part, shift),
        return_weight(grad_up_part, shift),
        return_weight(grad_down_part, shift).T,
    )


def solution(mesh):
    in_specs = (
        P(("dp", "row"), "col"),
        P(("dp", "row"), "col"),
        P(("dp", "row"), "col"),
        P(("dp", "row"), "col"),
        P("col", ("dp", "row")),
        P(("dp", "row"), "col"),
        P(("dp", "row"), "col"),
        P("col", ("dp", "row")),
        P(("dp", "row")),
        P(("dp", "row")),
        P("dp"),
        P(("dp", "row"), "col"),
    )
    out_specs = (
        P(("dp", "row"), "col"),
        P(("dp", "row"), "col"),
        P(("dp", "row")),
        P(("dp", "row")),
        P(("dp", "row"), "col"),
        P(("dp", "row"), "col"),
        P(("dp", "row"), "col"),
        P("col", ("dp", "row")),
        P(("dp", "row"), "col"),
        P(("dp", "row"), "col"),
        P("col", ("dp", "row")),
    )
    return jax.shard_map(
        per_device, mesh=mesh, in_specs=in_specs, out_specs=out_specs, check_vma=False
    )
```

time: 1680 us -> 1070 us (0.64)
  waiting for transfers between devices: 1360 us -> 430 us
  other arithmetic: 46.3 us -> 197 us
  starting transfers between devices: 1.43 us -> 129 us
  local copies, waits for them, and re-layouts: 21.3 us -> 73.8 us
  matrix products: 147 us -> 122 us
  blocking collectives: 79.2 us -> 99.2 us
    reduce_scatter x11 -> x0, waiting for transfers between devices: 724 us -> none  [the longest x1 148 us: per_device(): lax.psum_scatter(grad_down_part.astype(jnp.bfloat16), ('dp', 'row'), scat...]
    all_gather x11 -> x0, waiting for transfers between devices: 541 us -> none  [the longest x1 127 us: per_device(): lax.all_gather(w_down, ('dp', 'row'), axis=1, tiled=True)]
    ppermute x0 -> x74, waiting for transfers between devices: none -> 430 us  [swap(): return lax.ppermute(value, axis, [(i, i ^ bit) for i in range(size)])]
    ppermute x0 -> x74, starting transfers between devices: none -> 129 us  [swap(): return lax.ppermute(value, axis, [(i, i ^ bit) for i in range(size)])]
    psum x2 -> x0, waiting for transfers between devices: 83.8 us -> none  [col_total(): return lax.psum(value.astype(jnp.bfloat16), 'col').astype(jnp.float32)]
    psum x0 -> x1, blocking collectives: none -> 63.5 us  [per_device(): gain_grads = lax.psum(gain_grads, ('dp', 'row', 'col'))]
    concatenate x0 -> x19, other arithmetic: none -> 60.7 us  [the longest x4 30.8 us: gather_col(): near = swap(jnp.concatenate([value, far], axis=1), 'col', 1)]
    convert_element_type x17 -> x22, other arithmetic: 25.1 us -> 67.8 us  [the longest x2 20.2 us: per_device(): residual_full = gather_tokens(residual.astype(low)).astype(wide)]
  transfers between devices with their start and end apart: 24 -> 74, of which waited for: 21 -> 30; matrix products, arithmetic and copies ran while one was open for 8% -> 23% of each run, Pallas kernels for 0% -> 0%
where the time goes in v1:
time: 1070 us; the launch traced here: 1060 us
  waiting for transfers between devices  430 us (40%)
  other arithmetic  197 us (18%)
  starting transfers between devices  129 us (12%)
  matrix products  122 us (11%)
  blocking collectives  99.2 us (9%)
  local copies, waits for them, and re-layouts  73.8 us (7%)
    ppermute x74, waiting for transfers between devices, swap(): return lax.ppermute(value, axis, [(i, i ^ bit) for i in range(size)])  430 us
    ppermute x74, starting transfers between devices, swap(): return lax.ppermute(value, axis, [(i, i ^ bit) for i in range(size)])  129 us
    psum x1, blocking collectives, per_device(): gain_grads = lax.psum(gain_grads, ('dp', 'row', 'col'))  63.5 us
    dot_general x5, matrix products, times_transposed(): lax.dot_general(left, right, (((1,), (1,)), ((), ())), preferred_element_...  43.8 us
    all_gather x1, blocking collectives, per_device(): lax.all_gather(jnp.stack([gain_attn, gain_ffn]), ('dp', 'row'), axis=1, t...  35.7 us
    concatenate x4, other arithmetic, gather_col(): near = swap(jnp.concatenate([value, far], axis=1), 'col', 1)  30.8 us
    unnamed x248, local copies, waits for them, and re-layouts  25.7 us
    dot_general x5, matrix products, contract_rows(): lax.dot_general(left, right, (((0,), (0,)), ((), ())), preferred_element_...  24.6 us
  transfers between devices with their start and end apart: 74, of which 30 were waited for; matrix products, arithmetic and copies ran while one was open for 23% of the time, Pallas kernels for 0%

profile of v1, /device:TPU:0, one launch (start us, length us, event | category | flops | bytes accessed | tf_op | source)
XLA Modules:
  0.0 1058.3 jit_solution(17685789766980863923)
XLA Ops:
  1.7 5.1 collective-permute-start.7
  13.8 35.7 %all_gather.3 = bf16[2,2048]{1,0:T(2,128)(2,1)S(1)} all-gather(bf16[2,256]{1,0:T(2,128)(2,1)S(1)} %pad_maximum_fusion.26), channel_id=1, replica_groups=mesh['dp'=4,'row'=2,'col'=4] {'dp','row'}, dimensions={1}, use_global_device_ids=true | all-gather | bytes 9216 | tf_op jit(solution)/shard_map/all_gather | solution.py:305
  52.4 11.8 %collective-permute-start.9 = (bf16[256,512]{1,0:T(8,128)(2,1)S(1)}, bf16[256,512]{1,0:T(8,128)(2,1)S(1)}, u32[]{:S(2)}, u32[]{:S(2)}) collective-permute-start(bf16[256,512]{1,0:T(8,128)(2,1)S(1)} %bitcast.726), channel_id=1, source_target_pairs={{0,8},{8,0},{16,24},{24,16},{1,9},{9,1},{17,25},{25,17},{2,10},{10... | collective-permute-start | bytes 786440 | tf_op jit(solution)/shard_map/ppermute | solution.py:163
  70.9 9.1 collective-permute-done.9
  85.0 23.4 %collective-permute-done.3 = bf16[256,1024]{1,0:T(8,128)(2,1)S(1)} collective-permute-done((bf16[256,1024]{1,0:T(8,128)(2,1)S(1)}, bf16[256,1024]{1,0:T(8,128)(2,1)S(1)}, u32[]{:S(2)}, u32[]{:S(2)}) %collective-permute-start.3) | collective-permute-done | bytes 524320 | tf_op jit(solution)/shard_map/ppermute | solution.py:163
  113.0 63.0 %collective-permute-done.10 = bf16[4,1,256,512]{3,2,0,1:T(8,128)(2,1)S(1)} collective-permute-done((bf16[4,1,256,512]{3,2,0,1:T(8,128)(2,1)S(1)}, bf16[4,1,256,512]{3,2,0,1:T(8,128)(2,1)S(1)}, u32[]{:S(2)}, u32[]{:S(2)}) %collective-permute-start.10) | collective-permute-done | bytes 1048608 | tf_op jit(solution)/shard_map/ppermute | solution.py:163
  187.9 5.4 collective-permute-done.6
  195.6 7.5 while.39
  203.2 9.5 while.40
  204.7 3.1 fusion.218
  209.2 3.4 fusion.218
  220.7 3.4 collective-permute-start.36
  224.1 19.2 %collective-permute-done.35 = bf16[512,512]{1,0:T(8,128)(2,1)S(1)} collective-permute-done((bf16[512,512]{1,0:T(8,128)(2,1)S(1)}, bf16[512,512]{1,0:T(8,128)(2,1)S(1)}, u32[]{:S(2)}, u32[]{:S(2)}) %collective-permute-start.35) | collective-permute-done | bytes 524320 | tf_op jit(solution)/shard_map/ppermute | solution.py:163
  243.3 16.0 %collective-permute-done.36 = bf16[512,512]{1,0:T(8,128)(2,1)S(1)} collective-permute-done((bf16[512,512]{1,0:T(8,128)(2,1)S(1)}, bf16[512,512]{1,0:T(8,128)(2,1)S(1)}, u32[]{:S(2)}, u32[]{:S(2)}) %collective-permute-start.36) | collective-permute-done | bytes 524320 | tf_op jit(solution)/shard_map/ppermute | solution.py:163
  261.8 53.5 %collective-permute-done.12 = bf16[512,512]{1,0:T(8,128)(2,1)S(1)} collective-permute-done((bf16[512,512]{1,0:T(8,128)(2,1)S(1)}, bf16[512,512]{1,0:T(8,128)(2,1)S(1)}, u32[]{:S(2)}, u32[]{:S(2)}) %collective-permute-start.12) | collective-permute-done | bytes 524320 | tf_op jit(solution)/shard_map/ppermute | solution.py:163
  315.7 11.9 %collective-permute-start.13 = (bf16[512,512]{1,0:T(8,128)(2,1)S(1)}, bf16[512,512]{1,0:T(8,128)(2,1)S(1)}, u32[]{:S(2)}, u32[]{:S(2)}) collective-permute-start(bf16[512,512]{1,0:T(8,128)(2,1)S(1)} %fusion.138), channel_id=1, source_target_pairs={{0,8},{8,0},{16,24},{24,16},{1,9},{9,1},{17,25},{25,17},{2,10},{10... | collective-permute-start | bytes 1572872 | tf_op jit(solution)/shard_map/ppermute | solution.py:163
  330.0 16.8 %collective-permute-done.13 = bf16[512,512]{1,0:T(8,128)(2,1)S(1)} collective-permute-done((bf16[512,512]{1,0:T(8,128)(2,1)S(1)}, bf16[512,512]{1,0:T(8,128)(2,1)S(1)}, u32[]{:S(2)}, u32[]{:S(2)}) %collective-permute-start.13) | collective-permute-done | bytes 524320 | tf_op jit(solution)/shard_map/ppermute | solution.py:163
  346.8 18.9 %collective-permute-done.14 = bf16[512,512]{1,0:T(8,128)(2,1)S(1)} collective-permute-done((bf16[512,512]{1,0:T(8,128)(2,1)S(1)}, bf16[512,512]{1,0:T(8,128)(2,1)S(1)}, u32[]{:S(2)}, u32[]{:S(2)}) %collective-permute-start.14) | collective-permute-done | bytes 524320 | tf_op jit(solution)/shard_map/ppermute | solution.py:163
  368.9 14.8 %pad_maximum_fusion.4 = bf16[2048,1024]{1,0:T(8,128)(2,1)} fusion(bf16[2048,512]{1,0:T(8,128)(2,1)S(1)} %collective-permute-done.38, bf16[512,512]{1,0:T(8,128)(2,1)S(1)} %collective-permute-done.37, bf16[512,512]{1,0:T(8,128)(2,1)S(1)} %collective-permute-done.36, bf16[512,512]{1,0:T(8,128)(2,1)S(1)} %collective-permute-done.35, ...), kind=kLoop, calls=%fused_computation.90 | loop fusion | flops 20971520 | bytes 8388608 | tf_op jit(solution)/shard_map/concatenate | solution.py:169
  390.7 7.2 collective-permute-start.27
  404.2 16.3 %collective-permute-done.27 = bf16[256,512]{1,0:T(8,128)(2,1)} collective-permute-done((bf16[256,512]{1,0:T(8,128)(2,1)}, bf16[256,512]{1,0:T(8,128)(2,1)}, u32[]{:S(2)}, u32[]{:S(2)}) %collective-permute-start.27) | collective-permute-done | bytes 262176 | tf_op jit(solution)/shard_map/ppermute | solution.py:163
  420.4 3.0 collective-permute-start.24
  424.3 12.5 %collective-permute-done.23 = bf16[256,512]{1,0:T(8,128)(2,1)} collective-permute-done((bf16[256,512]{1,0:T(8,128)(2,1)}, bf16[256,512]{1,0:T(8,128)(2,1)}, u32[]{:S(2)}, u32[]{:S(2)}) %collective-permute-start.23) | collective-permute-done | bytes 262176 | tf_op jit(solution)/shard_map/ppermute | solution.py:163
  442.4 14.8 %pad_maximum_fusion.2 = bf16[2048,1024]{1,0:T(8,128)(2,1)} fusion(bf16[2048,512]{1,0:T(8,128)(2,1)S(1)} %collective-permute-done.16, bf16[512,512]{1,0:T(8,128)(2,1)S(1)} %copy-done.14, bf16[512,512]{1,0:T(8,128)(2,1)S(1)} %copy-done.11, bf16[512,512]{1,0:T(8,128)(2,1)S(1)} %collective-permute-done.13, bf16[512,512]{1,0:T(8,128)(2,1)S(1)} %fusion.138), kind=kLoop, calls=%fused_computation.88 | loop fusion | flops 20971520 | bytes 8388608 | tf_op jit(solution)/shard_map/concatenate | solution.py:169
  462.0 5.3 collective-permute-done.29
  469.5 20.4 %collective-permute-done.25 = bf16[4,1,256,512]{3,2,0,1:T(8,128)(2,1)} collective-permute-done((bf16[4,1,256,512]{3,2,0,1:T(8,128)(2,1)}, bf16[4,1,256,512]{3,2,0,1:T(8,128)(2,1)}, u32[]{:S(2)}, u32[]{:S(2)}) %collective-permute-start.25) | collective-permute-done | bytes 1048608 | tf_op jit(solution)/shard_map/ppermute | solution.py:163
  491.7 19.3 %collective-permute-done.21 = bf16[4,1,256,512]{3,2,0,1:T(8,128)(2,1)} collective-permute-done((bf16[4,1,256,512]{3,2,0,1:T(8,128)(2,1)}, bf16[4,1,256,512]{3,2,0,1:T(8,128)(2,1)}, u32[]{:S(2)}, u32[]{:S(2)}) %collective-permute-start.21) | collective-permute-done | bytes 1048608 | tf_op jit(solution)/shard_map/ppermute | solution.py:163
  517.5 19.6 %pad_maximum_fusion = bf16[2048,2048]{1,0:T(8,128)(2,1)S(1)} fusion(bf16[2048,512]{1,0:T(8,128)(2,1)S(1)} %get-tuple-element.424, bf16[2048,512]{1,0:T(8,128)(2,1)S(1)} %copy-done.30, bf16[2048,512]{1,0:T(8,128)(2,1)S(1)} %get-tuple-element.423, bf16[512,512]{1,0:T(8,128)(2,1)S(1)} %copy-done.39, bf16[512,512]{1,0:T(8,128)(2,1)S(1)} %copy-done.37, ...), kind=kLoop, calls=%fused_computation.72 | loop fusion | flops 58720256 | bytes 16777216 | tf_op jit(solution)/shard_map/concatenate | solution.py:170
  537.1 5.5 fusion.147
  542.7 15.6 %multiply_reduce_fusion = f32[2048]{0:T(1024)S(1)} fusion(bf16[2048,512]{1,0:T(8,128)(2,1)S(1)} %get-tuple-element.426, bf16[2048,512]{1,0:T(8,128)(2,1)S(1)} %collective-permute-done.16, bf16[2048,512]{1,0:T(8,128)(2,1)S(1)} %get-tuple-element.425, bf16[512,512]{1,0:T(8,128)(2,1)S(1)} %copy-done.15, bf16[512,512]{1,0:T(8,128)(2,1)S(1)} %copy-done.12, ...), kind=kLoop, calls=%fused_computation.70 | loop fusion | flops 67106816 | bytes 8396800 | tf_op jit(solution)/shard_map/reduce_sum | solution.py:47
  558.4 19.3 %multiply_convert_fusion = bf16[2048,2048]{1,0:T(8,128)(2,1)S(1)} fusion(f32[2048]{0:T(1024)S(1)} %bitcast.734, f32[2048]{0:T(1024)S(1)} %add_rsqrt_fusion, bf16[2048,512]{1,0:T(8,128)(2,1)S(1)} %get-tuple-element.426, bf16[2048,512]{1,0:T(8,128)(2,1)S(1)} %collective-permute-done.16, bf16[2048,512]{1,0:T(8,128)(2,1)S(1)} %get-tuple-element.425, ...), kind=kLoop, calls=%fused_computation.69 | loop fusion | flops 71303168 | bytes 16793600 | tf_op jit(solution)/shard_map/convert_element_type | solution.py:48
  577.7 6.0 fusion.161
  583.7 6.2 fusion.160
  589.9 10.3 multiply_convert_fusion.1
  600.2 7.8 fusion.165
  608.0 8.5 fusion.162
  616.5 19.9 %fusion.157 = (bf16[2048,2048]{1,0:T(8,128)(2,1)}, f32[2048,2048]{1,0:T(8,128)}) fusion(f32[2048,2048]{1,0:T(8,128)} %fusion.162, bf16[2048,512]{1,0:T(8,128)(2,1)} %get-tuple-element.415, bf16[2048,512]{1,0:T(8,128)(2,1)} %bitcast.698), kind=kOutput, calls=%fused_computation.386 | convolution fusion | flops 4303355904 | bytes 46137344 | tf_op jit(solution)/shard_map/dot_general | solution.py:65
  643.5 4.6 fusion.166
  654.6 5.0 fusion.164
  662.7 11.7 %fusion.159 = (bf16[2048,2048]{1,0:T(8,128)(2,1)}, f32[2048,2048]{1,0:T(8,128)}) fusion(bf16[2048,512]{1,0:T(8,128)(2,1)S(1)} %copy-done.44, bf16[2048,512]{1,0:T(8,128)(2,1)S(1)} %bitcast.696), kind=kOutput, calls=%fused_computation.388 | convolution fusion | flops 4299161600 | bytes 29360128 | tf_op jit(solution)/shard_map/dot_general | solution.py:65
  682.9 19.9 %maximum_convert_fusion = f32[2048,2048]{1,0:T(8,128)} fusion(bf16[2048,512]{1,0:T(8,128)(2,1)S(1)} %copy-done.6, bf16[2048,512]{1,0:T(8,128)(2,1)S(1)} %collective-permute-done.16, bf16[2048,512]{1,0:T(8,128)(2,1)S(1)} %copy-done.4, bf16[512,512]{1,0:T(8,128)(2,1)S(1)} %copy-done.15, bf16[512,512]{1,0:T(8,128)(2,1)S(1)} %copy-done.12, ...), kind=kLoop, calls=%fused_computation.71 | loop fusion | flops 58720256 | bytes 25165824 | tf_op jit(solution)/shard_map/convert_element_type | solution.py:353
  708.8 9.7 collective-permute-done.62
  724.4 11.1 %collective-permute-done.72 = bf16[256,512]{1,0:T(8,128)(2,1)S(1)} collective-permute-done((bf16[256,512]{1,0:T(8,128)(2,1)S(1)}, bf16[256,512]{1,0:T(8,128)(2,1)S(1)}, u32[]{:S(2)}, u32[]{:S(2)}) %collective-permute-start.72) | collective-permute-done | bytes 262176 | tf_op jit(solution)/shard_map/ppermute | solution.py:163
  736.3 3.4 fusion.140
  739.9 2.9 collective-permute-start.43
  744.6 18.1 %collective-permute-done.42 = bf16[512,512]{1,0:T(8,128)(2,1)S(1)} collective-permute-done((bf16[512,512]{1,0:T(8,128)(2,1)S(1)}, bf16[512,512]{1,0:T(8,128)(2,1)S(1)}, u32[]{:S(2)}, u32[]{:S(2)}) %collective-permute-start.42) | collective-permute-done | bytes 524320 | tf_op jit(solution)/shard_map/ppermute | solution.py:163
  762.7 23.9 %collective-permute-done.43 = bf16[512,512]{1,0:T(8,128)(2,1)S(1)} collective-permute-done((bf16[512,512]{1,0:T(8,128)(2,1)S(1)}, bf16[512,512]{1,0:T(8,128)(2,1)S(1)}, u32[]{:S(2)}, u32[]{:S(2)}) %collective-permute-start.43) | collective-permute-done | bytes 524320 | tf_op jit(solution)/shard_map/ppermute | solution.py:163
  790.9 16.5 %collective-permute-start.64 = (bf16[256,512]{1,0:T(8,128)(2,1)S(1)}, bf16[256,512]{1,0:T(8,128)(2,1)S(1)}, u32[]{:S(2)}, u32[]{:S(2)}) collective-permute-start(bf16[256,512]{1,0:T(8,128)(2,1)S(1)} %copy-done.91), channel_id=1, source_target_pairs={{0,16},{8,24},{16,0},{24,8},{1,17},{9,25},{17,1},{25,9},{2,18},{10... | collective-permute-start | bytes 786440 | tf_op jit(solution)/shard_map/ppermute | solution.py:163
  810.4 3.6 collective-permute-start.46
  822.0 8.8 collective-permute-done.47
  837.4 5.0 fusion.60
  854.5 20.2 %while.41 = (s32[]{:T(128)}, f32[1,2,512,256]{3,2,1,0:T(8,128)}, f32[2,512,1,256]{3,1,2,0:T(8,128)}, f32[2,512,1,256]{3,1,2,0:T(8,128)}, s32[2]{0:T(128)S(1)}, /...) while((s32[]{:T(128)}, f32[1,2,512,256]{3,2,1,0:T(8,128)}, ...), condition=%wide.region_11.12_spmd.clone, body=%wide.region_10.11_spmd.clone.sunk | while | flops 1347159040 | bytes 22300944 | solution.py:149
  878.1 3.1 fusion.163
  887.4 4.5 collective-permute-done.49
  895.0 4.0 fusion.95
  899.0 4.2 copy-done.33
  909.0 7.8 fusion.142
  925.5 5.5 collective-permute-done.59
  931.0 10.9 %collective-permute-done.60 = bf16[256,512]{1,0:T(8,128)(2,1)S(1)} collective-permute-done((bf16[256,512]{1,0:T(8,128)(2,1)S(1)}, bf16[256,512]{1,0:T(8,128)(2,1)S(1)}, u32[]{:S(2)}, u32[]{:S(2)}) %collective-permute-start.60) | collective-permute-done | bytes 262176 | tf_op jit(solution)/shard_map/ppermute | solution.py:163
  947.1 63.5 %psum.7 = f32[2,2048]{1,0:T(2,128)S(1)} all-reduce(f32[2,2048]{1,0:T(2,128)S(1)} %constant_dynamic-update-slice_fusion.3), channel_id=1, replica_groups=mesh['dp'=4,'row'=2,'col'=4] {'dp','row','col'}, use_global_device_ids=true, to_apply=%region_15.16 | all-reduce | flops 4096 | bytes 32768 | tf_op jit(solution)/shard_map/psum | solution.py:447
  1013.7 3.5 bitcast_add_fusion.1
  1022.0 4.1 fusion.72
  1026.1 13.3 %collective-permute-done.55 = bf16[256,1024]{1,0:T(8,128)(2,1)S(1)} collective-permute-done((bf16[256,1024]{1,0:T(8,128)(2,1)S(1)}, bf16[256,1024]{1,0:T(8,128)(2,1)S(1)}, u32[]{:S(2)}, u32[]{:S(2)}) %collective-permute-start.55) | collective-permute-done | bytes 524320 | tf_op jit(solution)/shard_map/ppermute | solution.py:163
  1039.4 16.4 %collective-permute-done.56 = bf16[256,1024]{1,0:T(8,128)(2,1)S(1)} collective-permute-done((bf16[256,1024]{1,0:T(8,128)(2,1)S(1)}, bf16[256,1024]{1,0:T(8,128)(2,1)S(1)}, u32[]{:S(2)}, u32[]{:S(2)}) %collective-permute-start.56) | collective-permute-done | bytes 524320 | tf_op jit(solution)/shard_map/ppermute | solution.py:163
  (557 shorter events, 233.1 us)
Async XLA Ops:
  1.7 65.6 %collective-permute-start.7 = (bf16[256,512]{1,0:T(8,128)(2,1)S(1)}, bf16[256,512]{1,0:T(8,128)(2,1)S(1)}, u32[]{:S(2)}, u32[]{:S(2)}) collective-permute-start(bf16[256,512]{1,0:T(8,128)(2,1)S(1)} %bitcast.724), channel_id=1, source_target_pairs={{0,24},{8,16},{16,8},{24,0},{1,25},{9,17},{17,9},{25,1},{2,26},{10... | collective-permute-start | bytes 786440 | tf_op jit(solution)/shard_map/ppermute | solution.py:163
  6.9 62.5 %collective-permute-start.8 = (bf16[256,512]{1,0:T(8,128)(2,1)S(1)}, bf16[256,512]{1,0:T(8,128)(2,1)S(1)}, u32[]{:S(2)}, u32[]{:S(2)}) collective-permute-start(bf16[256,512]{1,0:T(8,128)(2,1)S(1)} %bitcast.725), channel_id=1, source_target_pairs={{0,16},{8,24},{16,0},{24,8},{1,17},{9,25},{17,1},{25,9},{2,18},{10... | collective-permute-start | bytes 786440 | tf_op jit(solution)/shard_map/ppermute | solution.py:163
  8.1 44.3 %collective-permute-start.18 = (bf16[256,512]{1,0:T(8,128)(2,1)S(1)}, bf16[256,512]{1,0:T(8,128)(2,1)S(1)}, u32[]{:S(2)}, u32[]{:S(2)}) collective-permute-start(bf16[256,512]{1,0:T(8,128)(2,1)S(1)} %get-tuple-element.496), channel_id=1, source_target_pairs={{0,24},{8,16},{16,8},{24,0},{1,25},{9,17},{17,9},{25,1},{2,26},{10... | collective-permute-start | bytes 786440 | tf_op jit(solution)/shard_map/ppermute | solution.py:163
  10.0 54.9 %collective-permute-start.19 = (bf16[256,512]{1,0:T(8,128)(2,1)S(1)}, bf16[256,512]{1,0:T(8,128)(2,1)S(1)}, u32[]{:S(2)}, u32[]{:S(2)}) collective-permute-start(bf16[256,512]{1,0:T(8,128)(2,1)S(1)} %get-tuple-element.497), channel_id=1, source_target_pairs={{0,16},{8,24},{16,0},{24,8},{1,17},{9,25},{17,1},{25,9},{2,18},{10... | collective-permute-start | bytes 786440 | tf_op jit(solution)/shard_map/ppermute | solution.py:163
  11.1 56.2 %collective-permute-start.20 = (bf16[256,512]{1,0:T(8,128)(2,1)S(1)}, bf16[256,512]{1,0:T(8,128)(2,1)S(1)}, u32[]{:S(2)}, u32[]{:S(2)}) collective-permute-start(bf16[256,512]{1,0:T(8,128)(2,1)S(1)} %get-tuple-element.498), channel_id=1, source_target_pairs={{0,8},{8,0},{16,24},{24,16},{1,9},{9,1},{17,25},{25,17},{2,10},{10... | collective-permute-start | bytes 786440 | tf_op jit(solution)/shard_map/ppermute | solution.py:163
  52.4 27.6 %collective-permute-start.9 = (bf16[256,512]{1,0:T(8,128)(2,1)S(1)}, bf16[256,512]{1,0:T(8,128)(2,1)S(1)}, u32[]{:S(2)}, u32[]{:S(2)}) collective-permute-start(bf16[256,512]{1,0:T(8,128)(2,1)S(1)} %bitcast.726), channel_id=1, source_target_pairs={{0,8},{8,0},{16,24},{24,16},{1,9},{9,1},{17,25},{25,17},{2,10},{10... | collective-permute-start | bytes 786440 | tf_op jit(solution)/shard_map/ppermute | solution.py:163
  64.9 20.1 %collective-permute-start.2 = (bf16[256,1024]{1,0:T(8,128)(2,1)S(1)}, bf16[256,1024]{1,0:T(8,128)(2,1)S(1)}, u32[]{:S(2)}, u32[]{:S(2)}) collective-permute-start(bf16[256,1024]{1,0:T(8,128)(2,1)S(1)} %constant_dynamic-update-slice_fusion), channel_id=1, source_target_pairs={{0,24},{8,16},{16,8},{24,0},{1,25},{9,17},{17,9},{25,1},{2,26},{10... | collective-permute-start | bytes 1572872 | tf_op jit(solution)/shard_map/ppermute | solution.py:163
  67.3 41.0 %collective-permute-start.3 = (bf16[256,1024]{1,0:T(8,128)(2,1)S(1)}, bf16[256,1024]{1,0:T(8,128)(2,1)S(1)}, u32[]{:S(2)}, u32[]{:S(2)}) collective-permute-start(bf16[256,1024]{1,0:T(8,128)(2,1)S(1)} %constant_dynamic-update-slice_fusion), channel_id=1, source_target_pairs={{0,16},{8,24},{16,0},{24,8},{1,17},{9,25},{17,1},{25,9},{2,18},{10... | collective-permute-start | bytes 1572872 | tf_op jit(solution)/shard_map/ppermute | solution.py:163
  67.3 41.0 %collective-permute-start.4 = (bf16[256,1024]{1,0:T(8,128)(2,1)S(1)}, bf16[256,1024]{1,0:T(8,128)(2,1)S(1)}, u32[]{:S(2)}, u32[]{:S(2)}) collective-permute-start(bf16[256,1024]{1,0:T(8,128)(2,1)S(1)} %constant_dynamic-update-slice_fusion), channel_id=1, source_target_pairs={{0,8},{8,0},{16,24},{24,16},{1,9},{9,1},{17,25},{25,17},{2,10},{10... | collective-permute-start | bytes 1572872 | tf_op jit(solution)/shard_map/ppermute | solution.py:163
  69.4 42.4 %collective-permute-start = (bf16[512,512]{1,0:T(8,128)(2,1)}, bf16[512,512]{1,0:T(8,128)(2,1)S(1)}, u32[]{:S(2)}, u32[]{:S(2)}) collective-permute-start(bf16[512,512]{1,0:T(8,128)(2,1)} %param.18), channel_id=1, source_target_pairs={{0,2},{1,3},{2,0},{3,1},{4,6},{5,7},{6,4},{7,5},{8,10},{9,11},{10,... | collective-permute-start | bytes 1572872 | tf_op jit(solution)/shard_map/ppermute | solution.py:163
  108.9 68.0 %collective-permute-start.5 = (bf16[4,1,256,1024]{3,2,1,0:T(8,128)(2,1)S(1)}, bf16[4,1,256,1024]{3,2,1,0:T(8,128)(2,1)S(1)}, u32[]{:S(2)}, u32[]{:S(2)}) collective-permute-start(bf16[4,1,256,1024]{3,2,1,0:T(8,128)(2,1)S(1)} %maximum_bitcast_fusion), channel_id=1, source_target_pairs={{0,4},{4,0},{1,5},{5,1},{2,6},{6,2},{3,7},{7,3},{8,12},{12,8},{9,1... | collective-permute-start | bytes 6291464 | tf_op jit(solution)/shard_map/ppermute | solution.py:163
  110.4 65.6 %collective-permute-start.10 = (bf16[4,1,256,512]{3,2,0,1:T(8,128)(2,1)S(1)}, bf16[4,1,256,512]{3,2,0,1:T(8,128)(2,1)S(1)}, u32[]{:S(2)}, u32[]{:S(2)}) collective-permute-start(bf16[4,1,256,512]{3,2,0,1:T(8,128)(2,1)S(1)} %maximum_bitcast_fusion.1), channel_id=1, source_target_pairs={{0,4},{4,0},{1,5},{5,1},{2,6},{6,2},{3,7},{7,3},{8,12},{12,8},{9,1... | collective-permute-start | bytes 3145736 | tf_op jit(solution)/shard_map/ppermute | solution.py:163
  111.9 64.3 %collective-permute-start.1 = (bf16[512,1024]{1,0:T(8,128)(2,1)S(1)}, bf16[512,1024]{1,0:T(8,128)(2,1)S(1)}, u32[]{:S(2)}, u32[]{:S(2)}) collective-permute-start(bf16[512,1024]{1,0:T(8,128)(2,1)S(1)} %pad_maximum_fusion.14), channel_id=1, source_target_pairs={{0,1},{1,0},{2,3},{3,2},{4,5},{5,4},{6,7},{7,6},{8,9},{9,8},{10,11... | collective-permute-start | bytes 3145736 | tf_op jit(solution)/shard_map/ppermute | solution.py:163
  218.3 42.7 %collective-permute-start.11 = (bf16[512,1024]{1,0:T(8,128)(2,1)S(1)}, bf16[512,1024]{1,0:T(8,128)(2,1)S(1)}, u32[]{:S(2)}, u32[]{:S(2)}) collective-permute-start(bf16[512,1024]{1,0:T(8,128)(2,1)S(1)} %pad_maximum_fusion.15), channel_id=1, source_target_pairs={{0,1},{1,0},{2,3},{3,2},{4,5},{5,4},{6,7},{7,6},{8,9},{9,8},{10,11... | collective-permute-start | bytes 3145736 | tf_op jit(solution)/shard_map/ppermute | solution.py:163
  219.7 23.7 %collective-permute-start.35 = (bf16[512,512]{1,0:T(8,128)(2,1)S(1)}, bf16[512,512]{1,0:T(8,128)(2,1)S(1)}, u32[]{:S(2)}, u32[]{:S(2)}) collective-permute-start(bf16[512,512]{1,0:T(8,128)(2,1)S(1)} %multiply_convert_fusion.4), channel_id=1, source_target_pairs={{0,8},{8,0},{16,24},{24,16},{1,9},{9,1},{17,25},{25,17},{2,10},{10... | collective-permute-start | bytes 1572872 | tf_op jit(solution)/shard_map/ppermute | solution.py:163
  220.7 38.6 %collective-permute-start.36 = (bf16[512,512]{1,0:T(8,128)(2,1)S(1)}, bf16[512,512]{1,0:T(8,128)(2,1)S(1)}, u32[]{:S(2)}, u32[]{:S(2)}) collective-permute-start(bf16[512,512]{1,0:T(8,128)(2,1)S(1)} %multiply_convert_fusion.4), channel_id=1, source_target_pairs={{0,16},{8,24},{16,0},{24,8},{1,17},{9,25},{17,1},{25,9},{2,18},{10... | collective-permute-start | bytes 1572872 | tf_op jit(solution)/shard_map/ppermute | solution.py:163
  224.1 35.2 %collective-permute-start.37 = (bf16[512,512]{1,0:T(8,128)(2,1)S(1)}, bf16[512,512]{1,0:T(8,128)(2,1)S(1)}, u32[]{:S(2)}, u32[]{:S(2)}) collective-permute-start(bf16[512,512]{1,0:T(8,128)(2,1)S(1)} %multiply_convert_fusion.4), channel_id=1, source_target_pairs={{0,24},{8,16},{16,8},{24,0},{1,25},{9,17},{17,9},{25,1},{2,26},{10... | collective-permute-start | bytes 1572872 | tf_op jit(solution)/shard_map/ppermute | solution.py:163
  259.5 109.4 %collective-permute-start.38 = (bf16[2048,512]{1,0:T(8,128)(2,1)S(1)}, bf16[2048,512]{1,0:T(8,128)(2,1)S(1)}, u32[]{:S(2)}, u32[]{:S(2)}) collective-permute-start(bf16[2048,512]{1,0:T(8,128)(2,1)S(1)} %pad_maximum_fusion.12), channel_id=1, source_target_pairs={{0,2},{1,3},{2,0},{3,1},{4,6},{5,7},{6,4},{7,5},{8,10},{9,11},{10,... | collective-permute-start | bytes 6291464 | tf_op jit(solution)/shard_map/ppermute | solution.py:163
  261.2 54.1 %collective-permute-start.12 = (bf16[512,512]{1,0:T(8,128)(2,1)S(1)}, bf16[512,512]{1,0:T(8,128)(2,1)S(1)}, u32[]{:S(2)}, u32[]{:S(2)}) collective-permute-start(bf16[512,512]{1,0:T(8,128)(2,1)S(1)} %fusion.93), channel_id=1, source_target_pairs={{0,2},{1,3},{2,0},{3,1},{4,6},{5,7},{6,4},{7,5},{8,10},{9,11},{10,... | collective-permute-start | bytes 1572872 | tf_op jit(solution)/shard_map/ppermute | solution.py:163
  315.7 31.2 %collective-permute-start.13 = (bf16[512,512]{1,0:T(8,128)(2,1)S(1)}, bf16[512,512]{1,0:T(8,128)(2,1)S(1)}, u32[]{:S(2)}, u32[]{:S(2)}) collective-permute-start(bf16[512,512]{1,0:T(8,128)(2,1)S(1)} %fusion.138), channel_id=1, source_target_pairs={{0,8},{8,0},{16,24},{24,16},{1,9},{9,1},{17,25},{25,17},{2,10},{10... | collective-permute-start | bytes 1572872 | tf_op jit(solution)/shard_map/ppermute | solution.py:163
  327.6 38.2 %collective-permute-start.14 = (bf16[512,512]{1,0:T(8,128)(2,1)S(1)}, bf16[512,512]{1,0:T(8,128)(2,1)S(1)}, u32[]{:S(2)}, u32[]{:S(2)}) collective-permute-start(bf16[512,512]{1,0:T(8,128)(2,1)S(1)} %fusion.138), channel_id=1, source_target_pairs={{0,16},{8,24},{16,0},{24,8},{1,17},{9,25},{17,1},{25,9},{2,18},{10... | collective-permute-start | bytes 1572872 | tf_op jit(solution)/shard_map/ppermute | solution.py:163
  328.6 37.1 %collective-permute-start.15 = (bf16[512,512]{1,0:T(8,128)(2,1)S(1)}, bf16[512,512]{1,0:T(8,128)(2,1)S(1)}, u32[]{:S(2)}, u32[]{:S(2)}) collective-permute-start(bf16[512,512]{1,0:T(8,128)(2,1)S(1)} %fusion.138), channel_id=1, source_target_pairs={{0,24},{8,16},{16,8},{24,0},{1,25},{9,17},{17,9},{25,1},{2,26},{10... | collective-permute-start | bytes 1572872 | tf_op jit(solution)/shard_map/ppermute | solution.py:163
  367.4 74.9 %collective-permute-start.16 = (bf16[2048,512]{1,0:T(8,128)(2,1)}, bf16[2048,512]{1,0:T(8,128)(2,1)S(1)}, u32[]{:S(2)}, u32[]{:S(2)}) collective-permute-start(bf16[2048,512]{1,0:T(8,128)(2,1)} %pad_maximum_fusion.8), channel_id=1, source_target_pairs={{0,2},{1,3},{2,0},{3,1},{4,6},{5,7},{6,4},{7,5},{8,10},{9,11},{10,... | collective-permute-start | bytes 6291464 | tf_op jit(solution)/shard_map/ppermute | solution.py:163
  383.7 130.4 %collective-permute-start.39 = (bf16[2048,1024]{1,0:T(8,128)(2,1)}, bf16[2048,1024]{1,0:T(8,128)(2,1)}, u32[]{:S(2)}, u32[]{:S(2)}) collective-permute-start(bf16[2048,1024]{1,0:T(8,128)(2,1)} %pad_maximum_fusion.4), channel_id=1, source_target_pairs={{0,1},{1,0},{2,3},{3,2},{4,5},{5,4},{6,7},{7,6},{8,9},{9,8},{10,11... | collective-permute-start | bytes 12582920 | tf_op jit(solution)/shard_map/ppermute | solution.py:163
  386.5 15.3 %collective-permute-start.26 = (bf16[256,512]{1,0:T(8,128)(2,1)}, bf16[256,512]{1,0:T(8,128)(2,1)}, u32[]{:S(2)}, u32[]{:S(2)}) collective-permute-start(bf16[256,512]{1,0:T(8,128)(2,1)} %bitcast.731), channel_id=1, source_target_pairs={{0,24},{8,16},{16,8},{24,0},{1,25},{9,17},{17,9},{25,1},{2,26},{10... | collective-permute-start | bytes 786440 | tf_op jit(solution)/shard_map/ppermute | solution.py:163
  390.7 29.7 %collective-permute-start.27 = (bf16[256,512]{1,0:T(8,128)(2,1)}, bf16[256,512]{1,0:T(8,128)(2,1)}, u32[]{:S(2)}, u32[]{:S(2)}) collective-permute-start(bf16[256,512]{1,0:T(8,128)(2,1)} %bitcast.730), channel_id=1, source_target_pairs={{0,16},{8,24},{16,0},{24,8},{1,17},{9,25},{17,1},{25,9},{2,18},{10... | collective-permute-start | bytes 786440 | tf_op jit(solution)/shard_map/ppermute | solution.py:163
  399.7 20.7 %collective-permute-start.28 = (bf16[256,512]{1,0:T(8,128)(2,1)}, bf16[256,512]{1,0:T(8,128)(2,1)}, u32[]{:S(2)}, u32[]{:S(2)}) collective-permute-start(bf16[256,512]{1,0:T(8,128)(2,1)} %bitcast.729), channel_id=1, source_target_pairs={{0,8},{8,0},{16,24},{24,16},{1,9},{9,1},{17,25},{25,17},{2,10},{10... | collective-permute-start | bytes 786440 | tf_op jit(solution)/shard_map/ppermute | solution.py:163
  401.8 22.5 %collective-permute-start.22 = (bf16[256,512]{1,0:T(8,128)(2,1)}, bf16[256,512]{1,0:T(8,128)(2,1)}, u32[]{:S(2)}, u32[]{:S(2)}) collective-permute-start(bf16[256,512]{1,0:T(8,128)(2,1)} %get-tuple-element.499), channel_id=1, source_target_pairs={{0,24},{8,16},{16,8},{24,0},{1,25},{9,17},{17,9},{25,1},{2,26},{10... | collective-permute-start | bytes 786440 | tf_op jit(solution)/shard_map/ppermute | solution.py:163
  420.4 16.4 %collective-permute-start.23 = (bf16[256,512]{1,0:T(8,128)(2,1)}, bf16[256,512]{1,0:T(8,128)(2,1)}, u32[]{:S(2)}, u32[]{:S(2)}) collective-permute-start(bf16[256,512]{1,0:T(8,128)(2,1)} %get-tuple-element.500), channel_id=1, source_target_pairs={{0,16},{8,24},{16,0},{24,8},{1,17},{9,25},{17,1},{25,9},{2,18},{10... | collective-permute-start | bytes 786440 | tf_op jit(solution)/shard_map/ppermute | solution.py:163
  420.4 16.4 %collective-permute-start.24 = (bf16[256,512]{1,0:T(8,128)(2,1)}, bf16[256,512]{1,0:T(8,128)(2,1)}, u32[]{:S(2)}, u32[]{:S(2)}) collective-permute-start(bf16[256,512]{1,0:T(8,128)(2,1)} %get-tuple-element.501), channel_id=1, source_target_pairs={{0,8},{8,0},{16,24},{24,16},{1,9},{9,1},{17,25},{25,17},{2,10},{10... | collective-permute-start | bytes 786440 | tf_op jit(solution)/shard_map/ppermute | solution.py:163
  441.0 26.4 %collective-permute-start.29 = (bf16[4,1,256,512]{3,2,0,1:T(8,128)(2,1)}, bf16[4,1,256,512]{3,2,0,1:T(8,128)(2,1)}, u32[]{:S(2)}, u32[]{:S(2)}) collective-permute-start(bf16[4,1,256,512]{3,2,0,1:T(8,128)(2,1)} %maximum_bitcast_fusion.4), channel_id=1, source_target_pairs={{0,4},{4,0},{1,5},{5,1},{2,6},{6,2},{3,7},{7,3},{8,12},{12,8},{9,1... | collective-permute-start | bytes 3145736 | tf_op jit(solution)/shard_map/ppermute | solution.py:163
  457.2 80.0 %collective-permute-start.17 = (bf16[2048,1024]{1,0:T(8,128)(2,1)}, bf16[2048,1024]{1,0:T(8,128)(2,1)}, u32[]{:S(2)}, u32[]{:S(2)}) collective-permute-start(bf16[2048,1024]{1,0:T(8,128)(2,1)} %pad_maximum_fusion.2), channel_id=1, source_target_pairs={{0,1},{1,0},{2,3},{3,2},{4,5},{5,4},{6,7},{7,6},{8,9},{9,8},{10,11... | collective-permute-start | bytes 12582920 | tf_op jit(solution)/shard_map/ppermute | solution.py:163
  458.3 31.6 %collective-permute-start.25 = (bf16[4,1,256,512]{3,2,0,1:T(8,128)(2,1)}, bf16[4,1,256,512]{3,2,0,1:T(8,128)(2,1)}, u32[]{:S(2)}, u32[]{:S(2)}) collective-permute-start(bf16[4,1,256,512]{3,2,0,1:T(8,128)(2,1)} %maximum_bitcast_fusion.3), channel_id=1, source_target_pairs={{0,4},{4,0},{1,5},{5,1},{2,6},{6,2},{3,7},{7,3},{8,12},{12,8},{9,1... | collective-permute-start | bytes 3145736 | tf_op jit(solution)/shard_map/ppermute | solution.py:163
  460.1 50.8 %collective-permute-start.21 = (bf16[4,1,256,512]{3,2,0,1:T(8,128)(2,1)}, bf16[4,1,256,512]{3,2,0,1:T(8,128)(2,1)}, u32[]{:S(2)}, u32[]{:S(2)}) collective-permute-start(bf16[4,1,256,512]{3,2,0,1:T(8,128)(2,1)} %maximum_bitcast_fusion.2), channel_id=1, source_target_pairs={{0,4},{4,0},{1,5},{5,1},{2,6},{6,2},{3,7},{7,3},{8,12},{12,8},{9,1... | collective-permute-start | bytes 3145736 | tf_op jit(solution)/shard_map/ppermute | solution.py:163
  641.9 37.6 %collective-permute-start.40 = (bf16[2048,1024]{1,0:T(8,128)(2,1)}, bf16[2048,1024]{1,0:T(8,128)(2,1)}, u32[]{:S(2)}, u32[]{:S(2)}) collective-permute-start(bf16[2048,1024]{1,0:T(8,128)(2,1)} %pad_maximum_fusion.5), channel_id=1, source_target_pairs={{0,1},{1,0},{2,3},{3,2},{4,5},{5,4},{6,7},{7,6},{8,9},{9,8},{10,11... | collective-permute-start | bytes 12582920 | tf_op jit(solution)/shard_map/ppermute | solution.py:163
  649.2 53.6 %collective-permute-start.70 = (bf16[4,256,512]{2,1,0:T(8,128)(2,1)}, bf16[4,256,512]{2,1,0:T(8,128)(2,1)}, u32[]{:S(2)}, u32[]{:S(2)}) collective-permute-start(bf16[4,256,512]{2,1,0:T(8,128)(2,1)} %fusion.79), channel_id=1, source_target_pairs={{0,4},{4,0},{1,5},{5,1},{2,6},{6,2},{3,7},{7,3},{8,12},{12,8},{9,1... | collective-permute-start | bytes 3145736 | tf_op jit(solution)/shard_map/ppermute | solution.py:163
  653.3 53.9 %collective-permute-start.66 = (bf16[4,256,512]{2,1,0:T(8,128)(2,1)}, bf16[4,256,512]{2,1,0:T(8,128)(2,1)}, u32[]{:S(2)}, u32[]{:S(2)}) collective-permute-start(bf16[4,256,512]{2,1,0:T(8,128)(2,1)} %fusion.78), channel_id=1, source_target_pairs={{0,4},{4,0},{1,5},{5,1},{2,6},{6,2},{3,7},{7,3},{8,12},{12,8},{9,1... | collective-permute-start | bytes 3145736 | tf_op jit(solution)/shard_map/ppermute | solution.py:163
  661.9 56.6 %collective-permute-start.62 = (bf16[4,256,512]{2,1,0:T(8,128)(2,1)}, bf16[4,256,512]{2,1,0:T(8,128)(2,1)}, u32[]{:S(2)}, u32[]{:S(2)}) collective-permute-start(bf16[4,256,512]{2,1,0:T(8,128)(2,1)} %fusion.77), channel_id=1, source_target_pairs={{0,4},{4,0},{1,5},{5,1},{2,6},{6,2},{3,7},{7,3},{8,12},{12,8},{9,1... | collective-permute-start | bytes 3145736 | tf_op jit(solution)/shard_map/ppermute | solution.py:163
  679.5 157.9 %collective-permute-start.30 = (bf16[2048,1024]{1,0:T(8,128)(2,1)}, bf16[2048,1024]{1,0:T(8,128)(2,1)}, u32[]{:S(2)}, u32[]{:S(2)}) collective-permute-start(bf16[2048,1024]{1,0:T(8,128)(2,1)} %pad_maximum_fusion.3), channel_id=1, source_target_pairs={{0,1},{1,0},{2,3},{3,2},{4,5},{5,4},{6,7},{7,6},{8,9},{9,8},{10,11... | collective-permute-start | bytes 12582920 | tf_op jit(solution)/shard_map/ppermute | solution.py:163
  682.2 54.0 %collective-permute-start.41 = (bf16[2048,512]{1,0:T(8,128)(2,1)S(1)}, bf16[2048,512]{1,0:T(8,128)(2,1)}, u32[]{:S(2)}, u32[]{:S(2)}) collective-permute-start(bf16[2048,512]{1,0:T(8,128)(2,1)S(1)} %fusion.58), channel_id=1, source_target_pairs={{0,2},{1,3},{2,0},{3,1},{4,6},{5,7},{6,4},{7,5},{8,10},{9,11},{10,... | collective-permute-start | bytes 6291464 | tf_op jit(solution)/shard_map/ppermute | solution.py:163
  704.8 17.2 %collective-permute-start.71 = (bf16[256,512]{1,0:T(8,128)(2,1)S(1)}, bf16[256,512]{1,0:T(8,128)(2,1)S(1)}, u32[]{:S(2)}, u32[]{:S(2)}) collective-permute-start(bf16[256,512]{1,0:T(8,128)(2,1)S(1)} %get-tuple-element.470), channel_id=1, source_target_pairs={{0,24},{8,16},{16,8},{24,0},{1,25},{9,17},{17,9},{25,1},{2,26},{10... | collective-permute-start | bytes 786440 | tf_op jit(solution)/shard_map/ppermute | solution.py:163
  707.2 28.3 %collective-permute-start.72 = (bf16[256,512]{1,0:T(8,128)(2,1)S(1)}, bf16[256,512]{1,0:T(8,128)(2,1)S(1)}, u32[]{:S(2)}, u32[]{:S(2)}) collective-permute-start(bf16[256,512]{1,0:T(8,128)(2,1)S(1)} %get-tuple-element.471), channel_id=1, source_target_pairs={{0,16},{8,24},{16,0},{24,8},{1,17},{9,25},{17,1},{25,9},{2,18},{10... | collective-permute-start | bytes 786440 | tf_op jit(solution)/shard_map/ppermute | solution.py:163
  718.5 17.6 %collective-permute-start.73 = (bf16[256,512]{1,0:T(8,128)(2,1)S(1)}, bf16[256,512]{1,0:T(8,128)(2,1)S(1)}, u32[]{:S(2)}, u32[]{:S(2)}) collective-permute-start(bf16[256,512]{1,0:T(8,128)(2,1)S(1)} %get-tuple-element.469), channel_id=1, source_target_pairs={{0,8},{8,0},{16,24},{24,16},{1,9},{9,1},{17,25},{25,17},{2,10},{10... | collective-permute-start | bytes 786440 | tf_op jit(solution)/shard_map/ppermute | solution.py:163
  722.0 68.9 %collective-permute-start.67 = (bf16[256,512]{1,0:T(8,128)(2,1)}, bf16[256,512]{1,0:T(8,128)(2,1)S(1)}, u32[]{:S(2)}, u32[]{:S(2)}) collective-permute-start(bf16[256,512]{1,0:T(8,128)(2,1)} %get-tuple-element.476), channel_id=1, source_target_pairs={{0,24},{8,16},{16,8},{24,0},{1,25},{9,17},{17,9},{25,1},{2,26},{10... | collective-permute-start | bytes 786440 | tf_op jit(solution)/shard_map/ppermute | solution.py:163
  739.8 22.9 %collective-permute-start.42 = (bf16[512,512]{1,0:T(8,128)(2,1)S(1)}, bf16[512,512]{1,0:T(8,128)(2,1)S(1)}, u32[]{:S(2)}, u32[]{:S(2)}) collective-permute-start(bf16[512,512]{1,0:T(8,128)(2,1)S(1)} %get-tuple-element.434), channel_id=1, source_target_pairs={{0,8},{8,0},{16,24},{24,16},{1,9},{9,1},{17,25},{25,17},{2,10},{10... | collective-permute-start | bytes 1572872 | tf_op jit(solution)/shard_map/ppermute | solution.py:163
  739.9 46.7 %collective-permute-start.43 = (bf16[512,512]{1,0:T(8,128)(2,1)S(1)}, bf16[512,512]{1,0:T(8,128)(2,1)S(1)}, u32[]{:S(2)}, u32[]{:S(2)}) collective-permute-start(bf16[512,512]{1,0:T(8,128)(2,1)S(1)} %get-tuple-element.436), channel_id=1, source_target_pairs={{0,16},{8,24},{16,0},{24,8},{1,17},{9,25},{17,1},{25,9},{2,18},{10... | collective-permute-start | bytes 1572872 | tf_op jit(solution)/shard_map/ppermute | solution.py:163
  742.8 43.8 %collective-permute-start.44 = (bf16[512,512]{1,0:T(8,128)(2,1)S(1)}, bf16[512,512]{1,0:T(8,128)(2,1)S(1)}, u32[]{:S(2)}, u32[]{:S(2)}) collective-permute-start(bf16[512,512]{1,0:T(8,128)(2,1)S(1)} %get-tuple-element.435), channel_id=1, source_target_pairs={{0,24},{8,16},{16,8},{24,0},{1,25},{9,17},{17,9},{25,1},{2,26},{10... | collective-permute-start | bytes 1572872 | tf_op jit(solution)/shard_map/ppermute | solution.py:163
  762.7 46.5 %collective-permute-start.68 = (bf16[256,512]{1,0:T(8,128)(2,1)S(1)}, bf16[256,512]{1,0:T(8,128)(2,1)S(1)}, u32[]{:S(2)}, u32[]{:S(2)}) collective-permute-start(bf16[256,512]{1,0:T(8,128)(2,1)S(1)} %copy-done.94), channel_id=1, source_target_pairs={{0,16},{8,24},{16,0},{24,8},{1,17},{9,25},{17,1},{25,9},{2,18},{10... | collective-permute-start | bytes 786440 | tf_op jit(solution)/shard_map/ppermute | solution.py:163
  786.6 22.6 %collective-permute-start.69 = (bf16[256,512]{1,0:T(8,128)(2,1)S(1)}, bf16[256,512]{1,0:T(8,128)(2,1)S(1)}, u32[]{:S(2)}, u32[]{:S(2)}) collective-permute-start(bf16[256,512]{1,0:T(8,128)(2,1)S(1)} %copy-done.93), channel_id=1, source_target_pairs={{0,8},{8,0},{16,24},{24,16},{1,9},{9,1},{17,25},{25,17},{2,10},{10... | collective-permute-start | bytes 786440 | tf_op jit(solution)/shard_map/ppermute | solution.py:163
  786.7 32.7 %collective-permute-start.63 = (bf16[256,512]{1,0:T(8,128)(2,1)S(1)}, bf16[256,512]{1,0:T(8,128)(2,1)S(1)}, u32[]{:S(2)}, u32[]{:S(2)}) collective-permute-start(bf16[256,512]{1,0:T(8,128)(2,1)S(1)} %copy-done.92), channel_id=1, source_target_pairs={{0,24},{8,16},{16,8},{24,0},{1,25},{9,17},{17,9},{25,1},{2,26},{10... | collective-permute-start | bytes 786440 | tf_op jit(solution)/shard_map/ppermute | solution.py:163
  790.9 29.4 %collective-permute-start.64 = (bf16[256,512]{1,0:T(8,128)(2,1)S(1)}, bf16[256,512]{1,0:T(8,128)(2,1)S(1)}, u32[]{:S(2)}, u32[]{:S(2)}) collective-permute-start(bf16[256,512]{1,0:T(8,128)(2,1)S(1)} %copy-done.91), channel_id=1, source_target_pairs={{0,16},{8,24},{16,0},{24,8},{1,17},{9,25},{17,1},{25,9},{2,18},{10... | collective-permute-start | bytes 786440 | tf_op jit(solution)/shard_map/ppermute | solution.py:163
  842.4 66.6 %collective-permute-start.31 = (bf16[2048,512]{1,0:T(8,128)(2,1)}, bf16[2048,512]{1,0:T(8,128)(2,1)}, u32[]{:S(2)}, u32[]{:S(2)}) collective-permute-start(bf16[2048,512]{1,0:T(8,128)(2,1)} %fusion.60), channel_id=1, source_target_pairs={{0,2},{1,3},{2,0},{3,1},{4,6},{5,7},{6,4},{7,5},{8,10},{9,11},{10,... | collective-permute-start | bytes 6291464 | tf_op jit(solution)/shard_map/ppermute | solution.py:163
  884.3 32.5 %collective-permute-start.58 = (bf16[4,256,512]{2,1,0:T(8,128)(2,1)}, bf16[4,256,512]{2,1,0:T(8,128)(2,1)}, u32[]{:S(2)}, u32[]{:S(2)}) collective-permute-start(bf16[4,256,512]{2,1,0:T(8,128)(2,1)} %fusion.76), channel_id=1, source_target_pairs={{0,4},{4,0},{1,5},{5,1},{2,6},{6,2},{3,7},{7,3},{8,12},{12,8},{9,1... | collective-permute-start | bytes 3145736 | tf_op jit(solution)/shard_map/ppermute | solution.py:163
  904.9 108.7 %collective-permute-start.54 = (bf16[4,256,1024]{2,1,0:T(8,128)(2,1)}, bf16[4,256,1024]{2,1,0:T(8,128)(2,1)}, u32[]{:S(2)}, u32[]{:S(2)}) collective-permute-start(bf16[4,256,1024]{2,1,0:T(8,128)(2,1)} %fusion.63), channel_id=1, source_target_pairs={{0,4},{4,0},{1,5},{5,1},{2,6},{6,2},{3,7},{7,3},{8,12},{12,8},{9,1... | collective-permute-start | bytes 6291464 | tf_op jit(solution)/shard_map/ppermute | solution.py:163
  920.6 21.4 %collective-permute-start.60 = (bf16[256,512]{1,0:T(8,128)(2,1)S(1)}, bf16[256,512]{1,0:T(8,128)(2,1)S(1)}, u32[]{:S(2)}, u32[]{:S(2)}) collective-permute-start(bf16[256,512]{1,0:T(8,128)(2,1)S(1)} %get-tuple-element.431), channel_id=1, source_target_pairs={{0,16},{8,24},{16,0},{24,8},{1,17},{9,25},{17,1},{25,9},{2,18},{10... | collective-permute-start | bytes 786440 | tf_op jit(solution)/shard_map/ppermute | solution.py:163
  921.2 20.7 %collective-permute-start.61 = (bf16[256,512]{1,0:T(8,128)(2,1)S(1)}, bf16[256,512]{1,0:T(8,128)(2,1)S(1)}, u32[]{:S(2)}, u32[]{:S(2)}) collective-permute-start(bf16[256,512]{1,0:T(8,128)(2,1)S(1)} %get-tuple-element.430), channel_id=1, source_target_pairs={{0,24},{8,16},{16,8},{24,0},{1,25},{9,17},{17,9},{25,1},{2,26},{10... | collective-permute-start | bytes 786440 | tf_op jit(solution)/shard_map/ppermute | solution.py:163
  924.0 21.3 %collective-permute-start.51 = (bf16[512,512]{1,0:T(8,128)(2,1)}, bf16[512,512]{1,0:T(8,128)(2,1)S(1)}, u32[]{:S(2)}, u32[]{:S(2)}) collective-permute-start(bf16[512,512]{1,0:T(8,128)(2,1)} %fusion.85), channel_id=1, source_target_pairs={{0,2},{1,3},{2,0},{3,1},{4,6},{5,7},{6,4},{7,5},{8,10},{9,11},{10,... | collective-permute-start | bytes 1572872 | tf_op jit(solution)/shard_map/ppermute | solution.py:163
  931.0 86.5 %collective-permute-start.32 = (bf16[512,512]{1,0:T(8,128)(2,1)}, bf16[512,512]{1,0:T(8,128)(2,1)S(1)}, u32[]{:S(2)}, u32[]{:S(2)}) collective-permute-start(bf16[512,512]{1,0:T(8,128)(2,1)} %get-tuple-element.437), channel_id=1, source_target_pairs={{0,8},{8,0},{16,24},{24,16},{1,9},{9,1},{17,25},{25,17},{2,10},{10... | collective-permute-start | bytes 1572872 | tf_op jit(solution)/shard_map/ppermute | solution.py:163
  941.9 80.0 %collective-permute-start.33 = (bf16[512,512]{1,0:T(8,128)(2,1)}, bf16[512,512]{1,0:T(8,128)(2,1)}, u32[]{:S(2)}, u32[]{:S(2)}) collective-permute-start(bf16[512,512]{1,0:T(8,128)(2,1)} %get-tuple-element.439), channel_id=1, source_target_pairs={{0,16},{8,24},{16,0},{24,8},{1,17},{9,25},{17,1},{25,9},{2,18},{10... | collective-permute-start | bytes 1572872 | tf_op jit(solution)/shard_map/ppermute | solution.py:163
  941.9 80.0 %collective-permute-start.34 = (bf16[512,512]{1,0:T(8,128)(2,1)}, bf16[512,512]{1,0:T(8,128)(2,1)}, u32[]{:S(2)}, u32[]{:S(2)}) collective-permute-start(bf16[512,512]{1,0:T(8,128)(2,1)} %get-tuple-element.438), channel_id=1, source_target_pairs={{0,24},{8,16},{16,8},{24,0},{1,25},{9,17},{17,9},{25,1},{2,26},{10... | collective-permute-start | bytes 1572872 | tf_op jit(solution)/shard_map/ppermute | solution.py:163
  947.0 64.3 %collective-permute-start.52 = (f32[512,1]{0,1:T(1,128)S(1)}, f32[512,1]{0,1:T(1,128)S(1)}, u32[]{:S(2)}, u32[]{:S(2)}) collective-permute-start(f32[512,1]{0,1:T(1,128)S(1)} %bitcast.744), channel_id=1, source_target_pairs={{0,1},{1,0},{2,3},{3,2},{4,5},{5,4},{6,7},{7,6},{8,9},{9,8},{10,11... | collective-permute-start | bytes 6152 | tf_op jit(solution)/shard_map/ppermute | solution.py:163
  1017.4 21.9 %collective-permute-start.55 = (bf16[256,1024]{1,0:T(8,128)(2,1)S(1)}, bf16[256,1024]{1,0:T(8,128)(2,1)S(1)}, u32[]{:S(2)}, u32[]{:S(2)}) collective-permute-start(bf16[256,1024]{1,0:T(8,128)(2,1)S(1)} %get-tuple-element.420), channel_id=1, source_target_pairs={{0,8},{8,0},{16,24},{24,16},{1,9},{9,1},{17,25},{25,17},{2,10},{10... | collective-permute-start | bytes 1572872 | tf_op jit(solution)/shard_map/ppermute | solution.py:163
  1017.5 38.2 %collective-permute-start.56 = (bf16[256,1024]{1,0:T(8,128)(2,1)S(1)}, bf16[256,1024]{1,0:T(8,128)(2,1)S(1)}, u32[]{:S(2)}, u32[]{:S(2)}) collective-permute-start(bf16[256,1024]{1,0:T(8,128)(2,1)S(1)} %get-tuple-element.422), channel_id=1, source_target_pairs={{0,16},{8,24},{16,0},{24,8},{1,17},{9,25},{17,1},{25,9},{2,18},{10... | collective-permute-start | bytes 1572872 | tf_op jit(solution)/shard_map/ppermute | solution.py:163
  1019.9 35.9 %collective-permute-start.57 = (bf16[256,1024]{1,0:T(8,128)(2,1)S(1)}, bf16[256,1024]{1,0:T(8,128)(2,1)S(1)}, u32[]{:S(2)}, u32[]{:S(2)}) collective-permute-start(bf16[256,1024]{1,0:T(8,128)(2,1)S(1)} %get-tuple-element.421), channel_id=1, source_target_pairs={{0,24},{8,16},{16,8},{24,0},{1,25},{9,17},{17,9},{25,1},{2,26},{10... | collective-permute-start | bytes 1572872 | tf_op jit(solution)/shard_map/ppermute | solution.py:163
  (135 other events, 2803.5 us)

commit v2 on v1

--- a/solution.py
+++ b/solution.py
@@ -3,6 +3,8 @@
 import jax
 import jax.numpy as jnp
 from jax import lax
+from jax.experimental import pallas as pl
+from jax.experimental.pallas import tpu as pltpu
 from jax.sharding import PartitionSpec as P
 
 QUERY_HEADS = 8
@@ -272,6 +274,451 @@
             own[j * rows : (j + 1) * rows].astype(jnp.bfloat16), "dp", j
         ).astype(jnp.float32)
     return total
+
+
+def dot_nn(left, right):
+    return lax.dot_general(left, right, (((1,), (0,)), ((), ())), preferred_element_type=jnp.float32)
+
+
+def tiles(count, size, body):
+    def step(i, unused):
+        body(pl.ds(pl.multiple_of(i * size, size), size))
+        return unused
+
+    lax.fori_loop(0, count // size, step, 0)
+
+
+def remote(src, dst, send_sem, recv_sem, target):
+    return pltpu.make_async_remote_copy(
+        src_ref=src,
+        dst_ref=dst,
+        send_sem=send_sem,
+        recv_sem=recv_sem,
+        device_id=target,
+        device_id_type=pl.DeviceIdType.MESH,
+    )
+
+
+def greet(targets):
+    barrier = pltpu.get_barrier_semaphore()
+    for target in targets:
+        pl.semaphore_signal(
+            barrier, inc=1, device_id=target, device_id_type=pl.DeviceIdType.MESH
+        )
+    pl.semaphore_wait(barrier, len(targets))
+
+
+def ffn_kernel(
+    h_ref,
+    gain_ref,
+    do_hbm,
+    wg_hbm,
+    wu_hbm,
+    wd_hbm,
+    dhn_ref,
+    factor_ref,
+    out_hbm,
+    dwg_hbm,
+    dwu_hbm,
+    dwd_hbm,
+    full,
+    do,
+    wg,
+    wu,
+    wd,
+    hid,
+    dg,
+    du,
+    gate,
+    up,
+    dhid,
+    part,
+    outp,
+    core_in,
+    x_out,
+    x_in,
+    z_out,
+    z_in,
+    stage,
+    load_sem,
+    z_send,
+    f_send,
+    z_recv,
+    x_send,
+    x_recv,
+    c_send,
+    c_recv,
+    p_send,
+    p_recv,
+    rx_send,
+    rx_recv,
+    rz_send,
+    rz_recv,
+    o_sem,
+    s_sem,
+):
+    rows, width = h_ref.shape
+    model = width * 4
+    hidden = wg.shape[1]
+    low, wide = jnp.bfloat16, jnp.float32
+    z, col = lax.axis_index("dp"), lax.axis_index("col")
+    core, far = {"col": col ^ 1}, {"col": col ^ 2}
+    mid = jnp.logical_and(z > 0, z < 3)
+
+    def chunk(s):
+        return jnp.where(jnp.logical_and(mid, s >= 2), 5 - s, s)
+
+    def cols(p):
+        return pl.ds(p * width, width)
+
+    greet([{"dp": z ^ 1}, {"dp": z ^ 2}, {"dp": z ^ 3}, core, far])
+
+    def z_own(target, index):
+        slot = z ^ target
+        return remote(
+            h_ref, full.at[slot, :, cols(0)], z_send.at[index], z_recv.at[slot], {"dp": target}
+        )
+
+    @pl.when(z < 3)
+    def _():
+        z_own(z + 1, 0).start()
+
+    @pl.when(z > 0)
+    def _():
+        z_own(z - 1, 1).start()
+
+    def x_copy(j, src):
+        return remote(src, full.at[j, :, cols(2)], x_send.at[j], x_recv.at[j], far)
+
+    def c_copy(j, src, which):
+        return remote(
+            src, full.at[j, :, cols(1 + 2 * which)], c_send.at[which, j], c_recv.at[which, j], core
+        )
+
+    x_copy(0, h_ref).start()
+    c_copy(0, h_ref, 0).start()
+    loads = [
+        pltpu.make_async_copy(wg_hbm, wg, load_sem.at[0]),
+        pltpu.make_async_copy(wu_hbm, wu, load_sem.at[1]),
+        pltpu.make_async_copy(wd_hbm, wd, load_sem.at[2]),
+    ]
+    for load in loads:
+        load.start()
+
+    def do_load(j):
+        return pltpu.make_async_copy(do_hbm.at[j], do.at[j], load_sem.at[3 + j])
+
+    for j in range(4):
+        do_load(j).start()
+
+    def copy_own(r):
+        full[0, r, 0:width] = h_ref[r, :]
+
+    tiles(rows, 64, copy_own)
+
+    def forward(j, target):
+        return remote(
+            full.at[j, :, cols(0)],
+            full.at[(z ^ j) ^ target, :, cols(0)],
+            f_send.at[j],
+            z_recv.at[(z ^ j) ^ target],
+            {"dp": target},
+        )
+
+    def goes_up(j):
+        return jnp.logical_and((z ^ j) < z, z < 3)
+
+    def goes_down(j):
+        return jnp.logical_and((z ^ j) > z, z > 0)
+
+    def arrive(j):
+        block = full.at[j, :, cols(0)]
+        remote(block, block, f_send.at[j], z_recv.at[j], core).wait_recv()
+
+        @pl.when(goes_up(j))
+        def _():
+            forward(j, z + 1).start()
+
+        @pl.when(goes_down(j))
+        def _():
+            forward(j, z - 1).start()
+
+        x_copy(j, block).start()
+        c_copy(j, block, 0).start()
+
+    def settle(j):
+        block = full.at[j, :, cols(0)]
+        x_copy(j, block).wait_recv()
+        c_copy(j, full.at[j, :, cols(2)], 1).start()
+        x_copy(j, block).wait_send()
+        c_copy(j, block, 0).wait_send()
+
+        @pl.when(jnp.logical_and(j > 0, jnp.logical_or(goes_up(j), goes_down(j))))
+        def _():
+            forward(j, z ^ j).wait_send()
+
+        c_copy(j, block, 0).wait_recv()
+        c_copy(j, block, 1).wait()
+
+    def part_copy(s, slot):
+        return remote(
+            part.at[slot, :, pl.ds(2 * width, 2 * width)],
+            core_in.at[s],
+            p_send.at[s],
+            p_recv.at[s],
+            core,
+        )
+
+    def rx_copy(s):
+        return remote(x_out.at[s], x_in.at[s], rx_send.at[s], rx_recv.at[s], far)
+
+    def rz_copy(s, j):
+        return remote(z_out.at[s], z_in.at[j], rz_send.at[s], rz_recv.at[j], {"dp": z ^ j})
+
+    def reduce_core(s):
+        slot = lax.rem(s, 2)
+        part_copy(s, slot).wait()
+
+        def add(r):
+            x_out[s, r, :] = (
+                part[slot, r, width : 2 * width].astype(wide)
+                + core_in[s, r, width : 2 * width].astype(wide)
+            ).astype(low)
+            z_out[s, r, :] = (
+                part[slot, r, 0:width].astype(wide) + core_in[s, r, 0:width].astype(wide)
+            ).astype(low)
+
+        tiles(rows, 64, add)
+        rx_copy(s).start()
+
+    def reduce_far(s):
+        rx_copy(s).wait()
+
+        def add(r):
+            z_out[s, r, :] = (z_out[s, r, :].astype(wide) + x_in[s, r, :].astype(wide)).astype(low)
+
+        tiles(rows, 64, add)
+
+        @pl.when(s > 0)
+        def _():
+            rz_copy(s, chunk(s)).start()
+
+    def out_copy(s):
+        return pltpu.make_async_copy(
+            outp.at[lax.rem(s, 2)], out_hbm.at[chunk(s)], o_sem.at[lax.rem(s, 2)]
+        )
+
+    def step(s, unused):
+        j = chunk(s)
+        base = s * rows
+
+        @pl.when(jnp.logical_and(s < 3, jnp.logical_not(jnp.logical_and(s == 1, mid))))
+        def _():
+            arrive(chunk(s + 1))
+
+        @pl.when(jnp.logical_and(s == 0, mid))
+        def _():
+            arrive(chunk(2))
+
+        settle(j)
+
+        def norm(r):
+            x = full[j, r, :].astype(wide)
+            factor = lax.rsqrt(jnp.sum(x * x, axis=1, keepdims=True) * (1.0 / model) + EPSILON)
+            full[j, r, :] = (x * factor * gain_ref[...]).astype(low)
+
+            @pl.when(s == 0)
+            def _():
+                factor_ref[r, :] = jnp.broadcast_to(factor, (factor.shape[0], 128))
+
+        tiles(rows, 32, norm)
+
+        @pl.when(s == 0)
+        def _():
+            for load in loads:
+                load.wait()
+
+        gate[...] = dot_nn(full[j], wg[...])
+        up[...] = dot_nn(full[j], wu[...])
+
+        @pl.when(s > 0)
+        def _():
+            reduce_core(s - 1)
+
+        do_load(j).wait()
+        dhid[...] = dot_nn(do[j], wd[...])
+
+        def act(r):
+            g = gate[r, :]
+            u = up[r, :]
+            d = dhid[r, :]
+            sig = jax.nn.sigmoid(g)
+            silu = g * sig
+            at = pl.ds(pl.multiple_of(base + r.start, 64), 64)
+            hid[at, :] = (silu * u).astype(low)
+            dg[at, :] = (d * u * sig * (1.0 + g * (1.0 - sig))).astype(low)
+            du[at, :] = (d * silu).astype(low)
+
+        tiles(rows, 64, act)
+        slot = lax.rem(s, 2)
+        mine = pl.ds(pl.multiple_of(base, rows), rows)
+
+        def dhn(q, p):
+            w_rows = slice(p * width, (p + 1) * width)
+            part[slot, :, q * width : (q + 1) * width] = (
+                times_transposed(dg[mine, :], wg[w_rows, :])
+                + times_transposed(du[mine, :], wu[w_rows, :])
+            ).astype(low)
+
+        dhn(2, 1)
+        dhn(3, 3)
+        dhn(0, 0)
+        part_copy(s, slot).start()
+        dhn(1, 2)
+
+        @pl.when(s > 0)
+        def _():
+            reduce_far(s - 1)
+
+        @pl.when(s >= 2)
+        def _():
+            out_copy(s - 2).wait()
+
+        for p in range(4):
+            outp[slot, :, p * width : (p + 1) * width] = times_transposed(
+                hid[mine, :], wd[p * width : (p + 1) * width, :]
+            ).astype(low)
+        out_copy(s).start()
+        return unused
+
+    lax.fori_loop(0, 4, step, 0)
+
+    reduce_core(3)
+    count = model // width
+
+    def stage_copy(target, i, slot):
+        at = pl.ds(pl.multiple_of(i * width, width), width)
+        return pltpu.make_async_copy(stage.at[slot], target.at[at, :], s_sem.at[slot])
+
+    def weight_grad(target, right, left_of, first):
+        def tile(i, unused):
+            slot = lax.rem(i, 2)
+
+            @pl.when(jnp.logical_or(i >= 2, not first))
+            def _():
+                stage_copy(target, 0, slot).wait()
+
+            total = left_of(0, i, right)
+            for s in range(1, 4):
+                total = total + left_of(s, i, right)
+            stage[slot] = total.astype(low)
+            stage_copy(target, i, slot).start()
+            return unused
+
+        lax.fori_loop(0, count, tile, 0)
+
+    def from_full(s, i, right):
+        at = pl.ds(pl.multiple_of(i * width, width), width)
+        return contract_rows(full[chunk(s), :, at], right[s * rows : (s + 1) * rows, :])
+
+    def from_do(s, i, right):
+        at = pl.ds(pl.multiple_of(i * width, width), width)
+        return contract_rows(do[chunk(s), :, at], right[s * rows : (s + 1) * rows, :])
+
+    weight_grad(dwg_hbm, dg, from_full, True)
+    reduce_far(3)
+    weight_grad(dwu_hbm, du, from_full, False)
+    weight_grad(dwd_hbm, hid, from_do, False)
+    stage_copy(dwd_hbm, 0, 0).wait()
+    stage_copy(dwd_hbm, 0, 1).wait()
+    out_copy(2).wait()
+    out_copy(3).wait()
+    for s in range(1, 4):
+        rz_copy(s, chunk(s)).wait()
+
+    def final(r):
+        total = z_out[0, r, :].astype(wide)
+        for j in range(1, 4):
+            total = total + z_in[j, r, :].astype(wide)
+        dhn_ref[r, :] = total
+
+    tiles(rows, 64, final)
+
+    @pl.when(z < 3)
+    def _():
+        z_own(z + 1, 0).wait_send()
+
+    @pl.when(z > 0)
+    def _():
+        z_own(z - 1, 1).wait_send()
+
+
+def ffn_call(h_low, gain, grad_full, wg, wu, wd):
+    rows, width = h_low.shape
+    model, hidden = wg.shape
+    low, wide = jnp.bfloat16, jnp.float32
+    vmem = pl.BlockSpec(memory_space=pltpu.VMEM)
+    hbm = pl.BlockSpec(memory_space=pl.ANY)
+    dma = pltpu.SemaphoreType.DMA
+    tokens = 4 * rows
+    return pl.pallas_call(
+        ffn_kernel,
+        out_shape=(
+            jax.ShapeDtypeStruct((rows, width), wide),
+            jax.ShapeDtypeStruct((rows, 128), wide),
+            jax.ShapeDtypeStruct((4, rows, model), low),
+            jax.ShapeDtypeStruct((model, hidden), low),
+            jax.ShapeDtypeStruct((model, hidden), low),
+            jax.ShapeDtypeStruct((model, hidden), low),
+        ),
+        in_specs=[vmem, vmem, hbm, hbm, hbm, hbm],
+        out_specs=(vmem, vmem, hbm, hbm, hbm, hbm),
+        scratch_shapes=[
+            pltpu.VMEM((4, rows, model), low),
+            pltpu.VMEM((4, rows, model), low),
+            pltpu.VMEM((model, hidden), low),
+            pltpu.VMEM((model, hidden), low),
+            pltpu.VMEM((model, hidden), low),
+            pltpu.VMEM((tokens, hidden), low),
+            pltpu.VMEM((tokens, hidden), low),
+            pltpu.VMEM((tokens, hidden), low),
+            pltpu.VMEM((rows, hidden), wide),
+            pltpu.VMEM((rows, hidden), wide),
+            pltpu.VMEM((rows, hidden), wide),
+            pltpu.VMEM((2, rows, model), low),
+            pltpu.VMEM((2, rows, model), low),
+            pltpu.VMEM((4, rows, 2 * width), low),
+            pltpu.VMEM((4, rows, width), low),
+            pltpu.VMEM((4, rows, width), low),
+            pltpu.VMEM((4, rows, width), low),
+            pltpu.VMEM((4, rows, width), low),
+            pltpu.VMEM((2, width, hidden), low),
+            dma((7,)),
+            dma((2,)),
+            dma((4,)),
+            dma((4,)),
+            dma((4,)),
+            dma((4,)),
+            dma((2, 4)),
+            dma((2, 4)),
+            dma((4,)),
+            dma((4,)),
+            dma((4,)),
+            dma((4,)),
+            dma((4,)),
+            dma((4,)),
+            dma((2,)),
+            dma((2,)),
+        ],
+        compiler_params=pltpu.CompilerParams(
+            collective_id=2, has_side_effects=True, vmem_limit_bytes=66_000_000
+        ),
+        cost_estimate=pl.CostEstimate(
+            flops=18 * tokens * model * hidden,
+            bytes_accessed=40_000_000,
+            transcendentals=tokens * hidden,
+        ),
+    )(h_low, gain, grad_full, wg, wu, wd)
 
 
 def per_device(
@@ -350,29 +797,15 @@
     residual = tokens.astype(wide) + scatter_col(times_transposed(mixed_heads, out_weight))
 
     grad_out = (cotangent.astype(wide) * valid).astype(low)
-    residual_full = gather_tokens(residual.astype(low)).astype(wide)
-    grad_out_full = gather_tokens(grad_out)
-    factor_two, normed_two = norm_rows(residual_full, gain_two)
-    gate = jnp.dot(normed_two, gate_weight, preferred_element_type=wide)
-    upward = jnp.dot(normed_two, up_weight, preferred_element_type=wide)
-    sigmoid_gate = jax.nn.sigmoid(gate)
-    silu_gate = gate * sigmoid_gate
-    hidden = (silu_gate * upward).astype(low)
-    layer_out = (residual + scatter_tokens(times_transposed(hidden, down_weight))).astype(low)
-    grad_hidden = jnp.dot(grad_out_full, down_weight, preferred_element_type=wide)
-    grad_gate_act = (
-        grad_hidden * upward * sigmoid_gate * (1.0 + gate * (1.0 - sigmoid_gate))
-    ).astype(low)
-    grad_up_act = (grad_hidden * silu_gate).astype(low)
-    grad_down_part = contract_rows(grad_out_full, hidden)
-    grad_gate_part = contract_rows(normed_two, grad_gate_act)
-    grad_up_part = contract_rows(normed_two, grad_up_act)
-    grad_normed_two = scatter_tokens(
-        times_transposed(grad_gate_act, gate_weight) + times_transposed(grad_up_act, up_weight)
-    )
+    grad_out_full = gather_tokens(grad_out).reshape(4, row_count, model_width)
+    residual_low = residual.astype(low)
+    grad_normed_two, factor_two, out_part, grad_gate_part, grad_up_part, grad_down_part = ffn_call(
+        residual_low, gain_two[None], grad_out_full, gate_weight, up_weight, down_weight
+    )
+    layer_out = (residual + scatter_tokens(out_part.reshape(-1, model_width))).astype(low)
     own_gain_two = gain_two[:col_width]
-    own_factor_two = factor_two[:row_count]
-    own_residual = residual_full[:row_count, :col_width]
+    own_factor_two = factor_two[:, :1]
+    own_residual = residual_low.astype(wide)
     scaled = own_gain_two * grad_normed_two
     inner = col_sum(jnp.sum(scaled * own_residual, axis=1)[:, None]) / model_width
     grad_residual = (

time: 1070 us -> 904 us (0.84)
  Pallas kernels: 0 us -> 149 us
  other arithmetic: 197 us -> 110 us
  waiting for transfers between devices: 430 us -> 343 us
  matrix products: 122 us -> 37.9 us
  starting transfers between devices: 129 us -> 102 us
  blocking collectives: 99.2 us -> 75 us
    pallas_call x0 -> x1, Pallas kernels: none -> 149 us  [ffn_call(): pl.pallas_call(ffn_kernel, out_shape=(jax.ShapeDtypeStruct((rows, width),...]
    ppermute x74 -> x64, waiting for transfers between devices: 430 us -> 343 us  [swap(): return lax.ppermute(value, axis, [(i, i ^ bit) for i in range(size)])]
    dot_general x5 -> x2, matrix products: 43.8 us -> 3.75 us  [times_transposed(): lax.dot_general(left, right, (((1,), (1,)), ((), ())), preferred_element_...]
    convert_element_type x3 -> x2, other arithmetic: 39.5 us -> 1.74 us  [the longest x1 1.12 us: per_device(): residual_low = residual.astype(low)]
    ppermute x74 -> x64, starting transfers between devices: 129 us -> 102 us  [swap(): return lax.ppermute(value, axis, [(i, i ^ bit) for i in range(size)])]
    psum x1, blocking collectives: 63.5 us -> 38.8 us  [per_device(): gain_grads = lax.psum(gain_grads, ('dp', 'row', 'col'))]
    dot_general x3 -> x0, matrix products: 22.5 us -> none  [the longest x1 10.3 us: per_device(): jnp.dot(grad_out_full, down_weight, preferred_element_type=wide)]
    dot_general x5 -> x2, matrix products: 24.6 us -> 5.04 us  [contract_rows(): lax.dot_general(left, right, (((0,), (0,)), ((), ())), preferred_element_...]
  transfers between devices with their start and end apart: 74 -> 64, of which waited for: 30 -> 30; matrix products, arithmetic and copies ran while one was open for 23% -> 19% of each run, Pallas kernels for 0% -> 0%
where the time goes in v2:
time: 904 us; the launch traced here: 889 us
  waiting for transfers between devices  343 us (38%)
  Pallas kernels  149 us (16%)
  other arithmetic  110 us (12%)
  starting transfers between devices  102 us (11%)
  blocking collectives  75 us (8%)
  local copies, waits for them, and re-layouts  63.5 us (7%)
  matrix products  37.9 us (4%)
    ppermute x64, waiting for transfers between devices, swap(): return lax.ppermute(value, axis, [(i, i ^ bit) for i in range(size)])  343 us
    pallas_call x1, Pallas kernels, ffn_call(): pl.pallas_call(ffn_kernel, out_shape=(jax.ShapeDtypeStruct((rows, width),...  149 us
    ppermute x64, starting transfers between devices, swap(): return lax.ppermute(value, axis, [(i, i ^ bit) for i in range(size)])  102 us
    psum x1, blocking collectives, per_device(): gain_grads = lax.psum(gain_grads, ('dp', 'row', 'col'))  38.8 us
    all_gather x1, blocking collectives, per_device(): lax.all_gather(jnp.stack([gain_attn, gain_ffn]), ('dp', 'row'), axis=1, t...  36.2 us
    concatenate x1, other arithmetic, gather_col(): jnp.concatenate([value, near[:, :width], far, near[:, width:]], axis=1)  20.2 us
    unnamed x204, local copies, waits for them, and re-layouts  19.8 us
  transfers between devices with their start and end apart: 64, of which 30 were waited for; matrix products, arithmetic and copies ran while one was open for 19% of the time, Pallas kernels for 0%

profile of v2, /device:TPU:0, one launch (start us, length us, event | category | flops | bytes accessed | tf_op | source)
XLA Modules:
  0.0 888.5 jit_solution(5335965068778806738)
XLA Ops:
  1.9 5.1 collective-permute-start.7
  13.5 36.2 %all_gather.3 = bf16[2,2048]{1,0:T(2,128)(2,1)S(1)} all-gather(bf16[2,256]{1,0:T(2,128)(2,1)S(1)} %pad_maximum_fusion.23), channel_id=1, replica_groups=mesh['dp'=4,'row'=2,'col'=4] {'dp','row'}, dimensions={1}, use_global_device_ids=true | all-gather | bytes 9216 | tf_op jit(solution)/shard_map/all_gather | solution.py:752
  54.2 11.8 %collective-permute-start.9 = (bf16[256,512]{1,0:T(8,128)(2,1)S(1)}, bf16[256,512]{1,0:T(8,128)(2,1)}, u32[]{:S(2)}, u32[]{:S(2)}) collective-permute-start(bf16[256,512]{1,0:T(8,128)(2,1)S(1)} %bitcast.696), channel_id=1, source_target_pairs={{0,8},{8,0},{16,24},{24,16},{1,9},{9,1},{17,25},{25,17},{2,10},{10... | collective-permute-start | bytes 786440 | tf_op jit(solution)/shard_map/ppermute | solution.py:165
  66.0 2.4 collective-permute-start.2
  75.1 2.4 collective-permute-start.26
  77.6 4.5 collective-permute-done.9
  82.1 2.9 select_bitcast_fusion.11
  85.2 28.0 %collective-permute-done.26 = bf16[256,512]{1,0:T(8,128)(2,1)S(1)} collective-permute-done((bf16[256,512]{1,0:T(8,128)(2,1)}, bf16[256,512]{1,0:T(8,128)(2,1)S(1)}, u32[]{:S(2)}, u32[]{:S(2)}) %collective-permute-start.26) | collective-permute-done | bytes 262176 | tf_op jit(solution)/shard_map/ppermute | solution.py:165
  113.2 17.4 %collective-permute-start.28 = (bf16[256,512]{1,0:T(8,128)(2,1)}, bf16[256,512]{1,0:T(8,128)(2,1)S(1)}, u32[]{:S(2)}, u32[]{:S(2)}) collective-permute-start(bf16[256,512]{1,0:T(8,128)(2,1)} %bitcast.48), channel_id=1, source_target_pairs={{0,8},{8,0},{16,24},{24,16},{1,9},{9,1},{17,25},{25,17},{2,10},{10... | collective-permute-start | bytes 786440 | tf_op jit(solution)/shard_map/ppermute | solution.py:165
  130.6 4.5 collective-permute-start.22
  138.7 7.4 collective-permute-done.28
  150.5 9.5 %collective-permute-done.23 = bf16[256,512]{1,0:T(8,128)(2,1)S(1)} collective-permute-done((bf16[256,512]{1,0:T(8,128)(2,1)S(1)}, bf16[256,512]{1,0:T(8,128)(2,1)S(1)}, u32[]{:S(2)}, u32[]{:S(2)}) %collective-permute-start.23) | collective-permute-done | bytes 262176 | tf_op jit(solution)/shard_map/ppermute | solution.py:165
  160.0 3.4 collective-permute-start.14
  163.5 9.4 %collective-permute-done.24 = bf16[256,512]{1,0:T(8,128)(2,1)S(1)} collective-permute-done((bf16[256,512]{1,0:T(8,128)(2,1)S(1)}, bf16[256,512]{1,0:T(8,128)(2,1)S(1)}, u32[]{:S(2)}, u32[]{:S(2)}) %collective-permute-start.24) | collective-permute-done | bytes 262176 | tf_op jit(solution)/shard_map/ppermute | solution.py:165
  177.2 13.3 %collective-permute-done.14 = bf16[512,512]{1,0:T(8,128)(2,1)S(1)} collective-permute-done((bf16[512,512]{1,0:T(8,128)(2,1)S(1)}, bf16[512,512]{1,0:T(8,128)(2,1)S(1)}, u32[]{:S(2)}, u32[]{:S(2)}) %collective-permute-start.14) | collective-permute-done | bytes 524320 | tf_op jit(solution)/shard_map/ppermute | solution.py:165
  194.0 2.2 collective-permute-start.16
  198.8 20.2 %collective-permute-done.5 = bf16[4,1,256,1024]{3,2,1,0:T(8,128)(2,1)S(1)} collective-permute-done((bf16[4,1,256,1024]{3,2,1,0:T(8,128)(2,1)S(1)}, bf16[4,1,256,1024]{3,2,1,0:T(8,128)(2,1)S(1)}, u32[]{:S(2)}, u32[]{:S(2)}) %collective-permute-start.5) | collective-permute-done | bytes 2097184 | tf_op jit(solution)/shard_map/ppermute | solution.py:165
  220.2 2.4 fusion.95
  234.2 14.8 %pad_maximum_fusion.2 = bf16[2048,1024]{1,0:T(8,128)(2,1)} fusion(bf16[2048,512]{1,0:T(8,128)(2,1)} %collective-permute-done.16, bf16[512,512]{1,0:T(8,128)(2,1)S(1)} %collective-permute-done.15, bf16[512,512]{1,0:T(8,128)(2,1)S(1)} %collective-permute-done.14, bf16[512,512]{1,0:T(8,128)(2,1)S(1)} %collective-permute-done.13, ...), kind=kLoop, calls=%fused_computation.76 | loop fusion | flops 20971520 | bytes 8388608 | tf_op jit(solution)/shard_map/concatenate | solution.py:171
  249.0 12.3 %collective-permute-done.6 = bf16[512,512]{1,0:T(8,128)(2,1)} collective-permute-done((bf16[512,512]{1,0:T(8,128)(2,1)}, bf16[512,512]{1,0:T(8,128)(2,1)}, u32[]{:S(2)}, u32[]{:S(2)}) %collective-permute-start.6) | collective-permute-done | bytes 524320 | tf_op jit(solution)/shard_map/ppermute | solution.py:165
  263.5 7.1 while.39
  270.7 9.6 %while.40 = (s32[]{:T(128)}, f32[1,2,512,256]{3,2,1,0:T(8,128)}, s32[2]{0:T(128)S(1)}, bf16[2,512,1,256]{3,1,2,0:T(8,128)(2,1)}, bf16[1,2,512,256]{3,2,1,0:T(8,1...) while((s32[]{:T(128)}, f32[1,2,512,256]{3,2,1,0:T(8,128)}, ...), condition=%wide.region_6.7_spmd.clone, body=%wide.region_5.6_spmd.clone.sunk | while | flops 539755520 | bytes 3683479 | solution.py:115
  272.2 2.9 fusion.183
  276.6 3.3 fusion.183
  280.4 2.7 copy.56
  298.0 13.9 %collective-permute-done.21 = bf16[4,1,256,512]{3,2,0,1:T(8,128)(2,1)S(1)} collective-permute-done((bf16[4,1,256,512]{3,2,0,1:T(8,128)(2,1)S(1)}, bf16[4,1,256,512]{3,2,0,1:T(8,128)(2,1)S(1)}, u32[]{:S(2)}, u32[]{:S(2)}) %collective-permute-start.21) | collective-permute-done | bytes 1048608 | tf_op jit(solution)/shard_map/ppermute | solution.py:165
  315.0 2.6 fusion.139
  317.8 20.2 %pad_maximum_fusion = bf16[2048,2048]{1,0:T(8,128)(2,1)} fusion(bf16[2048,512]{1,0:T(8,128)(2,1)S(1)} %get-tuple-element.428, bf16[2048,512]{1,0:T(8,128)(2,1)} %collective-permute-done.16, bf16[2048,512]{1,0:T(8,128)(2,1)S(1)} %get-tuple-element.427, bf16[512,512]{1,0:T(8,128)(2,1)S(1)} %copy-done.29, bf16[512,512]{1,0:T(8,128)(2,1)S(1)} %copy-done.27, ...), kind=kLoop, calls=%fused_computation.69 | loop fusion | flops 58720256 | bytes 16777216 | tf_op jit(solution)/shard_map/concatenate | solution.py:172
  337.9 148.8 %shard_map.203 = (f32[512,512]{1,0:T(8,128)}, f32[512,128]{1,0:T(8,128)}, bf16[4,512,2048]{2,1,0:T(8,128)(2,1)}, bf16[2048,512]{1,0:T(8,128)(2,1)}, bf16[2048,51...) custom-call(bf16[512,512]{1,0:T(8,128)(2,1)} %fusion.136.h_ref, f32[1,2048]{1,0:T(1,128)} %get-tuple-element.519.gain_ref, ...), custom_call_target="tpu_custom_call" | custom-call | flops 38654705664 | bytes 40000000 | tf_op jit(solution)/shard_map/pallas_call | solution.py:664
  498.3 2.5 pad_maximum_fusion.3
  500.8 9.6 %collective-permute-done.37 = bf16[512,512]{1,0:T(8,128)(2,1)S(1)} collective-permute-done((bf16[512,512]{1,0:T(8,128)(2,1)S(1)}, bf16[512,512]{1,0:T(8,128)(2,1)S(1)}, u32[]{:S(2)}, u32[]{:S(2)}) %collective-permute-start.37) | collective-permute-done | bytes 524320 | tf_op jit(solution)/shard_map/ppermute | solution.py:165
  511.5 2.8 collective-permute-done.60
  516.7 20.1 %collective-permute-done.56 = bf16[4,256,512]{2,1,0:T(8,128)(2,1)S(1)} collective-permute-done((bf16[4,256,512]{2,1,0:T(8,128)(2,1)S(1)}, bf16[4,256,512]{2,1,0:T(8,128)(2,1)S(1)}, u32[]{:S(2)}, u32[]{:S(2)}) %collective-permute-start.56) | collective-permute-done | bytes 1048608 | tf_op jit(solution)/shard_map/ppermute | solution.py:165
  537.1 21.2 %collective-permute-done.52 = bf16[4,256,512]{2,1,0:T(8,128)(2,1)S(1)} collective-permute-done((bf16[4,256,512]{2,1,0:T(8,128)(2,1)S(1)}, bf16[4,256,512]{2,1,0:T(8,128)(2,1)S(1)}, u32[]{:S(2)}, u32[]{:S(2)}) %collective-permute-start.52) | collective-permute-done | bytes 1048608 | tf_op jit(solution)/shard_map/ppermute | solution.py:165
  564.1 2.9 collective-permute-done.63
  569.1 2.9 copy.81
  574.9 18.4 %collective-permute-done.58 = bf16[256,512]{1,0:T(8,128)(2,1)} collective-permute-done((bf16[256,512]{1,0:T(8,128)(2,1)}, bf16[256,512]{1,0:T(8,128)(2,1)}, u32[]{:S(2)}, u32[]{:S(2)}) %collective-permute-start.58) | collective-permute-done | bytes 262176 | tf_op jit(solution)/shard_map/ppermute | solution.py:165
  593.4 2.5 collective-permute-start.55
  595.9 12.8 %collective-permute-done.54 = bf16[256,512]{1,0:T(8,128)(2,1)S(1)} collective-permute-done((bf16[256,512]{1,0:T(8,128)(2,1)}, bf16[256,512]{1,0:T(8,128)(2,1)S(1)}, u32[]{:S(2)}, u32[]{:S(2)}) %collective-permute-start.54) | collective-permute-done | bytes 262176 | tf_op jit(solution)/shard_map/ppermute | solution.py:165
  620.0 20.8 %while.41 = (s32[]{:T(128)}, f32[1,2,512,256]{3,2,1,0:T(8,128)}, f32[2,512,1,256]{3,1,2,0:T(8,128)}, f32[2,512,1,256]{3,1,2,0:T(8,128)}, s32[2]{0:T(128)S(1)}, /...) while((s32[]{:T(128)}, f32[1,2,512,256]{3,2,1,0:T(8,128)}, ...), condition=%wide.region_10.11_spmd.clone, body=%wide.region_9.10_spmd.clone.sunk | while | flops 1347159040 | bytes 34883456 | solution.py:151
  623.9 2.6 fusion.196
  634.1 2.9 fusion.196
  640.7 3.1 fusion.108
  643.8 3.2 copy.85
  657.8 6.3 collective-permute-done.39
  667.3 3.7 fusion.93
  671.0 3.3 copy-done.23
  677.2 2.4 fusion.148
  680.0 6.6 collective-permute-done.48
  688.4 2.4 collective-permute-start.50
  692.8 4.1 add_convert_fusion
  701.0 6.0 collective-permute-done.50
  708.4 42.4 %collective-permute-done.41 = bf16[512,512]{1,0:T(8,128)(2,1)S(1)} collective-permute-done((bf16[512,512]{1,0:T(8,128)(2,1)S(1)}, bf16[512,512]{1,0:T(8,128)(2,1)S(1)}, u32[]{:S(2)}, u32[]{:S(2)}) %collective-permute-start.41) | collective-permute-done | bytes 524320 | tf_op jit(solution)/shard_map/ppermute | solution.py:165
  752.7 38.8 %psum.7 = f32[2,2048]{1,0:T(2,128)S(1)} all-reduce(f32[2,2048]{1,0:T(2,128)S(1)} %constant_dynamic-update-slice_fusion.3), channel_id=1, replica_groups=mesh['dp'=4,'row'=2,'col'=4] {'dp','row','col'}, use_global_device_ids=true, to_apply=%region_14.15 | all-reduce | flops 4096 | bytes 32768 | tf_op jit(solution)/shard_map/psum | solution.py:880
  791.5 2.3 collective-permute-start.43
  795.3 3.5 bitcast_add_fusion.1
  799.1 2.2 collective-permute-start.45
  803.8 3.9 fusion.137
  810.7 13.9 %collective-permute-done.45 = bf16[256,1024]{1,0:T(8,128)(2,1)S(1)} collective-permute-done((bf16[256,1024]{1,0:T(8,128)(2,1)S(1)}, bf16[256,1024]{1,0:T(8,128)(2,1)S(1)}, u32[]{:S(2)}, u32[]{:S(2)}) %collective-permute-start.45) | collective-permute-done | bytes 524320 | tf_op jit(solution)/shard_map/ppermute | solution.py:165
  824.6 2.3 collective-permute-start.34
  826.9 12.7 %collective-permute-done.46 = bf16[256,1024]{1,0:T(8,128)(2,1)S(1)} collective-permute-done((bf16[256,1024]{1,0:T(8,128)(2,1)S(1)}, bf16[256,1024]{1,0:T(8,128)(2,1)S(1)}, u32[]{:S(2)}, u32[]{:S(2)}) %collective-permute-start.46) | collective-permute-done | bytes 524320 | tf_op jit(solution)/shard_map/ppermute | solution.py:165
  841.9 5.6 collective-permute-done.32
  847.4 37.0 %collective-permute-done.33 = bf16[512,512]{1,0:T(8,128)(2,1)S(1)} collective-permute-done((bf16[512,512]{1,0:T(8,128)(2,1)S(1)}, bf16[512,512]{1,0:T(8,128)(2,1)S(1)}, u32[]{:S(2)}, u32[]{:S(2)}) %collective-permute-start.33) | collective-permute-done | bytes 524320 | tf_op jit(solution)/shard_map/ppermute | solution.py:165
  884.5 3.5 fusion.75
  (486 shorter events, 165.2 us)
Async XLA Ops:
  1.9 66.6 %collective-permute-start.7 = (bf16[256,512]{1,0:T(8,128)(2,1)S(1)}, bf16[256,512]{1,0:T(8,128)(2,1)}, u32[]{:S(2)}, u32[]{:S(2)}) collective-permute-start(bf16[256,512]{1,0:T(8,128)(2,1)S(1)} %bitcast.694), channel_id=1, source_target_pairs={{0,24},{8,16},{16,8},{24,0},{1,25},{9,17},{17,9},{25,1},{2,26},{10... | collective-permute-start | bytes 786440 | tf_op jit(solution)/shard_map/ppermute | solution.py:165
  7.0 68.1 %collective-permute-start.8 = (bf16[256,512]{1,0:T(8,128)(2,1)S(1)}, bf16[256,512]{1,0:T(8,128)(2,1)}, u32[]{:S(2)}, u32[]{:S(2)}) collective-permute-start(bf16[256,512]{1,0:T(8,128)(2,1)S(1)} %bitcast.695), channel_id=1, source_target_pairs={{0,16},{8,24},{16,0},{24,8},{1,17},{9,25},{17,1},{25,9},{2,18},{10... | collective-permute-start | bytes 786440 | tf_op jit(solution)/shard_map/ppermute | solution.py:165
  9.1 45.1 %collective-permute-start.18 = (bf16[256,512]{1,0:T(8,128)(2,1)S(1)}, bf16[256,512]{1,0:T(8,128)(2,1)}, u32[]{:S(2)}, u32[]{:S(2)}) collective-permute-start(bf16[256,512]{1,0:T(8,128)(2,1)S(1)} %get-tuple-element.498), channel_id=1, source_target_pairs={{0,24},{8,16},{16,8},{24,0},{1,25},{9,17},{17,9},{25,1},{2,26},{10... | collective-permute-start | bytes 786440 | tf_op jit(solution)/shard_map/ppermute | solution.py:165
  11.0 55.1 %collective-permute-start.19 = (bf16[256,512]{1,0:T(8,128)(2,1)}, bf16[256,512]{1,0:T(8,128)(2,1)}, u32[]{:S(2)}, u32[]{:S(2)}) collective-permute-start(bf16[256,512]{1,0:T(8,128)(2,1)} %get-tuple-element.499), channel_id=1, source_target_pairs={{0,16},{8,24},{16,0},{24,8},{1,17},{9,25},{17,1},{25,9},{2,18},{10... | collective-permute-start | bytes 786440 | tf_op jit(solution)/shard_map/ppermute | solution.py:165
  12.0 56.5 %collective-permute-start.20 = (bf16[256,512]{1,0:T(8,128)(2,1)}, bf16[256,512]{1,0:T(8,128)(2,1)}, u32[]{:S(2)}, u32[]{:S(2)}) collective-permute-start(bf16[256,512]{1,0:T(8,128)(2,1)} %get-tuple-element.500), channel_id=1, source_target_pairs={{0,8},{8,0},{16,24},{24,16},{1,9},{9,1},{17,25},{25,17},{2,10},{10... | collective-permute-start | bytes 786440 | tf_op jit(solution)/shard_map/ppermute | solution.py:165
  54.2 27.9 %collective-permute-start.9 = (bf16[256,512]{1,0:T(8,128)(2,1)S(1)}, bf16[256,512]{1,0:T(8,128)(2,1)}, u32[]{:S(2)}, u32[]{:S(2)}) collective-permute-start(bf16[256,512]{1,0:T(8,128)(2,1)S(1)} %bitcast.696), channel_id=1, source_target_pairs={{0,8},{8,0},{16,24},{24,16},{1,9},{9,1},{17,25},{25,17},{2,10},{10... | collective-permute-start | bytes 786440 | tf_op jit(solution)/shard_map/ppermute | solution.py:165
  66.0 64.5 %collective-permute-start.2 = (bf16[256,1024]{1,0:T(8,128)(2,1)S(1)}, bf16[256,1024]{1,0:T(8,128)(2,1)S(1)}, u32[]{:S(2)}, u32[]{:S(2)}) collective-permute-start(bf16[256,1024]{1,0:T(8,128)(2,1)S(1)} %constant_dynamic-update-slice_fusion), channel_id=1, source_target_pairs={{0,24},{8,16},{16,8},{24,0},{1,25},{9,17},{17,9},{25,1},{2,26},{10... | collective-permute-start | bytes 1572872 | tf_op jit(solution)/shard_map/ppermute | solution.py:165
  68.5 66.6 %collective-permute-start.3 = (bf16[256,1024]{1,0:T(8,128)(2,1)S(1)}, bf16[256,1024]{1,0:T(8,128)(2,1)}, u32[]{:S(2)}, u32[]{:S(2)}) collective-permute-start(bf16[256,1024]{1,0:T(8,128)(2,1)S(1)} %constant_dynamic-update-slice_fusion), channel_id=1, source_target_pairs={{0,16},{8,24},{16,0},{24,8},{1,17},{9,25},{17,1},{25,9},{2,18},{10... | collective-permute-start | bytes 1572872 | tf_op jit(solution)/shard_map/ppermute | solution.py:165
  68.5 68.1 %collective-permute-start.4 = (bf16[256,1024]{1,0:T(8,128)(2,1)S(1)}, bf16[256,1024]{1,0:T(8,128)(2,1)}, u32[]{:S(2)}, u32[]{:S(2)}) collective-permute-start(bf16[256,1024]{1,0:T(8,128)(2,1)S(1)} %constant_dynamic-update-slice_fusion), channel_id=1, source_target_pairs={{0,8},{8,0},{16,24},{24,16},{1,9},{9,1},{17,25},{25,17},{2,10},{10... | collective-permute-start | bytes 1572872 | tf_op jit(solution)/shard_map/ppermute | solution.py:165
  75.1 38.1 %collective-permute-start.26 = (bf16[256,512]{1,0:T(8,128)(2,1)}, bf16[256,512]{1,0:T(8,128)(2,1)S(1)}, u32[]{:S(2)}, u32[]{:S(2)}) collective-permute-start(bf16[256,512]{1,0:T(8,128)(2,1)} %bitcast.699), channel_id=1, source_target_pairs={{0,24},{8,16},{16,8},{24,0},{1,25},{9,17},{17,9},{25,1},{2,26},{10... | collective-permute-start | bytes 786440 | tf_op jit(solution)/shard_map/ppermute | solution.py:165
  82.1 56.4 %collective-permute-start.27 = (bf16[256,512]{1,0:T(8,128)(2,1)}, bf16[256,512]{1,0:T(8,128)(2,1)S(1)}, u32[]{:S(2)}, u32[]{:S(2)}) collective-permute-start(bf16[256,512]{1,0:T(8,128)(2,1)} %bitcast.47), channel_id=1, source_target_pairs={{0,16},{8,24},{16,0},{24,8},{1,17},{9,25},{17,1},{25,9},{2,18},{10... | collective-permute-start | bytes 786440 | tf_op jit(solution)/shard_map/ppermute | solution.py:165
  113.2 33.0 %collective-permute-start.28 = (bf16[256,512]{1,0:T(8,128)(2,1)}, bf16[256,512]{1,0:T(8,128)(2,1)S(1)}, u32[]{:S(2)}, u32[]{:S(2)}) collective-permute-start(bf16[256,512]{1,0:T(8,128)(2,1)} %bitcast.48), channel_id=1, source_target_pairs={{0,8},{8,0},{16,24},{24,16},{1,9},{9,1},{17,25},{25,17},{2,10},{10... | collective-permute-start | bytes 786440 | tf_op jit(solution)/shard_map/ppermute | solution.py:165
  130.6 17.4 %collective-permute-start.22 = (bf16[256,512]{1,0:T(8,128)(2,1)S(1)}, bf16[256,512]{1,0:T(8,128)(2,1)S(1)}, u32[]{:S(2)}, u32[]{:S(2)}) collective-permute-start(bf16[256,512]{1,0:T(8,128)(2,1)S(1)} %copy-done.90), channel_id=1, source_target_pairs={{0,24},{8,16},{16,8},{24,0},{1,25},{9,17},{17,9},{25,1},{2,26},{10... | collective-permute-start | bytes 786440 | tf_op jit(solution)/shard_map/ppermute | solution.py:165
  135.1 14.7 %collective-permute-start = (bf16[512,512]{1,0:T(8,128)(2,1)S(1)}, bf16[512,512]{1,0:T(8,128)(2,1)S(1)}, u32[]{:S(2)}, u32[]{:S(2)}) collective-permute-start(bf16[512,512]{1,0:T(8,128)(2,1)S(1)} %copy-done.6), channel_id=1, source_target_pairs={{0,2},{1,3},{2,0},{3,1},{4,6},{5,7},{6,4},{7,5},{8,10},{9,11},{10,... | collective-permute-start | bytes 1572872 | tf_op jit(solution)/shard_map/ppermute | solution.py:165
  136.6 36.3 %collective-permute-start.13 = (bf16[512,512]{1,0:T(8,128)(2,1)S(1)}, bf16[512,512]{1,0:T(8,128)(2,1)S(1)}, u32[]{:S(2)}, u32[]{:S(2)}) collective-permute-start(bf16[512,512]{1,0:T(8,128)(2,1)S(1)} %multiply_convert_fusion), channel_id=1, source_target_pairs={{0,8},{8,0},{16,24},{24,16},{1,9},{9,1},{17,25},{25,17},{2,10},{10... | collective-permute-start | bytes 1572872 | tf_op jit(solution)/shard_map/ppermute | solution.py:165
  138.4 21.6 %collective-permute-start.23 = (bf16[256,512]{1,0:T(8,128)(2,1)S(1)}, bf16[256,512]{1,0:T(8,128)(2,1)S(1)}, u32[]{:S(2)}, u32[]{:S(2)}) collective-permute-start(bf16[256,512]{1,0:T(8,128)(2,1)S(1)} %copy-done.89), channel_id=1, source_target_pairs={{0,16},{8,24},{16,0},{24,8},{1,17},{9,25},{17,1},{25,9},{2,18},{10... | collective-permute-start | bytes 786440 | tf_op jit(solution)/shard_map/ppermute | solution.py:165
  146.2 26.7 %collective-permute-start.24 = (bf16[256,512]{1,0:T(8,128)(2,1)S(1)}, bf16[256,512]{1,0:T(8,128)(2,1)S(1)}, u32[]{:S(2)}, u32[]{:S(2)}) collective-permute-start(bf16[256,512]{1,0:T(8,128)(2,1)S(1)} %get-tuple-element.497), channel_id=1, source_target_pairs={{0,8},{8,0},{16,24},{24,16},{1,9},{9,1},{17,25},{25,17},{2,10},{10... | collective-permute-start | bytes 786440 | tf_op jit(solution)/shard_map/ppermute | solution.py:165
  148.0 46.0 %collective-permute-start.10 = (bf16[4,1,256,512]{3,2,0,1:T(8,128)(2,1)S(1)}, bf16[4,1,256,512]{3,2,0,1:T(8,128)(2,1)S(1)}, u32[]{:S(2)}, u32[]{:S(2)}) collective-permute-start(bf16[4,1,256,512]{3,2,0,1:T(8,128)(2,1)S(1)} %maximum_bitcast_fusion.1), channel_id=1, source_target_pairs={{0,4},{4,0},{1,5},{5,1},{2,6},{6,2},{3,7},{7,3},{8,12},{12,8},{9,1... | collective-permute-start | bytes 3145736 | tf_op jit(solution)/shard_map/ppermute | solution.py:165
  149.7 69.2 %collective-permute-start.5 = (bf16[4,1,256,1024]{3,2,1,0:T(8,128)(2,1)S(1)}, bf16[4,1,256,1024]{3,2,1,0:T(8,128)(2,1)S(1)}, u32[]{:S(2)}, u32[]{:S(2)}) collective-permute-start(bf16[4,1,256,1024]{3,2,1,0:T(8,128)(2,1)S(1)} %maximum_bitcast_fusion), channel_id=1, source_target_pairs={{0,4},{4,0},{1,5},{5,1},{2,6},{6,2},{3,7},{7,3},{8,12},{12,8},{9,1... | collective-permute-start | bytes 6291464 | tf_op jit(solution)/shard_map/ppermute | solution.py:165
  160.0 30.5 %collective-permute-start.14 = (bf16[512,512]{1,0:T(8,128)(2,1)S(1)}, bf16[512,512]{1,0:T(8,128)(2,1)S(1)}, u32[]{:S(2)}, u32[]{:S(2)}) collective-permute-start(bf16[512,512]{1,0:T(8,128)(2,1)S(1)} %multiply_convert_fusion), channel_id=1, source_target_pairs={{0,16},{8,24},{16,0},{24,8},{1,17},{9,25},{17,1},{25,9},{2,18},{10... | collective-permute-start | bytes 1572872 | tf_op jit(solution)/shard_map/ppermute | solution.py:165
  172.9 19.2 %collective-permute-start.15 = (bf16[512,512]{1,0:T(8,128)(2,1)S(1)}, bf16[512,512]{1,0:T(8,128)(2,1)S(1)}, u32[]{:S(2)}, u32[]{:S(2)}) collective-permute-start(bf16[512,512]{1,0:T(8,128)(2,1)S(1)} %multiply_convert_fusion), channel_id=1, source_target_pairs={{0,24},{8,16},{16,8},{24,0},{1,25},{9,17},{17,9},{25,1},{2,26},{10... | collective-permute-start | bytes 1572872 | tf_op jit(solution)/shard_map/ppermute | solution.py:165
  172.9 25.3 %collective-permute-start.1 = (bf16[512,1024]{1,0:T(8,128)(2,1)S(1)}, bf16[512,1024]{1,0:T(8,128)(2,1)S(1)}, u32[]{:S(2)}, u32[]{:S(2)}) collective-permute-start(bf16[512,1024]{1,0:T(8,128)(2,1)S(1)} %pad_maximum_fusion.11), channel_id=1, source_target_pairs={{0,1},{1,0},{2,3},{3,2},{4,5},{5,4},{6,7},{7,6},{8,9},{9,8},{10,11... | collective-permute-start | bytes 3145736 | tf_op jit(solution)/shard_map/ppermute | solution.py:165
  190.5 98.5 %collective-permute-start.29 = (bf16[4,1,256,512]{3,2,0,1:T(8,128)(2,1)}, bf16[4,1,256,512]{3,2,0,1:T(8,128)(2,1)}, u32[]{:S(2)}, u32[]{:S(2)}) collective-permute-start(bf16[4,1,256,512]{3,2,0,1:T(8,128)(2,1)} %maximum_bitcast_fusion.4), channel_id=1, source_target_pairs={{0,4},{4,0},{1,5},{5,1},{2,6},{6,2},{3,7},{7,3},{8,12},{12,8},{9,1... | collective-permute-start | bytes 3145736 | tf_op jit(solution)/shard_map/ppermute | solution.py:165
  192.0 98.8 %collective-permute-start.25 = (bf16[4,1,256,512]{3,2,0,1:T(8,128)(2,1)}, bf16[4,1,256,512]{3,2,0,1:T(8,128)(2,1)}, u32[]{:S(2)}, u32[]{:S(2)}) collective-permute-start(bf16[4,1,256,512]{3,2,0,1:T(8,128)(2,1)} %maximum_bitcast_fusion.3), channel_id=1, source_target_pairs={{0,4},{4,0},{1,5},{5,1},{2,6},{6,2},{3,7},{7,3},{8,12},{12,8},{9,1... | collective-permute-start | bytes 3145736 | tf_op jit(solution)/shard_map/ppermute | solution.py:165
  194.0 40.1 %collective-permute-start.16 = (bf16[2048,512]{1,0:T(8,128)(2,1)}, bf16[2048,512]{1,0:T(8,128)(2,1)}, u32[]{:S(2)}, u32[]{:S(2)}) collective-permute-start(bf16[2048,512]{1,0:T(8,128)(2,1)} %pad_maximum_fusion.6), channel_id=1, source_target_pairs={{0,2},{1,3},{2,0},{3,1},{4,6},{5,7},{6,4},{7,5},{8,10},{9,11},{10,... | collective-permute-start | bytes 6291464 | tf_op jit(solution)/shard_map/ppermute | solution.py:165
  230.4 30.9 %collective-permute-start.6 = (bf16[512,512]{1,0:T(8,128)(2,1)}, bf16[512,512]{1,0:T(8,128)(2,1)}, u32[]{:S(2)}, u32[]{:S(2)}) collective-permute-start(bf16[512,512]{1,0:T(8,128)(2,1)} %pad_maximum_fusion.17), channel_id=1, source_target_pairs={{0,4},{4,0},{1,5},{5,1},{2,6},{6,2},{3,7},{7,3},{8,12},{12,8},{9,1... | collective-permute-start | bytes 1572872 | tf_op jit(solution)/shard_map/ppermute | solution.py:165
  249.0 66.1 %collective-permute-start.17 = (bf16[2048,1024]{1,0:T(8,128)(2,1)}, bf16[2048,1024]{1,0:T(8,128)(2,1)}, u32[]{:S(2)}, u32[]{:S(2)}) collective-permute-start(bf16[2048,1024]{1,0:T(8,128)(2,1)} %pad_maximum_fusion.2), channel_id=1, source_target_pairs={{0,1},{1,0},{2,3},{3,2},{4,5},{5,4},{6,7},{7,6},{8,9},{9,8},{10,11... | collective-permute-start | bytes 12582920 | tf_op jit(solution)/shard_map/ppermute | solution.py:165
  286.1 7.1 collective-permute-start.11
  287.9 24.1 %collective-permute-start.21 = (bf16[4,1,256,512]{3,2,0,1:T(8,128)(2,1)S(1)}, bf16[4,1,256,512]{3,2,0,1:T(8,128)(2,1)S(1)}, u32[]{:S(2)}, u32[]{:S(2)}) collective-permute-start(bf16[4,1,256,512]{3,2,0,1:T(8,128)(2,1)S(1)} %maximum_bitcast_fusion.2), channel_id=1, source_target_pairs={{0,4},{4,0},{1,5},{5,1},{2,6},{6,2},{3,7},{7,3},{8,12},{12,8},{9,1... | collective-permute-start | bytes 3145736 | tf_op jit(solution)/shard_map/ppermute | solution.py:165
  293.4 20.5 %collective-permute-start.12 = (bf16[512,512]{1,0:T(8,128)(2,1)S(1)}, bf16[512,512]{1,0:T(8,128)(2,1)S(1)}, u32[]{:S(2)}, u32[]{:S(2)}) collective-permute-start(bf16[512,512]{1,0:T(8,128)(2,1)S(1)} %fusion.91), channel_id=1, source_target_pairs={{0,2},{1,3},{2,0},{3,1},{4,6},{5,7},{6,4},{7,5},{8,10},{9,11},{10,... | collective-permute-start | bytes 1572872 | tf_op jit(solution)/shard_map/ppermute | solution.py:165
  488.2 26.1 %collective-permute-start.60 = (bf16[4,256,512]{2,1,0:T(8,128)(2,1)S(1)}, bf16[4,256,512]{2,1,0:T(8,128)(2,1)S(1)}, u32[]{:S(2)}, u32[]{:S(2)}) collective-permute-start(bf16[4,256,512]{2,1,0:T(8,128)(2,1)S(1)} %dynamic-slice_bitcast_fusion), channel_id=1, source_target_pairs={{0,4},{4,0},{1,5},{5,1},{2,6},{6,2},{3,7},{7,3},{8,12},{12,8},{9,1... | collective-permute-start | bytes 3145736 | tf_op jit(solution)/shard_map/ppermute | solution.py:165
  490.0 2.6 collective-permute-start.35
  491.7 45.1 %collective-permute-start.56 = (bf16[4,256,512]{2,1,0:T(8,128)(2,1)S(1)}, bf16[4,256,512]{2,1,0:T(8,128)(2,1)S(1)}, u32[]{:S(2)}, u32[]{:S(2)}) collective-permute-start(bf16[4,256,512]{2,1,0:T(8,128)(2,1)S(1)} %dynamic-slice_bitcast_fusion.1), channel_id=1, source_target_pairs={{0,4},{4,0},{1,5},{5,1},{2,6},{6,2},{3,7},{7,3},{8,12},{12,8},{9,1... | collective-permute-start | bytes 3145736 | tf_op jit(solution)/shard_map/ppermute | solution.py:165
  492.7 3.6 collective-permute-start.36
  494.4 63.9 %collective-permute-start.52 = (bf16[4,256,512]{2,1,0:T(8,128)(2,1)S(1)}, bf16[4,256,512]{2,1,0:T(8,128)(2,1)S(1)}, u32[]{:S(2)}, u32[]{:S(2)}) collective-permute-start(bf16[4,256,512]{2,1,0:T(8,128)(2,1)S(1)} %dynamic-slice_bitcast_fusion.2), channel_id=1, source_target_pairs={{0,4},{4,0},{1,5},{5,1},{2,6},{6,2},{3,7},{7,3},{8,12},{12,8},{9,1... | collective-permute-start | bytes 3145736 | tf_op jit(solution)/shard_map/ppermute | solution.py:165
  496.8 13.6 %collective-permute-start.37 = (bf16[512,512]{1,0:T(8,128)(2,1)S(1)}, bf16[512,512]{1,0:T(8,128)(2,1)S(1)}, u32[]{:S(2)}, u32[]{:S(2)}) collective-permute-start(bf16[512,512]{1,0:T(8,128)(2,1)S(1)} %fusion.67), channel_id=1, source_target_pairs={{0,2},{1,3},{2,0},{3,1},{4,6},{5,7},{6,4},{7,5},{8,10},{9,11},{10,... | collective-permute-start | bytes 1572872 | tf_op jit(solution)/shard_map/ppermute | solution.py:165
  500.8 190.0 %collective-permute-start.30 = (bf16[2048,1024]{1,0:T(8,128)(2,1)}, bf16[2048,1024]{1,0:T(8,128)(2,1)}, u32[]{:S(2)}, u32[]{:S(2)}) collective-permute-start(bf16[2048,1024]{1,0:T(8,128)(2,1)} %pad_maximum_fusion.3), channel_id=1, source_target_pairs={{0,1},{1,0},{2,3},{3,2},{4,5},{5,4},{6,7},{7,6},{8,9},{9,8},{10,11... | collective-permute-start | bytes 12582920 | tf_op jit(solution)/shard_map/ppermute | solution.py:165
  511.5 101.8 %collective-permute-start.38 = (bf16[512,1024]{1,0:T(8,128)(2,1)}, bf16[512,1024]{1,0:T(8,128)(2,1)}, u32[]{:S(2)}, u32[]{:S(2)}) collective-permute-start(bf16[512,1024]{1,0:T(8,128)(2,1)} %pad_maximum_fusion.13), channel_id=1, source_target_pairs={{0,1},{1,0},{2,3},{3,2},{4,5},{5,4},{6,7},{7,6},{8,9},{9,8},{10,11... | collective-permute-start | bytes 3145736 | tf_op jit(solution)/shard_map/ppermute | solution.py:165
  514.8 45.9 %collective-permute-start.61 = (bf16[256,512]{1,0:T(8,128)(2,1)S(1)}, bf16[256,512]{1,0:T(8,128)(2,1)S(1)}, u32[]{:S(2)}, u32[]{:S(2)}) collective-permute-start(bf16[256,512]{1,0:T(8,128)(2,1)S(1)} %get-tuple-element.469), channel_id=1, source_target_pairs={{0,24},{8,16},{16,8},{24,0},{1,25},{9,17},{17,9},{25,1},{2,26},{10... | collective-permute-start | bytes 786440 | tf_op jit(solution)/shard_map/ppermute | solution.py:165
  536.8 25.8 %collective-permute-start.62 = (bf16[256,512]{1,0:T(8,128)(2,1)S(1)}, bf16[256,512]{1,0:T(8,128)(2,1)S(1)}, u32[]{:S(2)}, u32[]{:S(2)}) collective-permute-start(bf16[256,512]{1,0:T(8,128)(2,1)S(1)} %get-tuple-element.470), channel_id=1, source_target_pairs={{0,16},{8,24},{16,0},{24,8},{1,17},{9,25},{17,1},{25,9},{2,18},{10... | collective-permute-start | bytes 786440 | tf_op jit(solution)/shard_map/ppermute | solution.py:165
  558.3 8.7 collective-permute-start.63
  560.7 12.3 %collective-permute-start.57 = (bf16[256,512]{1,0:T(8,128)(2,1)}, bf16[256,512]{1,0:T(8,128)(2,1)S(1)}, u32[]{:S(2)}, u32[]{:S(2)}) collective-permute-start(bf16[256,512]{1,0:T(8,128)(2,1)} %get-tuple-element.475), channel_id=1, source_target_pairs={{0,24},{8,16},{16,8},{24,0},{1,25},{9,17},{17,9},{25,1},{2,26},{10... | collective-permute-start | bytes 786440 | tf_op jit(solution)/shard_map/ppermute | solution.py:165
  562.6 30.8 %collective-permute-start.58 = (bf16[256,512]{1,0:T(8,128)(2,1)}, bf16[256,512]{1,0:T(8,128)(2,1)}, u32[]{:S(2)}, u32[]{:S(2)}) collective-permute-start(bf16[256,512]{1,0:T(8,128)(2,1)} %get-tuple-element.476), channel_id=1, source_target_pairs={{0,16},{8,24},{16,0},{24,8},{1,17},{9,25},{17,1},{25,9},{2,18},{10... | collective-permute-start | bytes 786440 | tf_op jit(solution)/shard_map/ppermute | solution.py:165
  567.0 26.3 %collective-permute-start.59 = (bf16[256,512]{1,0:T(8,128)(2,1)}, bf16[256,512]{1,0:T(8,128)(2,1)}, u32[]{:S(2)}, u32[]{:S(2)}) collective-permute-start(bf16[256,512]{1,0:T(8,128)(2,1)} %get-tuple-element.474), channel_id=1, source_target_pairs={{0,8},{8,0},{16,24},{24,16},{1,9},{9,1},{17,25},{25,17},{2,10},{10... | collective-permute-start | bytes 786440 | tf_op jit(solution)/shard_map/ppermute | solution.py:165
  572.9 23.0 %collective-permute-start.53 = (bf16[256,512]{1,0:T(8,128)(2,1)}, bf16[256,512]{1,0:T(8,128)(2,1)S(1)}, u32[]{:S(2)}, u32[]{:S(2)}) collective-permute-start(bf16[256,512]{1,0:T(8,128)(2,1)} %get-tuple-element.481), channel_id=1, source_target_pairs={{0,24},{8,16},{16,8},{24,0},{1,25},{9,17},{17,9},{25,1},{2,26},{10... | collective-permute-start | bytes 786440 | tf_op jit(solution)/shard_map/ppermute | solution.py:165
  593.3 15.4 %collective-permute-start.54 = (bf16[256,512]{1,0:T(8,128)(2,1)}, bf16[256,512]{1,0:T(8,128)(2,1)S(1)}, u32[]{:S(2)}, u32[]{:S(2)}) collective-permute-start(bf16[256,512]{1,0:T(8,128)(2,1)} %get-tuple-element.482), channel_id=1, source_target_pairs={{0,16},{8,24},{16,0},{24,8},{1,17},{9,25},{17,1},{25,9},{2,18},{10... | collective-permute-start | bytes 786440 | tf_op jit(solution)/shard_map/ppermute | solution.py:165
  593.4 15.4 %collective-permute-start.55 = (bf16[256,512]{1,0:T(8,128)(2,1)}, bf16[256,512]{1,0:T(8,128)(2,1)S(1)}, u32[]{:S(2)}, u32[]{:S(2)}) collective-permute-start(bf16[256,512]{1,0:T(8,128)(2,1)} %get-tuple-element.480), channel_id=1, source_target_pairs={{0,8},{8,0},{16,24},{24,16},{1,9},{9,1},{17,25},{25,17},{2,10},{10... | collective-permute-start | bytes 786440 | tf_op jit(solution)/shard_map/ppermute | solution.py:165
  649.0 15.1 %collective-permute-start.39 = (bf16[512,512]{1,0:T(8,128)(2,1)}, bf16[512,512]{1,0:T(8,128)(2,1)}, u32[]{:S(2)}, u32[]{:S(2)}) collective-permute-start(bf16[512,512]{1,0:T(8,128)(2,1)} %fusion.98), channel_id=1, source_target_pairs={{0,4},{4,0},{1,5},{5,1},{2,6},{6,2},{3,7},{7,3},{8,12},{12,8},{9,1... | collective-permute-start | bytes 1572872 | tf_op jit(solution)/shard_map/ppermute | solution.py:165
  654.6 32.0 %collective-permute-start.48 = (bf16[4,256,512]{2,1,0:T(8,128)(2,1)}, bf16[4,256,512]{2,1,0:T(8,128)(2,1)}, u32[]{:S(2)}, u32[]{:S(2)}) collective-permute-start(bf16[4,256,512]{2,1,0:T(8,128)(2,1)} %fusion.79), channel_id=1, source_target_pairs={{0,4},{4,0},{1,5},{5,1},{2,6},{6,2},{3,7},{7,3},{8,12},{12,8},{9,1... | collective-permute-start | bytes 3145736 | tf_op jit(solution)/shard_map/ppermute | solution.py:165
  675.9 119.4 %collective-permute-start.44 = (bf16[4,256,1024]{2,1,0:T(8,128)(2,1)}, bf16[4,256,1024]{2,1,0:T(8,128)(2,1)}, u32[]{:S(2)}, u32[]{:S(2)}) collective-permute-start(bf16[4,256,1024]{2,1,0:T(8,128)(2,1)} %fusion.58), channel_id=1, source_target_pairs={{0,4},{4,0},{1,5},{5,1},{2,6},{6,2},{3,7},{7,3},{8,12},{12,8},{9,1... | collective-permute-start | bytes 6291464 | tf_op jit(solution)/shard_map/ppermute | solution.py:165
  679.9 17.0 %collective-permute-start.40 = (bf16[512,1024]{1,0:T(8,128)(2,1)S(1)}, bf16[512,1024]{1,0:T(8,128)(2,1)S(1)}, u32[]{:S(2)}, u32[]{:S(2)}) collective-permute-start(bf16[512,1024]{1,0:T(8,128)(2,1)S(1)} %pad_maximum_fusion.15), channel_id=1, source_target_pairs={{0,1},{1,0},{2,3},{3,2},{4,5},{5,4},{6,7},{7,6},{8,9},{9,8},{10,11... | collective-permute-start | bytes 3145736 | tf_op jit(solution)/shard_map/ppermute | solution.py:165
  688.3 11.1 %collective-permute-start.49 = (bf16[256,512]{1,0:T(8,128)(2,1)S(1)}, bf16[256,512]{1,0:T(8,128)(2,1)S(1)}, u32[]{:S(2)}, u32[]{:S(2)}) collective-permute-start(bf16[256,512]{1,0:T(8,128)(2,1)S(1)} %get-tuple-element.431), channel_id=1, source_target_pairs={{0,8},{8,0},{16,24},{24,16},{1,9},{9,1},{17,25},{25,17},{2,10},{10... | collective-permute-start | bytes 786440 | tf_op jit(solution)/shard_map/ppermute | solution.py:165
  688.4 18.7 %collective-permute-start.50 = (bf16[256,512]{1,0:T(8,128)(2,1)S(1)}, bf16[256,512]{1,0:T(8,128)(2,1)S(1)}, u32[]{:S(2)}, u32[]{:S(2)}) collective-permute-start(bf16[256,512]{1,0:T(8,128)(2,1)S(1)} %get-tuple-element.433), channel_id=1, source_target_pairs={{0,16},{8,24},{16,0},{24,8},{1,17},{9,25},{17,1},{25,9},{2,18},{10... | collective-permute-start | bytes 786440 | tf_op jit(solution)/shard_map/ppermute | solution.py:165
  690.8 16.2 %collective-permute-start.51 = (bf16[256,512]{1,0:T(8,128)(2,1)S(1)}, bf16[256,512]{1,0:T(8,128)(2,1)S(1)}, u32[]{:S(2)}, u32[]{:S(2)}) collective-permute-start(bf16[256,512]{1,0:T(8,128)(2,1)S(1)} %get-tuple-element.432), channel_id=1, source_target_pairs={{0,24},{8,16},{16,8},{24,0},{1,25},{9,17},{17,9},{25,1},{2,26},{10... | collective-permute-start | bytes 786440 | tf_op jit(solution)/shard_map/ppermute | solution.py:165
  696.9 106.9 %collective-permute-start.31 = (bf16[2048,512]{1,0:T(8,128)(2,1)}, bf16[2048,512]{1,0:T(8,128)(2,1)}, u32[]{:S(2)}, u32[]{:S(2)}) collective-permute-start(bf16[2048,512]{1,0:T(8,128)(2,1)} %add_convert_fusion), channel_id=1, source_target_pairs={{0,2},{1,3},{2,0},{3,1},{4,6},{5,7},{6,4},{7,5},{8,10},{9,11},{10,... | collective-permute-start | bytes 6291464 | tf_op jit(solution)/shard_map/ppermute | solution.py:165
  699.4 51.4 %collective-permute-start.41 = (bf16[512,512]{1,0:T(8,128)(2,1)S(1)}, bf16[512,512]{1,0:T(8,128)(2,1)S(1)}, u32[]{:S(2)}, u32[]{:S(2)}) collective-permute-start(bf16[512,512]{1,0:T(8,128)(2,1)S(1)} %fusion.85), channel_id=1, source_target_pairs={{0,2},{1,3},{2,0},{3,1},{4,6},{5,7},{6,4},{7,5},{8,10},{9,11},{10,... | collective-permute-start | bytes 1572872 | tf_op jit(solution)/shard_map/ppermute | solution.py:165
  752.6 38.9 %collective-permute-start.42 = (f32[512,1]{0,1:T(1,128)S(1)}, f32[512,1]{0,1:T(1,128)S(1)}, u32[]{:S(2)}, u32[]{:S(2)}) collective-permute-start(f32[512,1]{0,1:T(1,128)S(1)} %bitcast.709), channel_id=1, source_target_pairs={{0,1},{1,0},{2,3},{3,2},{4,5},{5,4},{6,7},{7,6},{8,9},{9,8},{10,11... | collective-permute-start | bytes 6152 | tf_op jit(solution)/shard_map/ppermute | solution.py:165
  791.5 3.9 collective-permute-start.43
  799.1 25.5 %collective-permute-start.45 = (bf16[256,1024]{1,0:T(8,128)(2,1)S(1)}, bf16[256,1024]{1,0:T(8,128)(2,1)S(1)}, u32[]{:S(2)}, u32[]{:S(2)}) collective-permute-start(bf16[256,1024]{1,0:T(8,128)(2,1)S(1)} %get-tuple-element.424), channel_id=1, source_target_pairs={{0,8},{8,0},{16,24},{24,16},{1,9},{9,1},{17,25},{25,17},{2,10},{10... | collective-permute-start | bytes 1572872 | tf_op jit(solution)/shard_map/ppermute | solution.py:165
  801.3 38.2 %collective-permute-start.46 = (bf16[256,1024]{1,0:T(8,128)(2,1)S(1)}, bf16[256,1024]{1,0:T(8,128)(2,1)S(1)}, u32[]{:S(2)}, u32[]{:S(2)}) collective-permute-start(bf16[256,1024]{1,0:T(8,128)(2,1)S(1)} %get-tuple-element.426), channel_id=1, source_target_pairs={{0,16},{8,24},{16,0},{24,8},{1,17},{9,25},{17,1},{25,9},{2,18},{10... | collective-permute-start | bytes 1572872 | tf_op jit(solution)/shard_map/ppermute | solution.py:165
  802.2 37.3 %collective-permute-start.47 = (bf16[256,1024]{1,0:T(8,128)(2,1)S(1)}, bf16[256,1024]{1,0:T(8,128)(2,1)S(1)}, u32[]{:S(2)}, u32[]{:S(2)}) collective-permute-start(bf16[256,1024]{1,0:T(8,128)(2,1)S(1)} %get-tuple-element.425), channel_id=1, source_target_pairs={{0,24},{8,16},{16,8},{24,0},{1,25},{9,17},{17,9},{25,1},{2,26},{10... | collective-permute-start | bytes 1572872 | tf_op jit(solution)/shard_map/ppermute | solution.py:165
  807.8 39.6 %collective-permute-start.32 = (bf16[512,512]{1,0:T(8,128)(2,1)S(1)}, bf16[512,512]{1,0:T(8,128)(2,1)S(1)}, u32[]{:S(2)}, u32[]{:S(2)}) collective-permute-start(bf16[512,512]{1,0:T(8,128)(2,1)S(1)} %get-tuple-element.436), channel_id=1, source_target_pairs={{0,8},{8,0},{16,24},{24,16},{1,9},{9,1},{17,25},{25,17},{2,10},{10... | collective-permute-start | bytes 1572872 | tf_op jit(solution)/shard_map/ppermute | solution.py:165
  808.9 75.6 %collective-permute-start.33 = (bf16[512,512]{1,0:T(8,128)(2,1)S(1)}, bf16[512,512]{1,0:T(8,128)(2,1)S(1)}, u32[]{:S(2)}, u32[]{:S(2)}) collective-permute-start(bf16[512,512]{1,0:T(8,128)(2,1)S(1)} %get-tuple-element.438), channel_id=1, source_target_pairs={{0,16},{8,24},{16,0},{24,8},{1,17},{9,25},{17,1},{25,9},{2,18},{10... | collective-permute-start | bytes 1572872 | tf_op jit(solution)/shard_map/ppermute | solution.py:165
  824.6 59.9 %collective-permute-start.34 = (bf16[512,512]{1,0:T(8,128)(2,1)S(1)}, bf16[512,512]{1,0:T(8,128)(2,1)S(1)}, u32[]{:S(2)}, u32[]{:S(2)}) collective-permute-start(bf16[512,512]{1,0:T(8,128)(2,1)S(1)} %get-tuple-element.437), channel_id=1, source_target_pairs={{0,24},{8,16},{16,8},{24,0},{1,25},{9,17},{17,9},{25,1},{2,26},{10... | collective-permute-start | bytes 1572872 | tf_op jit(solution)/shard_map/ppermute | solution.py:165
  (111 other events, 1412.3 us)

commit v3 on v2

--- a/solution.py
+++ b/solution.py
@@ -721,6 +721,592 @@
     )(h_low, gain, grad_full, wg, wu, wd)
 
 
+class Relay:
+    def __init__(self, z, place, own_send, forward_send, recv):
+        self.z, self.place = z, place
+        self.own_send, self.forward_send, self.recv = own_send, forward_send, recv
+
+    def own_copy(self, src, target, index):
+        return remote(
+            src,
+            self.place(self.z, target),
+            self.own_send.at[index],
+            self.recv.at[self.z],
+            {"dp": target},
+        )
+
+    def own(self, src, wait=False):
+        @pl.when(self.z < 3)
+        def _():
+            copy = self.own_copy(src, self.z + 1, 0)
+            copy.wait_send() if wait else copy.start()
+
+        @pl.when(self.z > 0)
+        def _():
+            copy = self.own_copy(src, self.z - 1, 1)
+            copy.wait_send() if wait else copy.start()
+
+    def forward_copy(self, o, target):
+        return remote(
+            self.place(o, self.z),
+            self.place(o, target),
+            self.forward_send.at[o],
+            self.recv.at[o],
+            {"dp": target},
+        )
+
+    def forward(self, o, wait=False):
+        @pl.when(jnp.logical_and(o < self.z, self.z < 3))
+        def _():
+            copy = self.forward_copy(o, self.z + 1)
+            copy.wait_send() if wait else copy.start()
+
+        @pl.when(jnp.logical_and(o > self.z, self.z > 0))
+        def _():
+            copy = self.forward_copy(o, self.z - 1)
+            copy.wait_send() if wait else copy.start()
+
+    def arrive(self, o):
+        self.forward_copy(o, self.z ^ 1).wait_recv()
+        self.forward(o)
+
+
+def attn_fwd_kernel(
+    tok_ref,
+    cot_ref,
+    gains_ref,
+    cos_ref,
+    sin_ref,
+    valid_ref,
+    wq_hbm,
+    wk_hbm,
+    wv_hbm,
+    wo_hbm,
+    wg_hbm,
+    wu_hbm,
+    wd_hbm,
+    xn_ref,
+    factor_ref,
+    q_ref,
+    kv_ref,
+    lse_ref,
+    mix_ref,
+    h_ref,
+    aw_ref,
+    wo_ref,
+    gain_ref,
+    fg_hbm,
+    fu_hbm,
+    fd_hbm,
+    do_hbm,
+    full,
+    qkv,
+    gain_in,
+    own_piece,
+    part,
+    core_in,
+    x_out,
+    x_in,
+    load_sem,
+    piece_sem,
+    do_sem,
+    g_send,
+    g_recv,
+    x_send,
+    x_recv,
+    t_send,
+    t_recv,
+    a_own,
+    a_fwd,
+    a_recv,
+    ay_send,
+    ay_recv,
+    o_own,
+    o_fwd,
+    o_recv,
+    oy_send,
+    oy_recv,
+    f_send,
+    f_recv,
+    fy_send,
+    fy_recv,
+    d_own,
+    d_fwd,
+    d_recv,
+    dx_send,
+    dx_recv,
+    dc_send,
+    dc_recv,
+    kv_send,
+    kv_recv,
+    p_send,
+    p_recv,
+    r_send,
+    r_recv,
+):
+    rows, width = tok_ref.shape
+    model = 4 * width
+    low, wide = jnp.bfloat16, jnp.float32
+    row_size = lax.axis_size("row")
+    local = wq_hbm.shape[0]
+    q_cols, k_cols = wq_hbm.shape[1], wk_hbm.shape[1]
+    hidden = fg_hbm.shape[1]
+    half = HEAD_SIZE // 2
+    z, y, col = (lax.axis_index(name) for name in ("dp", "row", "col"))
+    core, far = {"col": col ^ 1}, {"col": col ^ 2}
+    mid = jnp.logical_and(z > 0, z < 3)
+    others = range(1, row_size)
+
+    def chunk(s):
+        return jnp.where(mid, 5 - s, s) if s >= 2 else s
+
+    def cols(p):
+        return pl.ds(p * width, width)
+
+    def slot(o, r):
+        return pl.ds(pl.multiple_of(((o ^ col) * row_size + r) * local, local), local)
+
+    greet(
+        [{"dp": z ^ j, "row": y ^ k} for j in range(4) for k in range(row_size) if j + k > 0]
+        + [core, far]
+    )
+
+    loads = [
+        pltpu.make_async_copy(src, aw_ref.at[slot(z, y), pl.ds(at, src.shape[1])], load_sem.at[i])
+        for i, (src, at) in enumerate(
+            ((wq_hbm, 0), (wk_hbm, q_cols), (wv_hbm, q_cols + k_cols))
+        )
+    ]
+    load_out = pltpu.make_async_copy(wo_hbm, wo_ref.at[slot(z, y)], load_sem.at[3])
+    for load in loads:
+        load.start()
+    load_out.start()
+
+    def t_copy(which):
+        src = full.at[:, cols(2)] if which == 2 else tok_ref
+        target = far if which == 1 else core
+        dst = full.at[:, cols((1, 2, 3)[which])]
+        return remote(src, dst, t_send.at[which], t_recv.at[which], target)
+
+    t_copy(1).start()
+    t_copy(0).start()
+
+    def g_copy(j, k):
+        at = (z ^ col) * row_size + y
+        return remote(
+            gains_ref,
+            gain_in.at[at],
+            g_send.at[j, k],
+            g_recv.at[j, k],
+            {"dp": z ^ j, "row": y ^ k},
+        )
+
+    pairs = [(j, k) for j in range(4) for k in range(row_size) if j + k > 0]
+    for j, k in pairs:
+        g_copy(j, k).start()
+    gain_in[(z ^ col) * row_size + y] = gains_ref[...]
+
+    attn = Relay(z, lambda o, t: aw_ref.at[slot(o, y)], a_own, a_fwd, a_recv)
+    outw = Relay(z, lambda o, t: wo_ref.at[slot(o, y)], o_own, o_fwd, o_recv)
+    douts = Relay(z, lambda o, t: do_hbm.at[o ^ t, :, cols(0)], d_own, d_fwd, d_recv)
+
+    def row_copy(ref, o, k, send, recv):
+        block = ref.at[slot(o, y)]
+        return remote(block, block, send.at[k, o], recv.at[k, o], {"row": y ^ k})
+
+    def row_wait(ref, o, k, send, recv):
+        block = ref.at[slot(o, y ^ k)]
+        remote(block, block, send.at[k, o], recv.at[k, o], {"row": y ^ k}).wait_recv()
+
+    for load in loads:
+        load.wait()
+    attn.own(aw_ref.at[slot(z, y)])
+    for k in others:
+        row_copy(aw_ref, z, k, ay_send, ay_recv).start()
+
+    weights = ((wg_hbm, fg_hbm), (wu_hbm, fu_hbm), (wd_hbm, fd_hbm))
+
+    def quarter(j):
+        return pl.ds(pl.multiple_of((z ^ j) * hidden, hidden), hidden)
+
+    pieces = [
+        pltpu.make_async_copy(weights[a][0].at[:, quarter(0)], own_piece.at[a], piece_sem.at[a])
+        for a in range(3)
+    ]
+    for piece in pieces:
+        piece.start()
+
+    full[:, 0:width] = tok_ref[...]
+    t_copy(1).wait_recv()
+    t_copy(2).start()
+    attn.arrive(z ^ 1)
+    for k in others:
+        row_copy(aw_ref, z ^ 1, k, ay_send, ay_recv).start()
+    load_out.wait()
+
+    def attn_arrive(j):
+        attn.arrive(z ^ j)
+        for k in others:
+            row_copy(aw_ref, z ^ j, k, ay_send, ay_recv).start()
+
+    @pl.when(mid)
+    def _():
+        attn_arrive(3)
+
+    outw.own(wo_ref.at[slot(z, y)])
+
+    for j, k in pairs:
+        g_copy(j, k).wait_recv()
+    for i in range(4 * row_size):
+        gain_ref[:, i * local : (i + 1) * local] = gain_in[i]
+    t_copy(0).wait_recv()
+    t_copy(2).wait_recv()
+
+    def norm(r):
+        x = full[r, :].astype(wide)
+        factor = lax.rsqrt(jnp.sum(x * x, axis=1, keepdims=True) * (1.0 / model) + EPSILON)
+        xn_ref[r, :] = (x * factor * gain_ref[0:1, :]).astype(low)
+        factor_ref[r, :] = jnp.broadcast_to(factor, (factor.shape[0], 128))
+
+    tiles(rows, 32, norm)
+
+    @pl.when(jnp.logical_not(mid))
+    def _():
+        attn_arrive(2)
+
+    attn_arrive_last = jnp.where(mid, 2, 3)
+    attn.arrive(z ^ attn_arrive_last)
+    for k in others:
+        row_copy(aw_ref, z ^ attn_arrive_last, k, ay_send, ay_recv).start()
+    for s in range(1, 4):
+        outw.arrive(z ^ chunk(s))
+
+    def f_copy(a, j):
+        src, dst = weights[a]
+        return remote(
+            src.at[:, quarter(j)],
+            dst.at[slot(z, y)],
+            f_send.at[a, j],
+            f_recv.at[a, j],
+            {"dp": z ^ j},
+        )
+
+    for a in range(3):
+        for j in (3, 2, 1):
+            f_copy(a, j).start()
+
+    def fy_copy(a, j, k):
+        src = own_piece.at[a] if j == 0 else weights[a][1].at[slot(z ^ j, y)]
+        return remote(
+            src,
+            weights[a][1].at[slot(z ^ j, y)],
+            fy_send.at[a, k, j],
+            fy_recv.at[a, k, j],
+            {"row": y ^ k},
+        )
+
+    for o in range(4):
+        for k in others:
+            row_wait(aw_ref, o, k, ay_send, ay_recv)
+    for n in range(0, q_cols + 2 * k_cols, 512):
+        qkv[:, n : n + 512] = dot_nn(xn_ref[...], aw_ref[:, n : n + 512])
+
+    def rope(r, at):
+        c, s = cos_ref[r, :], sin_ref[r, :]
+        first, second = qkv[r, at : at + half], qkv[r, at + half : at + 2 * half]
+        return first * c - second * s, second * c + first * s
+
+    def keys(r):
+        first, second = rope(r, q_cols)
+        kv_ref[y, r, 0:half] = first.astype(low)
+        kv_ref[y, r, half : 2 * half] = second.astype(low)
+        kv_ref[y, r, k_cols : 2 * k_cols] = qkv[r, q_cols + k_cols : q_cols + 2 * k_cols].astype(low)
+
+    tiles(rows, 64, keys)
+    heads = q_cols // HEAD_SIZE
+
+    def queries(r):
+        for h in range(heads):
+            first, second = rope(r, h * HEAD_SIZE)
+            q_ref[h, r, 0:half] = first.astype(low)
+            q_ref[h, r, half : 2 * half] = second.astype(low)
+
+    tiles(rows, 64, queries)
+
+    def kv_copy(k, source):
+        block = kv_ref.at[source]
+        return remote(block, block, kv_send.at[k], kv_recv.at[k], {"row": y ^ k})
+
+    for k in others:
+
+        @pl.when((y ^ k) > y)
+        def _():
+            kv_copy(k, y).start()
+
+    for o in range(4):
+        for k in others:
+            row_copy(wo_ref, o, k, oy_send, oy_recv).start()
+
+    douts.own(cot_ref)
+
+    def dx_copy(j):
+        src = cot_ref if j == 0 else do_hbm.at[j, :, cols(0)]
+        return remote(src, do_hbm.at[j, :, cols(2)], dx_send.at[j], dx_recv.at[j], far)
+
+    def dc_copy(j, which):
+        if which:
+            src = do_hbm.at[j, :, cols(2)]
+        else:
+            src = cot_ref if j == 0 else do_hbm.at[j, :, cols(0)]
+        return remote(
+            src, do_hbm.at[j, :, cols(1 + 2 * which)], dc_send.at[which, j], dc_recv.at[which, j], core
+        )
+
+    dx_copy(0).start()
+    dc_copy(0, 0).start()
+    do_own = pltpu.make_async_copy(cot_ref, do_hbm.at[0, :, cols(0)], do_sem)
+    do_own.start()
+    for piece in pieces:
+        piece.wait()
+    stores = [
+        pltpu.make_async_copy(own_piece.at[a], weights[a][1].at[slot(z, y)], piece_sem.at[a])
+        for a in range(3)
+    ]
+    for a in range(3):
+        stores[a].start()
+        for k in others:
+            fy_copy(a, 0, k).start()
+    for k in others:
+
+        @pl.when((y ^ k) < y)
+        def _():
+            kv_copy(k, y ^ k).wait_recv()
+
+    q_tile = 256
+    score_scale = 1.0 / math.sqrt(HEAD_SIZE)
+
+    def attend_tile(i, unused):
+        at = pl.ds(pl.multiple_of(i * q_tile, q_tile), q_tile)
+        query_pos = y * rows + i * q_tile + lax.broadcasted_iota(jnp.int32, (q_tile, rows), 0)
+        for h in range(heads):
+            query = q_ref[h, at, :]
+
+            def block(b, carry):
+                top, total, accum = carry
+                scores = times_transposed(query, kv_ref[b, :, 0:k_cols]) * score_scale
+                key_pos = b * rows + lax.broadcasted_iota(jnp.int32, (q_tile, rows), 1)
+                scores = jnp.where(key_pos <= query_pos, scores, -1e30)
+                new_top = jnp.maximum(top, jnp.max(scores, axis=1, keepdims=True))
+                probs = jnp.exp(scores - new_top)
+                keep = jnp.exp(top - new_top)
+                total = total * keep + jnp.sum(probs, axis=1, keepdims=True)
+                accum = accum * keep + dot_nn(probs.astype(low), kv_ref[b, :, k_cols : 2 * k_cols])
+                return new_top, total, accum
+
+            top, total, accum = lax.fori_loop(
+                0,
+                y + 1,
+                block,
+                (
+                    jnp.full((q_tile, 1), -1e30, wide),
+                    jnp.zeros((q_tile, 1), wide),
+                    jnp.zeros((q_tile, HEAD_SIZE), wide),
+                ),
+            )
+            lse_ref[h, at, :] = jnp.broadcast_to(top + jnp.log(total), (q_tile, 128))
+            mix_ref[at, h * HEAD_SIZE : (h + 1) * HEAD_SIZE] = (
+                accum / total * valid_ref[at, :]
+            ).astype(low)
+        return unused
+
+    lax.fori_loop(0, rows // q_tile, attend_tile, 0)
+
+    for o in range(4):
+        for k in others:
+            row_wait(wo_ref, o, k, oy_send, oy_recv)
+    part_copy = remote(part.at[:, pl.ds(2 * width, 2 * width)], core_in, p_send, p_recv, core)
+    for at, p in ((2, 1), (3, 3), (0, 0)):
+        part[:, at * width : (at + 1) * width] = times_transposed(
+            mix_ref[...], wo_ref[p * width : (p + 1) * width, :]
+        ).astype(low)
+    part_copy.start()
+    part[:, width : 2 * width] = times_transposed(
+        mix_ref[...], wo_ref[2 * width : 3 * width, :]
+    ).astype(low)
+    part_copy.wait()
+
+    def add_core(r):
+        x_out[r, :] = (
+            part[r, width : 2 * width].astype(wide) + core_in[r, width : 2 * width].astype(wide)
+        ).astype(low)
+        h_ref[r, :] = (
+            tok_ref[r, :].astype(wide)
+            + part[r, 0:width].astype(wide)
+            + core_in[r, 0:width].astype(wide)
+        )
+
+    tiles(rows, 64, add_core)
+    r_copy = remote(x_out, x_in, r_send, r_recv, far)
+    r_copy.start()
+
+    def f_arrive(a, j):
+        f_copy(a, j).wait_recv()
+        for k in others:
+            fy_copy(a, j, k).start()
+
+    for j in (1, 2, 3):
+        f_arrive(0, j)
+    r_copy.wait()
+
+    def add_far(r):
+        h_ref[r, :] = h_ref[r, :] + x_in[r, :].astype(wide)
+
+    tiles(rows, 64, add_far)
+    for a in (1, 2):
+        for j in (1, 2, 3):
+            f_arrive(a, j)
+
+    def d_arrive(j):
+        douts.arrive(z ^ j)
+        dx_copy(j).start()
+        dc_copy(j, 0).start()
+
+    def d_settle(j):
+        dx_copy(j).wait_recv()
+        dc_copy(j, 1).start()
+
+    d_settle(0)
+    for s in range(1, 4):
+        for j in sorted({s, 5 - s} if s >= 2 else {s}):
+            if s < 2:
+                d_arrive(j)
+            else:
+
+                @pl.when(chunk(s) == j)
+                def _():
+                    d_arrive(j)
+
+    for j in (1, 2, 3):
+        d_settle(j)
+
+    for a in range(3):
+        stores[a].wait()
+        for j in range(4):
+            for k in others:
+                fy_copy(a, j, k).wait_send()
+                block = weights[a][1].at[slot(z ^ j, y ^ k)]
+                remote(
+                    block, block, fy_send.at[a, k, j], fy_recv.at[a, k, j], {"row": y ^ k}
+                ).wait_recv()
+            if j:
+                f_copy(a, j).wait_send()
+    do_own.wait()
+    for j in range(4):
+        dx_copy(j).wait_send()
+        dc_copy(j, 0).wait()
+        dc_copy(j, 1).wait()
+    for relay, src in ((attn, aw_ref.at[slot(z, y)]), (outw, wo_ref.at[slot(z, y)]), (douts, cot_ref)):
+        relay.own(src, wait=True)
+        for j in (1, 2, 3):
+            relay.forward(z ^ j, wait=True)
+    for o in range(4):
+        for k in others:
+            row_copy(aw_ref, o, k, ay_send, ay_recv).wait_send()
+            row_copy(wo_ref, o, k, oy_send, oy_recv).wait_send()
+    for k in others:
+
+        @pl.when((y ^ k) > y)
+        def _():
+            kv_copy(k, y).wait_send()
+
+    for j, k in pairs:
+        g_copy(j, k).wait_send()
+    for which in range(3):
+        t_copy(which).wait_send()
+
+
+def attn_fwd_call(tokens, cot, gains, cos, sin, valid, wq, wk, wv, wo, wg, wu, wd):
+    rows, width = tokens.shape
+    model = 4 * width
+    low, wide = jnp.bfloat16, jnp.float32
+    row_size = lax.axis_size("row")
+    local, q_cols = wq.shape
+    k_cols = wk.shape[1]
+    hidden = wg.shape[1] // 4
+    heads = q_cols // HEAD_SIZE
+    vmem = pl.BlockSpec(memory_space=pltpu.VMEM)
+    hbm = pl.BlockSpec(memory_space=pl.ANY)
+    dma = pltpu.SemaphoreType.DMA
+    relay = [dma((2,)), dma((4,)), dma((4,))]
+    over_row = [dma((row_size, 4)), dma((row_size, 4))]
+    shape = jax.ShapeDtypeStruct
+    return pl.pallas_call(
+        attn_fwd_kernel,
+        out_shape=(
+            shape((rows, model), low),
+            shape((rows, 128), wide),
+            shape((heads, rows, HEAD_SIZE), low),
+            shape((row_size, rows, 2 * k_cols), low),
+            shape((heads, rows, 128), wide),
+            shape((rows, q_cols), low),
+            shape((rows, width), wide),
+            shape((model, q_cols + 2 * k_cols), low),
+            shape((model, q_cols), low),
+            shape((8, model), wide),
+            shape((model, hidden), low),
+            shape((model, hidden), low),
+            shape((model, hidden), low),
+            shape((4, rows, model), low),
+        ),
+        in_specs=[vmem] * 6 + [hbm] * 7,
+        out_specs=(vmem,) * 10 + (hbm,) * 4,
+        scratch_shapes=[
+            pltpu.VMEM((rows, model), low),
+            pltpu.VMEM((rows, q_cols + 2 * k_cols), wide),
+            pltpu.VMEM((4 * row_size, 8, local), wide),
+            pltpu.VMEM((3, local, hidden), low),
+            pltpu.VMEM((rows, model), low),
+            pltpu.VMEM((rows, 2 * width), low),
+            pltpu.VMEM((rows, width), low),
+            pltpu.VMEM((rows, width), low),
+            dma((4,)),
+            dma((3,)),
+            dma(()),
+            dma((4, row_size)),
+            dma((4, row_size)),
+            dma((1,)),
+            dma((1,)),
+            dma((3,)),
+            dma((3,)),
+            *relay,
+            *over_row,
+            *relay,
+            *over_row,
+            dma((3, 4)),
+            dma((3, 4)),
+            dma((3, row_size, 4)),
+            dma((3, row_size, 4)),
+            *relay,
+            dma((4,)),
+            dma((4,)),
+            dma((2, 4)),
+            dma((2, 4)),
+            dma((row_size,)),
+            dma((row_size,)),
+            dma(()),
+            dma(()),
+            dma(()),
+            dma(()),
+        ],
+        compiler_params=pltpu.CompilerParams(
+            collective_id=1, has_side_effects=True, vmem_limit_bytes=60_000_000
+        ),
+        cost_estimate=pl.CostEstimate(
+            flops=10_000_000_000, bytes_accessed=40_000_000, transcendentals=2_000_000
+        ),
+    )(tokens, cot, gains, cos, sin, valid, wq, wk, wv, wo, wg, wu, wd)
+
+
 def per_device(
     tokens,
     w_query,
@@ -749,58 +1335,59 @@
     valid = (query_pos < lengths[0]).astype(wide)[:, None]
     cosine_table, sine_table = rope_tables(query_pos.astype(wide))
 
-    gains = lax.all_gather(jnp.stack([gain_attn, gain_ffn]), ("dp", "row"), axis=1, tiled=True)
-    gains = gains.reshape(2, 4, col_width)
-    gains = jnp.concatenate(reorder([gains[:, p] for p in range(4)], me_col), axis=1)
-    gain_one, gain_two = gains[0].astype(wide), gains[1].astype(wide)
-
-    x_full = gather_col(tokens)
+    gains = jnp.zeros((8, gain_attn.shape[0]), wide)
+    gains = gains.at[0].set(gain_attn.astype(wide)).at[1].set(gain_ffn.astype(wide))
     q_cols, k_cols = w_query.shape[1], key_matrix.shape[1]
-    attn_weight = gather_weight(
-        jnp.concatenate([w_query, key_matrix, value_matrix], axis=1), shift
-    )
-    out_weight = gather_weight(w_output.T, shift)
-    down_weight = exchange_weight(w_down.T, shift)
-    gate_weight = exchange_weight(w_gate, shift)
-    up_weight = exchange_weight(w_up, shift)
-    x_wide = x_full.astype(wide)
-    factor_one, normed = norm_rows(x_wide, gain_one)
-    qkv = jnp.dot(normed, attn_weight, preferred_element_type=wide)
     kv_heads = k_cols // HEAD_SIZE
-    query_rot = rotary_apply(
-        qkv[:, :q_cols].reshape(row_count, kv_heads * query_group, HEAD_SIZE),
+    grad_out = (cotangent.astype(wide) * valid).astype(low)
+    (
+        normed,
+        factor_one,
+        query_rows,
+        kv_all,
+        log_total,
+        mixed_heads,
+        residual,
+        attn_weight,
+        out_weight,
+        gains,
+        gate_weight,
+        up_weight,
+        down_weight,
+        grad_out_full,
+    ) = attn_fwd_call(
+        tokens,
+        grad_out,
+        gains,
         cosine_table,
         sine_table,
-    ).astype(low)
-    key_rot = rotary_apply(
-        qkv[:, q_cols : q_cols + k_cols].reshape(row_count, kv_heads, HEAD_SIZE),
-        cosine_table,
-        sine_table,
-    ).astype(low)
-    kv_all = gather_row(
-        jnp.concatenate(
-            [key_rot.reshape(row_count, k_cols), qkv[:, q_cols + k_cols :].astype(low)], axis=1
-        ),
-        0,
-    )
-    keys_all = kv_all[:, :k_cols].reshape(slot_size, kv_heads, HEAD_SIZE)
-    values_all = kv_all[:, k_cols:].reshape(slot_size, kv_heads, HEAD_SIZE)
-    query_rows = query_rot.reshape(row_count, kv_heads, query_group, HEAD_SIZE).transpose(
-        1, 2, 0, 3
-    )
-    attended, log_total = attend(
-        query_rows, keys_all, values_all, query_pos, key_block, score_scale
-    )
-    mixed_heads = (
-        attended.transpose(2, 0, 1, 3).reshape(row_count, q_cols) * valid
-    ).astype(low)
-    residual = tokens.astype(wide) + scatter_col(times_transposed(mixed_heads, out_weight))
-
-    grad_out = (cotangent.astype(wide) * valid).astype(low)
-    grad_out_full = gather_tokens(grad_out).reshape(4, row_count, model_width)
+        valid,
+        w_query,
+        key_matrix,
+        value_matrix,
+        w_output.T,
+        w_gate,
+        w_up,
+        w_down.T,
+    )
+    factor_one = factor_one[:, :1]
+    gain_one, gain_two = gains[0], gains[1]
+    query_rows = query_rows.reshape(kv_heads, query_group, row_count, HEAD_SIZE)
+    log_total = log_total[:, :, 0].reshape(kv_heads, query_group, row_count)
+    attended = (
+        mixed_heads.astype(wide)
+        .reshape(row_count, kv_heads, query_group, HEAD_SIZE)
+        .transpose(1, 2, 0, 3)
+    )
+    keys_all = kv_all[:, :, :k_cols].reshape(slot_size, kv_heads, HEAD_SIZE)
+    values_all = kv_all[:, :, k_cols:].reshape(slot_size, kv_heads, HEAD_SIZE)
+    seen = (jnp.arange(slot_size) < (me_row + 1) * row_count)[:, None, None]
+    keys_all = jnp.where(seen, keys_all, 0)
+    values_all = jnp.where(seen, values_all, 0)
+
     residual_low = residual.astype(low)
     grad_normed_two, factor_two, out_part, grad_gate_part, grad_up_part, grad_down_part = ffn_call(
-        residual_low, gain_two[None], grad_out_full, gate_weight, up_weight, down_weight
+        residual_low, gains[1:2], grad_out_full, gate_weight, up_weight, down_weight
     )
     layer_out = (residual + scatter_tokens(out_part.reshape(-1, model_width))).astype(low)
     own_gain_two = gain_two[:col_width]

time: 904 us -> 759 us (0.84)
  waiting for transfers between devices: 343 us -> 158 us
  Pallas kernels: 149 us -> 329 us
  starting transfers between devices: 102 us -> 43.3 us
  other arithmetic: 110 us -> 57.9 us
  matrix products: 37.9 us -> 26.3 us
    ppermute x64 -> x34, waiting for transfers between devices: 343 us -> 158 us  [swap(): return lax.ppermute(value, axis, [(i, i ^ bit) for i in range(size)])]
    pallas_call x0 -> x1, Pallas kernels: none -> 183 us  [attn_fwd_call(): pl.pallas_call(attn_fwd_kernel, out_shape=(shape((rows, model), low), sha...]
    ppermute x64 -> x34, starting transfers between devices: 102 us -> 43.3 us  [swap(): return lax.ppermute(value, axis, [(i, i ^ bit) for i in range(size)])]
    all_gather x1 -> x0, blocking collectives: 36.2 us -> none  [per_device(): lax.all_gather(jnp.stack([gain_attn, gain_ffn]), ('dp', 'row'), axis=1, t...]
    psum x1, blocking collectives: 38.8 us -> 69.8 us  [per_device(): gain_grads = lax.psum(gain_grads, ('dp', 'row', 'col'))]
    concatenate x12 -> x0, other arithmetic: 26.7 us -> none  [the longest x1 20.2 us: gather_col(): jnp.concatenate([value, near[:, :width], far, near[:, width:]], axis=1)]
    concatenate x3 -> x1, other arithmetic: 16.1 us -> 2.12 us  [gather_col(): near = swap(jnp.concatenate([value, far], axis=1), 'col', 1)]
    dynamic_slice x8 -> x9, local copies, waits for them, and re-layouts: 7.69 us -> 17.6 us  [the longest x4 9.41 us: scatter_row(): mine = lax.dynamic_index_in_dim(value, me, axis, keepdims=False)]
  transfers between devices with their start and end apart: 64 -> 34, of which waited for: 30 -> 14; matrix products, arithmetic and copies ran while one was open for 19% -> 16% of each run, Pallas kernels for 0% -> 0%
where the time goes in v3:
time: 759 us; the launch traced here: 748 us
  Pallas kernels  329 us (43%)
  waiting for transfers between devices  158 us (21%)
  blocking collectives  69.8 us (9%)
  local copies, waits for them, and re-layouts  59.3 us (8%)
  other arithmetic  57.9 us (8%)
  starting transfers between devices  43.3 us (6%)
  matrix products  26.3 us (3%)
    pallas_call x1, Pallas kernels, attn_fwd_call(): pl.pallas_call(attn_fwd_kernel, out_shape=(shape((rows, model), low), sha...  183 us
    ppermute x34, waiting for transfers between devices, swap(): return lax.ppermute(value, axis, [(i, i ^ bit) for i in range(size)])  158 us
    pallas_call x1, Pallas kernels, ffn_call(): pl.pallas_call(ffn_kernel, out_shape=(jax.ShapeDtypeStruct((rows, width),...  146 us
    psum x1, blocking collectives, per_device(): gain_grads = lax.psum(gain_grads, ('dp', 'row', 'col'))  69.8 us
    ppermute x34, starting transfers between devices, swap(): return lax.ppermute(value, axis, [(i, i ^ bit) for i in range(size)])  43.3 us
    unnamed x83, local copies, waits for them, and re-layouts  23.4 us
  transfers between devices with their start and end apart: 34, of which 14 were waited for; matrix products, arithmetic and copies ran while one was open for 16% of the time, Pallas kernels for 0%

profile of v3, /device:TPU:0, one launch (start us, length us, event | category | flops | bytes accessed | tf_op | source)
XLA Modules:
  0.0 747.6 jit_solution(10024876220178595880)
XLA Ops:
  2.2 2.3 copy.71
  5.3 1.8 multiply_sine_fusion.1
  8.7 183.0 %shard_map.203 = (bf16[512,2048]{1,0:T(8,128)(2,1)}, f32[512,128]{1,0:T(8,128)}, bf16[2,512,256]{2,1,0:T(8,128)(2,1)S(1)}, bf16[2,512,512]{2,1,0:T(8,128)(2,1)},...) custom-call(bf16[512,512]{1,0:T(8,128)(2,1)} %tok_ref.1, ...), custom_call_target="tpu_custom_call" | custom-call | flops 10000000000 | bytes 40000000 | tf_op jit(solution)/shard_map/pallas_call | solution.py:1243
  194.0 2.1 convert_element_type.236.h_ref
  196.1 146.0 %shard_map.204 = (f32[512,512]{1,0:T(8,128)}, f32[512,128]{1,0:T(8,128)}, bf16[4,512,2048]{2,1,0:T(8,128)(2,1)}, bf16[2048,512]{1,0:T(8,128)(2,1)}, bf16[2048,51...) custom-call(bf16[512,512]{1,0:T(8,128)(2,1)} %convert_element_type.236.h_ref, f32[1,2048]{1,0:T(1,128)} %slice.212.gain_ref, ...), custom_call_target="tpu_custom_call" | custom-call | flops 38654705664 | bytes 40000000 | tf_op jit(solution)/shard_map/pallas_call | solution.py:664
  343.2 1.9 fusion.35
  345.2 3.9 constant_dynamic-slice_fusion.1
  349.1 2.3 copy.91
  351.4 2.5 collective-permute-start.30
  353.8 2.3 copy.89
  356.1 1.9 collective-permute-start.6
  358.1 2.7 fusion.77
  362.2 2.8 pad_maximum_fusion
  366.7 2.4 copy.104
  375.4 2.1 pad_maximum_fusion.2
  377.5 22.9 %collective-permute-done.26 = bf16[4,256,512]{1,2,0:T(8,128)(2,1)} collective-permute-done((bf16[4,256,512]{1,2,0:T(8,128)(2,1)}, bf16[4,256,512]{1,2,0:T(8,128)(2,1)}, u32[]{:S(2)}, u32[]{:S(2)}) %collective-permute-start.26) | collective-permute-done | bytes 1048608 | tf_op jit(solution)/shard_map/ppermute | solution.py:165
  403.5 3.0 collective-permute-start.29
  409.0 4.2 collective-permute-done.27
  414.5 17.2 %collective-permute-done.28 = bf16[256,512]{0,1:T(8,128)(2,1)S(1)} collective-permute-done((bf16[256,512]{0,1:T(8,128)(2,1)S(1)}, bf16[256,512]{0,1:T(8,128)(2,1)S(1)}, u32[]{:S(2)}, u32[]{:S(2)}) %collective-permute-start.28) | collective-permute-done | bytes 262176 | tf_op jit(solution)/shard_map/ppermute | solution.py:165
  431.7 3.0 collective-permute-start.33
  436.4 2.9 copy.93
  439.3 8.3 %collective-permute-done.32 = bf16[256,512]{0,1:T(8,128)(2,1)} collective-permute-done((bf16[256,512]{0,1:T(8,128)(2,1)}, bf16[256,512]{0,1:T(8,128)(2,1)}, u32[]{:S(2)}, u32[]{:S(2)}) %collective-permute-start.32) | collective-permute-done | bytes 262176 | tf_op jit(solution)/shard_map/ppermute | solution.py:165
  451.7 2.7 fusion.63
  454.5 1.9 constant_dynamic-slice_fusion.5
  457.2 2.3 copy.87
  460.9 2.3 copy.102
  465.0 3.3 fusion.27
  470.0 20.8 %while.17 = (s32[]{:T(128)}, f32[1,2,512,256]{3,2,1,0:T(8,128)}, f32[2,512,1,256]{1,3,0,2:T(8,128)}, f32[2,512,1,256]{1,3,0,2:T(8,128)}, s32[2]{0:T(128)S(1)}, /...) while((s32[]{:T(128)}, f32[1,2,512,256]{3,2,1,0:T(8,128)}, ...), condition=%wide.region_3.4_spmd.clone, body=%wide.region_2.3_spmd.clone.sunk | while | flops 1347159040 | bytes 34883456 | solution.py:151
  471.6 1.7 fusion.116
  473.9 2.5 fusion.118
  484.1 2.9 fusion.118
  490.8 2.1 fusion.56
  494.4 1.8 constant_dynamic-slice_fusion.7
  496.1 1.8 copy.84
  499.2 18.4 %collective-permute-done.9 = bf16[512,512]{0,1:T(8,128)(2,1)} collective-permute-done((bf16[512,512]{0,1:T(8,128)(2,1)}, bf16[512,512]{0,1:T(8,128)(2,1)}, u32[]{:S(2)}, u32[]{:S(2)}) %collective-permute-start.9) | collective-permute-done | bytes 524320 | tf_op jit(solution)/shard_map/ppermute | solution.py:165
  520.8 2.4 fusion.84
  523.5 2.8 copy-done.42
  526.3 2.4 fusion.57
  530.7 3.5 fusion.26
  534.3 2.5 collective-permute-start.23
  536.8 1.9 collective-permute-start.25
  541.1 4.3 collective-permute-done.23
  546.5 11.1 %collective-permute-done.24 = bf16[256,512]{0,1:T(8,128)(2,1)S(1)} collective-permute-done((bf16[256,512]{0,1:T(8,128)(2,1)S(1)}, bf16[256,512]{0,1:T(8,128)(2,1)S(1)}, u32[]{:S(2)}, u32[]{:S(2)}) %collective-permute-start.24) | collective-permute-done | bytes 262176 | tf_op jit(solution)/shard_map/ppermute | solution.py:165
  557.6 2.0 collective-permute-start.20
  559.8 2.5 collective-permute-start.21
  563.3 1.9 collective-permute-start.11
  565.2 4.3 add_convert_fusion
  569.4 1.8 collective-permute-start.1
  572.7 2.9 copy.92
  575.6 2.9 collective-permute-done.20
  578.5 2.1 add_bitcast_fusion
  580.6 2.0 fusion.43
  582.7 69.8 %psum.7 = f32[2,2048]{1,0:T(2,128)S(1)} all-reduce(f32[2,2048]{1,0:T(2,128)S(1)} %maximum_dynamic-update-slice_fusion), channel_id=1, replica_groups=mesh['dp'=4,'row'=2,'col'=4] {'dp','row','col'}, use_global_device_ids=true, to_apply=%region_7.8 | all-reduce | flops 4096 | bytes 32768 | tf_op jit(solution)/shard_map/psum | solution.py:1467
  652.5 2.3 collective-permute-start.13
  656.4 2.7 fusion.40
  659.1 3.5 bitcast_add_fusion
  662.9 2.8 collective-permute-start.16
  667.3 3.9 fusion.76
  671.4 2.8 collective-permute-start.3
  674.3 12.3 %collective-permute-done.15 = bf16[256,1024]{1,0:T(8,128)(2,1)S(1)} collective-permute-done((bf16[256,1024]{1,0:T(8,128)(2,1)S(1)}, bf16[256,1024]{1,0:T(8,128)(2,1)S(1)}, u32[]{:S(2)}, u32[]{:S(2)}) %collective-permute-start.15) | collective-permute-done | bytes 524320 | tf_op jit(solution)/shard_map/ppermute | solution.py:165
  686.6 2.3 collective-permute-start.4
  688.8 12.4 %collective-permute-done.16 = bf16[256,1024]{1,0:T(8,128)(2,1)S(1)} collective-permute-done((bf16[256,1024]{1,0:T(8,128)(2,1)S(1)}, bf16[256,1024]{1,0:T(8,128)(2,1)S(1)}, u32[]{:S(2)}, u32[]{:S(2)}) %collective-permute-start.16) | collective-permute-done | bytes 524320 | tf_op jit(solution)/shard_map/ppermute | solution.py:165
  703.5 5.5 collective-permute-done.2
  709.0 37.1 %collective-permute-done.3 = bf16[512,512]{1,0:T(8,128)(2,1)S(1)} collective-permute-done((bf16[512,512]{1,0:T(8,128)(2,1)S(1)}, bf16[512,512]{1,0:T(8,128)(2,1)S(1)}, u32[]{:S(2)}, u32[]{:S(2)}) %collective-permute-start.3) | collective-permute-done | bytes 524320 | tf_op jit(solution)/shard_map/ppermute | solution.py:165
  (228 shorter events, 68.2 us)
Async XLA Ops:
  0.6 3.8 copy-start.37
  0.7 4.6 copy-start.40
  0.7 4.7 copy-start.41
  0.7 6.5 copy-start.26
  345.1 11.0 %collective-permute-start.5 = (f32[512,1]{0,1:T(1,128)S(1)}, f32[512,1]{0,1:T(1,128)S(1)}, u32[]{:S(2)}, u32[]{:S(2)}) collective-permute-start(f32[512,1]{0,1:T(1,128)S(1)} %bitcast.442), channel_id=1, source_target_pairs={{0,1},{1,0},{2,3},{3,2},{4,5},{5,4},{6,7},{7,6},{8,9},{9,8},{10,11... | collective-permute-start | bytes 6152 | tf_op jit(solution)/shard_map/ppermute | solution.py:165
  351.4 52.1 %collective-permute-start.30 = (bf16[4,256,512]{1,2,0:T(8,128)(2,1)}, bf16[4,256,512]{1,2,0:T(8,128)(2,1)}, u32[]{:S(2)}, u32[]{:S(2)}) collective-permute-start(bf16[4,256,512]{1,2,0:T(8,128)(2,1)} %bitcast.423), channel_id=1, source_target_pairs={{0,4},{4,0},{1,5},{5,1},{2,6},{6,2},{3,7},{7,3},{8,12},{12,8},{9,1... | collective-permute-start | bytes 3145736 | tf_op jit(solution)/shard_map/ppermute | solution.py:165
  356.1 44.3 %collective-permute-start.26 = (bf16[4,256,512]{1,2,0:T(8,128)(2,1)}, bf16[4,256,512]{1,2,0:T(8,128)(2,1)}, u32[]{:S(2)}, u32[]{:S(2)}) collective-permute-start(bf16[4,256,512]{1,2,0:T(8,128)(2,1)} %bitcast.424), channel_id=1, source_target_pairs={{0,4},{4,0},{1,5},{5,1},{2,6},{6,2},{3,7},{7,3},{8,12},{12,8},{9,1... | collective-permute-start | bytes 3145736 | tf_op jit(solution)/shard_map/ppermute | solution.py:165
  356.1 4.6 collective-permute-start.6
  358.1 2.8 copy-start.14
  358.1 3.0 copy-start.27
  361.5 13.9 %copy-start.10 = (bf16[512,512]{1,0:T(8,128)(2,1)}, bf16[512,512]{1,0:T(8,128)(2,1)S(1)}, u32[]{:S(2)}) copy-start(bf16[512,512]{1,0:T(8,128)(2,1)S(1)} %fusion.32) | copy-start | bytes 1572868
  361.5 13.9 %collective-permute-start.7 = (bf16[512,512]{1,0:T(8,128)(2,1)S(1)}, bf16[512,512]{1,0:T(8,128)(2,1)}, u32[]{:S(2)}, u32[]{:S(2)}) collective-permute-start(bf16[512,512]{1,0:T(8,128)(2,1)S(1)} %fusion.32), channel_id=1, source_target_pairs={{0,2},{1,3},{2,0},{3,1},{4,6},{5,7},{6,4},{7,5},{8,10},{9,11},{10,... | collective-permute-start | bytes 1572872 | tf_op jit(solution)/shard_map/ppermute | solution.py:165
  362.2 3.6 copy-start.29
  365.0 198.3 %collective-permute-start = (bf16[2048,1024]{1,0:T(8,128)(2,1)}, bf16[2048,1024]{1,0:T(8,128)(2,1)}, u32[]{:S(2)}, u32[]{:S(2)}) collective-permute-start(bf16[2048,1024]{1,0:T(8,128)(2,1)} %pad_maximum_fusion), channel_id=1, source_target_pairs={{0,1},{1,0},{2,3},{3,2},{4,5},{5,4},{6,7},{7,6},{8,9},{9,8},{10,11... | collective-permute-start | bytes 12582920 | tf_op jit(solution)/shard_map/ppermute | solution.py:165
  366.7 3.9 copy-start.33
  369.0 4.4 copy-start.38
  370.5 3.1 copy-start.28
  373.6 26.9 %copy-start.16 = (bf16[4,1,256,512]{2,3,0,1:T(8,128)(2,1)S(1)}, bf16[4,1,256,512]{2,3,0,1:T(8,128)(2,1)}, u32[]{:S(2)}) copy-start(bf16[4,1,256,512]{2,3,0,1:T(8,128)(2,1)} %copy.103) | copy-start | bytes 3145732
  377.5 29.0 %copy-start.15 = (bf16[4,1,256,512]{2,3,0,1:T(8,128)(2,1)S(1)}, bf16[4,1,256,512]{2,3,0,1:T(8,128)(2,1)}, u32[]{:S(2)}) copy-start(bf16[4,1,256,512]{2,3,0,1:T(8,128)(2,1)} %copy.104) | copy-start | bytes 3145732
  377.5 72.9 %collective-permute-start.8 = (bf16[512,1024]{1,0:T(8,128)(2,1)}, bf16[512,1024]{1,0:T(8,128)(2,1)}, u32[]{:S(2)}, u32[]{:S(2)}) collective-permute-start(bf16[512,1024]{1,0:T(8,128)(2,1)} %pad_maximum_fusion.2), channel_id=1, source_target_pairs={{0,1},{1,0},{2,3},{3,2},{4,5},{5,4},{6,7},{7,6},{8,9},{9,8},{10,11... | collective-permute-start | bytes 3145736 | tf_op jit(solution)/shard_map/ppermute | solution.py:165
  402.0 11.1 %collective-permute-start.27 = (bf16[256,512]{0,1:T(8,128)(2,1)S(1)}, bf16[256,512]{0,1:T(8,128)(2,1)S(1)}, u32[]{:S(2)}, u32[]{:S(2)}) collective-permute-start(bf16[256,512]{0,1:T(8,128)(2,1)S(1)} %get-tuple-element.324), channel_id=1, source_target_pairs={{0,24},{8,16},{16,8},{24,0},{1,25},{9,17},{17,9},{25,1},{2,26},{10... | collective-permute-start | bytes 786440 | tf_op jit(solution)/shard_map/ppermute | solution.py:165
  403.5 28.3 %collective-permute-start.28 = (bf16[256,512]{0,1:T(8,128)(2,1)S(1)}, bf16[256,512]{0,1:T(8,128)(2,1)S(1)}, u32[]{:S(2)}, u32[]{:S(2)}) collective-permute-start(bf16[256,512]{0,1:T(8,128)(2,1)S(1)} %get-tuple-element.325), channel_id=1, source_target_pairs={{0,16},{8,24},{16,0},{24,8},{1,17},{9,25},{17,1},{25,9},{2,18},{10... | collective-permute-start | bytes 786440 | tf_op jit(solution)/shard_map/ppermute | solution.py:165
  403.5 28.3 %collective-permute-start.29 = (bf16[256,512]{0,1:T(8,128)(2,1)S(1)}, bf16[256,512]{0,1:T(8,128)(2,1)S(1)}, u32[]{:S(2)}, u32[]{:S(2)}) collective-permute-start(bf16[256,512]{0,1:T(8,128)(2,1)S(1)} %get-tuple-element.323), channel_id=1, source_target_pairs={{0,8},{8,0},{16,24},{24,16},{1,9},{9,1},{17,25},{25,17},{2,10},{10... | collective-permute-start | bytes 786440 | tf_op jit(solution)/shard_map/ppermute | solution.py:165
  413.2 26.1 %collective-permute-start.31 = (bf16[256,512]{0,1:T(8,128)(2,1)}, bf16[256,512]{0,1:T(8,128)(2,1)S(1)}, u32[]{:S(2)}, u32[]{:S(2)}) collective-permute-start(bf16[256,512]{0,1:T(8,128)(2,1)} %get-tuple-element.318), channel_id=1, source_target_pairs={{0,24},{8,16},{16,8},{24,0},{1,25},{9,17},{17,9},{25,1},{2,26},{10... | collective-permute-start | bytes 786440 | tf_op jit(solution)/shard_map/ppermute | solution.py:165
  431.7 15.9 %collective-permute-start.32 = (bf16[256,512]{0,1:T(8,128)(2,1)}, bf16[256,512]{0,1:T(8,128)(2,1)}, u32[]{:S(2)}, u32[]{:S(2)}) collective-permute-start(bf16[256,512]{0,1:T(8,128)(2,1)} %get-tuple-element.319), channel_id=1, source_target_pairs={{0,16},{8,24},{16,0},{24,8},{1,17},{9,25},{17,1},{25,9},{2,18},{10... | collective-permute-start | bytes 786440 | tf_op jit(solution)/shard_map/ppermute | solution.py:165
  431.7 15.9 %collective-permute-start.33 = (bf16[256,512]{0,1:T(8,128)(2,1)}, bf16[256,512]{0,1:T(8,128)(2,1)}, u32[]{:S(2)}, u32[]{:S(2)}) collective-permute-start(bf16[256,512]{0,1:T(8,128)(2,1)} %get-tuple-element.317), channel_id=1, source_target_pairs={{0,8},{8,0},{16,24},{24,16},{1,9},{9,1},{17,25},{25,17},{2,10},{10... | collective-permute-start | bytes 786440 | tf_op jit(solution)/shard_map/ppermute | solution.py:165
  448.9 2.8 copy-start.11
  448.9 2.8 copy-start.34
  459.4 70.9 %collective-permute-start.22 = (bf16[4,256,512]{1,2,0:T(8,128)(2,1)}, bf16[4,256,512]{1,2,0:T(8,128)(2,1)}, u32[]{:S(2)}, u32[]{:S(2)}) collective-permute-start(bf16[4,256,512]{1,2,0:T(8,128)(2,1)} %bitcast.422), channel_id=1, source_target_pairs={{0,4},{4,0},{1,5},{5,1},{2,6},{6,2},{3,7},{7,3},{8,12},{12,8},{9,1... | collective-permute-start | bytes 3145736 | tf_op jit(solution)/shard_map/ppermute | solution.py:165
  464.5 72.3 %collective-permute-start.18 = (bf16[4,256,512]{1,2,0:T(8,128)(2,1)}, bf16[4,256,512]{1,2,0:T(8,128)(2,1)}, u32[]{:S(2)}, u32[]{:S(2)}) collective-permute-start(bf16[4,256,512]{1,2,0:T(8,128)(2,1)} %bitcast.421), channel_id=1, source_target_pairs={{0,4},{4,0},{1,5},{5,1},{2,6},{6,2},{3,7},{7,3},{8,12},{12,8},{9,1... | collective-permute-start | bytes 3145736 | tf_op jit(solution)/shard_map/ppermute | solution.py:165
  470.0 3.3 copy-start.5
  473.9 5.1 copy-start.1
  480.2 3.3 copy-start.5
  484.1 2.9 copy-start.18
  484.1 5.4 copy-start.1
  492.9 24.7 %collective-permute-start.9 = (bf16[512,512]{0,1:T(8,128)(2,1)}, bf16[512,512]{0,1:T(8,128)(2,1)}, u32[]{:S(2)}, u32[]{:S(2)}) collective-permute-start(bf16[512,512]{0,1:T(8,128)(2,1)} %fusion.56), channel_id=1, source_target_pairs={{0,4},{4,0},{1,5},{5,1},{2,6},{6,2},{3,7},{7,3},{8,12},{12,8},{9,1... | collective-permute-start | bytes 1572872 | tf_op jit(solution)/shard_map/ppermute | solution.py:165
  498.3 19.3 %copy-start.20 = (f32[2,512,1,256]{1,3,0,2:T(8,128)S(1)}, f32[2,512,1,256]{1,3,0,2:T(8,128)}, u32[]{:S(2)}) copy-start(f32[2,512,1,256]{1,3,0,2:T(8,128)} %get-tuple-element.135) | copy-start | bytes 3145732
  517.6 3.2 copy-start.43
  523.2 39.1 %copy-start.21 = (f32[512,2048]{1,0:T(8,128)}, f32[512,2048]{1,0:T(8,128)S(1)}, u32[]{:S(2)}) copy-start(f32[512,2048]{1,0:T(8,128)S(1)} %get-tuple-element.345) | copy-start | bytes 12582916
  523.2 3.1 copy-start.42
  523.5 36.4 %collective-permute-start.10 = (bf16[512,1024]{1,0:T(8,128)(2,1)S(1)}, bf16[512,1024]{1,0:T(8,128)(2,1)S(1)}, u32[]{:S(2)}, u32[]{:S(2)}) collective-permute-start(bf16[512,1024]{1,0:T(8,128)(2,1)S(1)} %pad_maximum_fusion.4), channel_id=1, source_target_pairs={{0,1},{1,0},{2,3},{3,2},{4,5},{5,4},{6,7},{7,6},{8,9},{9,8},{10,11... | collective-permute-start | bytes 3145736 | tf_op jit(solution)/shard_map/ppermute | solution.py:165
  528.7 11.6 %copy-start.9 = (f32[2048,1024]{1,0:T(8,128)}, f32[2048,1024]{1,0:T(8,128)S(1)}, u32[]{:S(2)}) copy-start(f32[2048,1024]{1,0:T(8,128)S(1)} %fusion.57) | copy-start | bytes 25165828
  530.4 8.3 %copy-start.7 = (f32[4,1,256,512]{2,3,0,1:T(8,128)S(1)}, f32[4,1,256,512]{2,3,0,1:T(8,128)}, u32[]{:S(2)}) copy-start(f32[4,1,256,512]{2,3,0,1:T(8,128)} %copy.84) | copy-start | bytes 6291460
  534.3 11.1 %collective-permute-start.23 = (bf16[256,512]{0,1:T(8,128)(2,1)S(1)}, bf16[256,512]{0,1:T(8,128)(2,1)S(1)}, u32[]{:S(2)}, u32[]{:S(2)}) collective-permute-start(bf16[256,512]{0,1:T(8,128)(2,1)S(1)} %get-tuple-element.330), channel_id=1, source_target_pairs={{0,24},{8,16},{16,8},{24,0},{1,25},{9,17},{17,9},{25,1},{2,26},{10... | collective-permute-start | bytes 786440 | tf_op jit(solution)/shard_map/ppermute | solution.py:165
  536.8 20.8 %collective-permute-start.24 = (bf16[256,512]{0,1:T(8,128)(2,1)S(1)}, bf16[256,512]{0,1:T(8,128)(2,1)S(1)}, u32[]{:S(2)}, u32[]{:S(2)}) collective-permute-start(bf16[256,512]{0,1:T(8,128)(2,1)S(1)} %get-tuple-element.331), channel_id=1, source_target_pairs={{0,16},{8,24},{16,0},{24,8},{1,17},{9,25},{17,1},{25,9},{2,18},{10... | collective-permute-start | bytes 786440 | tf_op jit(solution)/shard_map/ppermute | solution.py:165
  536.8 20.8 %collective-permute-start.25 = (bf16[256,512]{0,1:T(8,128)(2,1)S(1)}, bf16[256,512]{0,1:T(8,128)(2,1)S(1)}, u32[]{:S(2)}, u32[]{:S(2)}) collective-permute-start(bf16[256,512]{0,1:T(8,128)(2,1)S(1)} %get-tuple-element.329), channel_id=1, source_target_pairs={{0,8},{8,0},{16,24},{24,16},{1,9},{9,1},{17,25},{25,17},{2,10},{10... | collective-permute-start | bytes 786440 | tf_op jit(solution)/shard_map/ppermute | solution.py:165
  545.4 113.7 %collective-permute-start.14 = (bf16[4,256,1024]{2,1,0:T(8,128)(2,1)}, bf16[4,256,1024]{2,1,0:T(8,128)(2,1)}, u32[]{:S(2)}, u32[]{:S(2)}) collective-permute-start(bf16[4,256,1024]{2,1,0:T(8,128)(2,1)} %fusion.23), channel_id=1, source_target_pairs={{0,4},{4,0},{1,5},{5,1},{2,6},{6,2},{3,7},{7,3},{8,12},{12,8},{9,1... | collective-permute-start | bytes 6291464 | tf_op jit(solution)/shard_map/ppermute | solution.py:165
  557.6 11.8 %collective-permute-start.19 = (bf16[256,512]{0,1:T(8,128)(2,1)S(1)}, bf16[256,512]{0,1:T(8,128)(2,1)}, u32[]{:S(2)}, u32[]{:S(2)}) collective-permute-start(bf16[256,512]{0,1:T(8,128)(2,1)S(1)} %get-tuple-element.302), channel_id=1, source_target_pairs={{0,8},{8,0},{16,24},{24,16},{1,9},{9,1},{17,25},{25,17},{2,10},{10... | collective-permute-start | bytes 786440 | tf_op jit(solution)/shard_map/ppermute | solution.py:165
  557.6 20.9 %collective-permute-start.20 = (bf16[256,512]{0,1:T(8,128)(2,1)}, bf16[256,512]{0,1:T(8,128)(2,1)}, u32[]{:S(2)}, u32[]{:S(2)}) collective-permute-start(bf16[256,512]{0,1:T(8,128)(2,1)} %get-tuple-element.304), channel_id=1, source_target_pairs={{0,16},{8,24},{16,0},{24,8},{1,17},{9,25},{17,1},{25,9},{2,18},{10... | collective-permute-start | bytes 786440 | tf_op jit(solution)/shard_map/ppermute | solution.py:165
  559.8 18.6 %collective-permute-start.21 = (bf16[256,512]{0,1:T(8,128)(2,1)S(1)}, bf16[256,512]{0,1:T(8,128)(2,1)}, u32[]{:S(2)}, u32[]{:S(2)}) collective-permute-start(bf16[256,512]{0,1:T(8,128)(2,1)S(1)} %get-tuple-element.303), channel_id=1, source_target_pairs={{0,24},{8,16},{16,8},{24,0},{1,25},{9,17},{17,9},{25,1},{2,26},{10... | collective-permute-start | bytes 786440 | tf_op jit(solution)/shard_map/ppermute | solution.py:165
  563.3 17.3 %collective-permute-start.11 = (bf16[512,512]{1,0:T(8,128)(2,1)}, bf16[512,512]{1,0:T(8,128)(2,1)}, u32[]{:S(2)}, u32[]{:S(2)}) collective-permute-start(bf16[512,512]{1,0:T(8,128)(2,1)} %fusion.49), channel_id=1, source_target_pairs={{0,2},{1,3},{2,0},{3,1},{4,6},{5,7},{6,4},{7,5},{8,10},{9,11},{10,... | collective-permute-start | bytes 1572872 | tf_op jit(solution)/shard_map/ppermute | solution.py:165
  569.4 97.9 %collective-permute-start.1 = (bf16[2048,512]{1,0:T(8,128)(2,1)}, bf16[2048,512]{1,0:T(8,128)(2,1)}, u32[]{:S(2)}, u32[]{:S(2)}) collective-permute-start(bf16[2048,512]{1,0:T(8,128)(2,1)} %add_convert_fusion), channel_id=1, source_target_pairs={{0,2},{1,3},{2,0},{3,1},{4,6},{5,7},{6,4},{7,5},{8,10},{9,11},{10,... | collective-permute-start | bytes 6291464 | tf_op jit(solution)/shard_map/ppermute | solution.py:165
  575.6 5.0 copy-start.24
  580.6 75.8 %copy-start.12 = (bf16[512,512]{1,0:T(8,128)(2,1)S(1)}, bf16[512,512]{1,0:T(8,128)(2,1)}, u32[]{:S(2)}) copy-start(bf16[512,512]{1,0:T(8,128)(2,1)} %copy-done.10) | copy-start | bytes 1572868
  580.6 75.8 %copy-start.25 = (bf16[512,512]{1,0:T(8,128)(2,1)S(1)}, bf16[512,512]{1,0:T(8,128)(2,1)}, u32[]{:S(2)}) copy-start(bf16[512,512]{1,0:T(8,128)(2,1)} %tok_ref.1) | copy-start | bytes 1572868
  582.6 69.9 %collective-permute-start.12 = (f32[512,1]{0,1:T(1,128)S(1)}, f32[512,1]{0,1:T(1,128)S(1)}, u32[]{:S(2)}, u32[]{:S(2)}) collective-permute-start(f32[512,1]{0,1:T(1,128)S(1)} %bitcast.436), channel_id=1, source_target_pairs={{0,1},{1,0},{2,3},{3,2},{4,5},{5,4},{6,7},{7,6},{8,9},{9,8},{10,11... | collective-permute-start | bytes 6152 | tf_op jit(solution)/shard_map/ppermute | solution.py:165
  652.5 3.9 collective-permute-start.13
  662.9 23.7 %collective-permute-start.15 = (bf16[256,1024]{1,0:T(8,128)(2,1)S(1)}, bf16[256,1024]{1,0:T(8,128)(2,1)S(1)}, u32[]{:S(2)}, u32[]{:S(2)}) collective-permute-start(bf16[256,1024]{1,0:T(8,128)(2,1)S(1)} %get-tuple-element.293), channel_id=1, source_target_pairs={{0,8},{8,0},{16,24},{24,16},{1,9},{9,1},{17,25},{25,17},{2,10},{10... | collective-permute-start | bytes 1572872 | tf_op jit(solution)/shard_map/ppermute | solution.py:165
  662.9 38.3 %collective-permute-start.16 = (bf16[256,1024]{1,0:T(8,128)(2,1)S(1)}, bf16[256,1024]{1,0:T(8,128)(2,1)S(1)}, u32[]{:S(2)}, u32[]{:S(2)}) collective-permute-start(bf16[256,1024]{1,0:T(8,128)(2,1)S(1)} %get-tuple-element.295), channel_id=1, source_target_pairs={{0,16},{8,24},{16,0},{24,8},{1,17},{9,25},{17,1},{25,9},{2,18},{10... | collective-permute-start | bytes 1572872 | tf_op jit(solution)/shard_map/ppermute | solution.py:165
  665.8 35.4 %collective-permute-start.17 = (bf16[256,1024]{1,0:T(8,128)(2,1)S(1)}, bf16[256,1024]{1,0:T(8,128)(2,1)S(1)}, u32[]{:S(2)}, u32[]{:S(2)}) collective-permute-start(bf16[256,1024]{1,0:T(8,128)(2,1)S(1)} %get-tuple-element.294), channel_id=1, source_target_pairs={{0,24},{8,16},{16,8},{24,0},{1,25},{9,17},{17,9},{25,1},{2,26},{10... | collective-permute-start | bytes 1572872 | tf_op jit(solution)/shard_map/ppermute | solution.py:165
  671.4 37.7 %collective-permute-start.2 = (bf16[512,512]{1,0:T(8,128)(2,1)S(1)}, bf16[512,512]{1,0:T(8,128)(2,1)S(1)}, u32[]{:S(2)}, u32[]{:S(2)}) collective-permute-start(bf16[512,512]{1,0:T(8,128)(2,1)S(1)} %get-tuple-element.307), channel_id=1, source_target_pairs={{0,8},{8,0},{16,24},{24,16},{1,9},{9,1},{17,25},{25,17},{2,10},{10... | collective-permute-start | bytes 1572872 | tf_op jit(solution)/shard_map/ppermute | solution.py:165
  671.4 74.7 %collective-permute-start.3 = (bf16[512,512]{1,0:T(8,128)(2,1)S(1)}, bf16[512,512]{1,0:T(8,128)(2,1)S(1)}, u32[]{:S(2)}, u32[]{:S(2)}) collective-permute-start(bf16[512,512]{1,0:T(8,128)(2,1)S(1)} %get-tuple-element.309), channel_id=1, source_target_pairs={{0,16},{8,24},{16,0},{24,8},{1,17},{9,25},{17,1},{25,9},{2,18},{10... | collective-permute-start | bytes 1572872 | tf_op jit(solution)/shard_map/ppermute | solution.py:165
  686.6 59.6 %collective-permute-start.4 = (bf16[512,512]{1,0:T(8,128)(2,1)S(1)}, bf16[512,512]{1,0:T(8,128)(2,1)S(1)}, u32[]{:S(2)}, u32[]{:S(2)}) collective-permute-start(bf16[512,512]{1,0:T(8,128)(2,1)S(1)} %get-tuple-element.308), channel_id=1, source_target_pairs={{0,24},{8,16},{16,8},{24,0},{1,25},{9,17},{17,9},{25,1},{2,26},{10... | collective-permute-start | bytes 1572872 | tf_op jit(solution)/shard_map/ppermute | solution.py:165
  701.8 44.3 %copy-start.4 = (f32[512,512]{1,0:T(8,128)S(1)}, f32[512,512]{1,0:T(8,128)}, u32[]{:S(2)}) copy-start(f32[512,512]{1,0:T(8,128)} %get-tuple-element.119) | copy-start | bytes 3145732
  (21 other events, 39.4 us)

commit v4 on v3

--- a/solution.py
+++ b/solution.py
@@ -7,11 +7,7 @@
 from jax.experimental.pallas import tpu as pltpu
 from jax.sharding import PartitionSpec as P
 
-QUERY_HEADS = 8
-KEY_VALUE_HEADS = 4
 HEAD_SIZE = 256
-
-
 EPSILON = 1e-06
 ROPE_BASE = 1000042.0
 
@@ -23,40 +19,6 @@
     return (jnp.cos(angle), jnp.sin(angle))
 
 
-def rotary_apply(values, cosine_table, sine_table):
-    half = values.shape[-1] // 2
-    first = values[..., :half]
-    second = values[..., half:]
-    cos_part = cosine_table[:, None, :]
-    sin_part = sine_table[:, None, :]
-    return jnp.concatenate(
-        [first * cos_part - second * sin_part, second * cos_part + first * sin_part], axis=-1
-    )
-
-
-def rotate_back(grads, cosine_table, sine_table):
-    half = grads.shape[-1] // 2
-    first = grads[..., :half]
-    second = grads[..., half:]
-    cos_part = cosine_table[:, None, :]
-    sin_part = sine_table[:, None, :]
-    return jnp.concatenate(
-        [first * cos_part + second * sin_part, second * cos_part - first * sin_part], axis=-1
-    )
-
-
-def norm_rows(full, gain):
-    factor = lax.rsqrt(jnp.mean(full * full, axis=1, keepdims=True) + EPSILON)
-    return (factor, (full * factor * gain).astype(jnp.bfloat16))
-
-
-def norm_back(full, factor, gain, grad):
-    inner = jnp.mean(gain * grad * full, axis=1, keepdims=True)
-    back = factor * gain * grad - full * factor * factor * factor * inner
-    gain_grad = jnp.sum(grad * full * factor, axis=0)
-    return (back, gain_grad)
-
-
 def contract_rows(left, right):
     return lax.dot_general(
         left, right, (((0,), (0,)), ((), ())), preferred_element_type=jnp.float32
@@ -67,213 +29,6 @@
     return lax.dot_general(
         left, right, (((1,), (1,)), ((), ())), preferred_element_type=jnp.float32
     )
-
-
-def masked_scores(query_rows, key_part, query_pos, index, key_block, score_scale):
-    scores = (
-        jnp.einsum("hgqd,khd->hgqk", query_rows, key_part, preferred_element_type=jnp.float32)
-        * score_scale
-    )
-    key_pos = index * key_block + jnp.arange(key_block, dtype=jnp.int32)
-    return jnp.where(key_pos[None, :] <= query_pos[:, None], scores, -1e30)
-
-
-def attend(query_rows, keys, values, query_pos, key_block, score_scale):
-    heads, query_group, token_count, size = query_rows.shape
-    blocks = keys.shape[0] // key_block
-    key_parts = keys.reshape(blocks, key_block, heads, size)
-    value_parts = values.reshape(blocks, key_block, heads, size)
-    indices = jnp.arange(blocks, dtype=jnp.int32)
-
-    def totals(carry, item):
-        top, total = carry
-        key_part, index = item
-        scores = masked_scores(query_rows, key_part, query_pos, index, key_block, score_scale)
-        new_top = jnp.maximum(top, jnp.max(scores, axis=-1))
-        total = total * jnp.exp(top - new_top) + jnp.sum(
-            jnp.exp(scores - new_top[..., None]), axis=-1
-        )
-        return ((new_top, total), None)
-
-    start = (
-        jnp.full((heads, query_group, token_count), -1e30, jnp.float32),
-        jnp.zeros((heads, query_group, token_count), jnp.float32),
-    )
-    (top, total), unused = lax.scan(totals, start, (key_parts, indices))
-    log_total = top + jnp.log(total)
-
-    def mixing(accum, item):
-        key_part, value_part, index = item
-        scores = masked_scores(query_rows, key_part, query_pos, index, key_block, score_scale)
-        probs = jnp.exp(scores - log_total[..., None]).astype(jnp.bfloat16)
-        return (
-            accum
-            + jnp.einsum("hgqk,khd->hgqd", probs, value_part, preferred_element_type=jnp.float32),
-            None,
-        )
-
-    accum, unused = lax.scan(
-        mixing,
-        jnp.zeros((heads, query_group, token_count, size), jnp.float32),
-        (key_parts, value_parts, indices),
-    )
-    return (accum, log_total)
-
-
-def attend_back(
-    query_rows, keys, values, query_pos, key_block, score_scale, log_total, delta, grad_out
-):
-    heads, query_group, token_count, size = query_rows.shape
-    blocks = keys.shape[0] // key_block
-    key_parts = keys.reshape(blocks, key_block, heads, size)
-    value_parts = values.reshape(blocks, key_block, heads, size)
-
-    def step(grad_query, item):
-        key_part, value_part, index = item
-        scores = masked_scores(query_rows, key_part, query_pos, index, key_block, score_scale)
-        probs = jnp.exp(scores - log_total[..., None])
-        probs_low = probs.astype(jnp.bfloat16)
-        grad_probs = jnp.einsum(
-            "hgqd,khd->hgqk", grad_out, value_part, preferred_element_type=jnp.float32
-        )
-        grad_scores = (probs * (grad_probs - delta[..., None]) * score_scale).astype(jnp.bfloat16)
-        grad_query = grad_query + jnp.einsum(
-            "hgqk,khd->hgqd", grad_scores, key_part, preferred_element_type=jnp.float32
-        )
-        grad_key = jnp.einsum(
-            "hgqk,hgqd->khd", grad_scores, query_rows, preferred_element_type=jnp.float32
-        )
-        grad_value = jnp.einsum(
-            "hgqk,hgqd->khd", probs_low, grad_out, preferred_element_type=jnp.float32
-        )
-        return (grad_query, (grad_key, grad_value))
-
-    grad_query, (grad_keys, grad_values) = lax.scan(
-        step,
-        jnp.zeros((heads, query_group, token_count, size), jnp.float32),
-        (key_parts, value_parts, jnp.arange(blocks, dtype=jnp.int32)),
-    )
-    return (
-        grad_query,
-        grad_keys.reshape(blocks * key_block, heads * size),
-        grad_values.reshape(blocks * key_block, heads * size),
-    )
-
-
-def swap(value, axis, bit):
-    size = lax.axis_size(axis)
-    return lax.ppermute(value, axis, [(i, i ^ bit) for i in range(size)])
-
-
-def gather_col(value):
-    width = value.shape[1]
-    far = swap(value, "col", 2)
-    near = swap(jnp.concatenate([value, far], axis=1), "col", 1)
-    return jnp.concatenate([value, near[:, :width], far, near[:, width:]], axis=1)
-
-
-def scatter_col(value):
-    width = value.shape[1] // 4
-    part = [value[:, p * width : (p + 1) * width].astype(jnp.float32) for p in range(4)]
-    low = jnp.bfloat16
-    got = swap(jnp.concatenate([part[1], part[3]], axis=1).astype(low), "col", 1)
-    keep_own = part[0] + got[:, :width].astype(jnp.float32)
-    keep_far = part[2] + got[:, width:].astype(jnp.float32)
-    return keep_own + swap(keep_far.astype(low), "col", 2).astype(jnp.float32)
-
-
-def col_sum(value):
-    value = value + swap(value, "col", 1)
-    return value + swap(value, "col", 2)
-
-
-def gather_row(value, axis):
-    if lax.axis_size("row") == 2:
-        other = swap(value, "row", 1)
-        first = lax.axis_index("row") == 0
-        return jnp.concatenate(
-            [jnp.where(first, value, other), jnp.where(first, other, value)], axis=axis
-        )
-    return lax.all_gather(value, "row", axis=axis, tiled=True)
-
-
-def scatter_row(value, axis):
-    if lax.axis_size("row") == 2:
-        me = lax.axis_index("row")
-        mine = lax.dynamic_index_in_dim(value, me, axis, keepdims=False)
-        theirs = lax.dynamic_index_in_dim(value, 1 - me, axis, keepdims=False)
-        got = swap(theirs.astype(jnp.bfloat16), "row", 1)
-        return mine.astype(jnp.float32) + got.astype(jnp.float32)
-    value = lax.psum_scatter(value.astype(jnp.bfloat16), "row", scatter_dimension=axis, tiled=True)
-    return jnp.squeeze(value, axis).astype(jnp.float32)
-
-
-def reorder(blocks, shift):
-    out = []
-    for p in range(4):
-        pick = blocks[p]
-        for s in range(1, 4):
-            pick = jnp.where(shift == s, blocks[p ^ s], pick)
-        out.append(pick)
-    return out
-
-
-def gather_weight(local, shift):
-    got = [local] + [swap(local, "dp", j) for j in range(1, 4)]
-    full = gather_row(jnp.stack(reorder(got, shift))[:, None], 1)
-    return full.reshape(-1, local.shape[1])
-
-
-def exchange_weight(local, shift):
-    me = lax.axis_index("dp")
-    quarter = local.shape[1] // 4
-
-    def part(j):
-        return lax.dynamic_slice_in_dim(local, (me ^ j) * quarter, quarter, 1)
-
-    got = [part(0)] + [swap(part(j), "dp", j) for j in range(1, 4)]
-    full = gather_row(jnp.stack(reorder(got, shift))[:, None], 1)
-    return full.reshape(-1, quarter)
-
-
-def return_weight(grad, shift):
-    rows, quarter = grad.shape
-    row_size = lax.axis_size("row")
-    own = scatter_row(grad.reshape(4, row_size, rows // (4 * row_size), quarter), 1)
-    own = own.astype(jnp.bfloat16)
-    sends = reorder([own[p] for p in range(4)], shift)
-    got = [sends[0]] + [swap(sends[j], "dp", j) for j in range(1, 4)]
-    natural = reorder(got, lax.axis_index("dp"))
-    return jnp.concatenate(natural, axis=1).astype(jnp.float32)
-
-
-def sum_weight(grad, shift):
-    rows, width = grad.shape
-    row_size = lax.axis_size("row")
-    own = scatter_row(grad.reshape(4, row_size, rows // (4 * row_size), width), 1)
-    sends = reorder([own[p] for p in range(4)], shift)
-    total = sends[0]
-    for j in range(1, 4):
-        total = total + swap(sends[j].astype(jnp.bfloat16), "dp", j).astype(jnp.float32)
-    return total
-
-
-def gather_tokens(value):
-    full = gather_col(
-        jnp.concatenate([value] + [swap(value, "dp", j) for j in range(1, 4)], axis=0)
-    )
-    return full
-
-
-def scatter_tokens(value):
-    own = scatter_col(value)
-    rows = own.shape[0] // 4
-    total = own[:rows]
-    for j in range(1, 4):
-        total = total + swap(
-            own[j * rows : (j + 1) * rows].astype(jnp.bfloat16), "dp", j
-        ).astype(jnp.float32)
-    return total
 
 
 def dot_nn(left, right):
@@ -1307,6 +1062,835 @@
     )(tokens, cot, gains, cos, sin, valid, wq, wk, wv, wo, wg, wu, wd)
 
 
+def lane_sums(value):
+    total = value[:, 0:128]
+    for at in range(128, value.shape[1], 128):
+        total = total + value[:, at : at + 128]
+    return total
+
+
+def attn_bwd_kernel(
+    dhn_ref,
+    factor_two_ref,
+    h_ref,
+    dout_ref,
+    gain_ref,
+    tok_ref,
+    factor_one_ref,
+    cos_ref,
+    sin_ref,
+    valid_ref,
+    q_ref,
+    lse_ref,
+    mix_ref,
+    xn_hbm,
+    kv_hbm,
+    aw_hbm,
+    wo_hbm,
+    out_hbm,
+    dwg_hbm,
+    dwu_hbm,
+    dwd_hbm,
+    layer_ref,
+    dtok_ref,
+    gains_ref,
+    dattn_ref,
+    dwo_ref,
+    gg_ref,
+    gu_ref,
+    gd_ref,
+    full,
+    xn,
+    kv,
+    aw,
+    wo,
+    lanes,
+    lanes_in,
+    do,
+    delta,
+    dq,
+    dkv,
+    dkv_out,
+    dkv_in,
+    graw,
+    dw_attn,
+    dw_out,
+    own_f,
+    row_f,
+    row_a,
+    row_o,
+    z_a,
+    z_o,
+    in_a,
+    in_o,
+    out_own,
+    core_in,
+    x_in,
+    z_in,
+    pcore_in,
+    px_out,
+    px_in,
+    gvec,
+    g_in,
+    load_sem,
+    l_send,
+    l_recv,
+    t_send,
+    t_recv,
+    fy_send,
+    fy_recv,
+    fz_send,
+    fz_recv,
+    own_sem,
+    oc_send,
+    oc_recv,
+    oo_sem,
+    ox_send,
+    ox_recv,
+    oz_send,
+    oz_recv,
+    kv_send,
+    kv_recv,
+    ay_send,
+    ay_recv,
+    az_send,
+    az_recv,
+    wy_send,
+    wy_recv,
+    wz_send,
+    wz_recv,
+    p_send,
+    p_recv,
+    r_send,
+    r_recv,
+    g_send,
+    g_recv,
+    gc_send,
+    gc_recv,
+):
+    rows, width = tok_ref.shape
+    model = 4 * width
+    low, wide = jnp.bfloat16, jnp.float32
+    row_size = lax.axis_size("row")
+    local = model // (4 * row_size)
+    heads = q_ref.shape[0]
+    q_cols = heads * HEAD_SIZE
+    all_cols = graw.shape[1]
+    k_cols = (all_cols - q_cols) // 2
+    hidden = own_f.shape[3]
+    half = HEAD_SIZE // 2
+    score_scale = 1.0 / math.sqrt(HEAD_SIZE)
+    z, y, col = (lax.axis_index(name) for name in ("dp", "row", "col"))
+    core, far = {"col": col ^ 1}, {"col": col ^ 2}
+    others = range(1, row_size)
+    partials = (dwg_hbm, dwu_hbm, dwd_hbm)
+    results = (gg_ref, gu_ref, gd_ref)
+
+    def cols(p):
+        return pl.ds(p * width, width)
+
+    greet(
+        [{"dp": z ^ j, "row": y ^ k} for j in range(4) for k in range(row_size) if j + k > 0]
+        + [{"col": col ^ m} for m in (1, 2, 3)]
+    )
+
+    def fy_copy(a, j, k):
+        at = z ^ j ^ col
+        return remote(
+            partials[a].at[at, y ^ k],
+            row_f.at[a, k - 1, j],
+            fy_send.at[a, k, j],
+            fy_recv.at[a, k, j],
+            {"row": y ^ k},
+        )
+
+    far_first = (3, 2, 1, 0)
+    for a in (0, 1):
+        for j in far_first:
+            for k in others:
+                fy_copy(a, j, k).start()
+
+    def own_load(a, j):
+        return pltpu.make_async_copy(
+            partials[a].at[z ^ j ^ col, y], own_f.at[a, j], own_sem.at[a, j]
+        )
+
+    def oc_copy(j, which):
+        return remote(
+            out_hbm.at[j, :, cols(1 + 2 * which)],
+            core_in.at[j, :, cols(which)],
+            oc_send.at[which, j],
+            oc_recv.at[which, j],
+            core,
+        )
+
+    def oo_copy(j, which):
+        return pltpu.make_async_copy(
+            out_hbm.at[j, :, cols(2 * which)], out_own.at[j, :, cols(which)], oo_sem.at[which, j]
+        )
+
+    loads = [
+        pltpu.make_async_copy(src, dst, load_sem.at[i])
+        for i, (src, dst) in enumerate(((wo_hbm, wo), (xn_hbm, xn), (aw_hbm, aw)))
+    ]
+
+    gain_two = gain_ref[1:2, 0:width]
+    gain_one = gain_ref[0:1, 0:width]
+
+    def residual(r):
+        return h_ref[r, :].astype(low).astype(wide)
+
+    def inner_two(r):
+        lanes[0, r, :] = lane_sums(gain_two * dhn_ref[r, :] * residual(r)).astype(low)
+
+    tiles(rows, 64, inner_two)
+    for j in far_first:
+        for which in (0, 1):
+            oc_copy(j, which).start()
+            oo_copy(j, which).start()
+
+    def l_copy(n, m):
+        return remote(
+            lanes.at[n], lanes_in.at[n, m - 1], l_send.at[n, m - 1], l_recv.at[n, m - 1], {"col": col ^ m}
+        )
+
+    for m in (2, 3, 1):
+        l_copy(0, m).start()
+    for load in loads:
+        load.start()
+    for a in range(3):
+        for j in far_first:
+            own_load(a, j).start()
+
+    def inner(n, r):
+        total = lanes[n, r, :].astype(wide)
+        for m in range(3):
+            total = total + lanes_in[n, m, r, :].astype(wide)
+        return jnp.sum(total, axis=1, keepdims=True) * (1.0 / model)
+
+    def gain_two_sum(i, total):
+        r = pl.ds(pl.multiple_of(i * 64, 64), 64)
+        return total + jnp.sum(
+            dhn_ref[r, :] * residual(r) * factor_two_ref[r, 0:1], axis=0, keepdims=True
+        )
+
+    gain_two_grad = lax.fori_loop(0, rows // 64, gain_two_sum, jnp.zeros((1, width), wide))
+    for m in (1, 2, 3):
+        l_copy(0, m).wait_recv()
+
+    def grad_residual(r):
+        factor = factor_two_ref[r, 0:1]
+        grad = (
+            dout_ref[r, :].astype(wide)
+            + factor * gain_two * dhn_ref[r, :]
+            - residual(r) * factor * factor * factor * inner(0, r)
+        ).astype(low)
+        full[r, 0:width] = grad
+        dtok_ref[r, :] = grad
+
+    tiles(rows, 64, grad_residual)
+
+    def t_copy(which):
+        src = full.at[:, cols(2)] if which == 2 else full.at[:, cols(0)]
+        dst = full.at[:, cols((1, 2, 3)[which])]
+        return remote(
+            src, dst, t_send.at[which], t_recv.at[which], far if which == 1 else core
+        )
+
+    def ox_copy(j):
+        return remote(out_own.at[j, :, cols(1)], x_in.at[j], ox_send.at[j], ox_recv.at[j], far)
+
+    def out_core(j):
+        for which in (0, 1):
+            oo_copy(j, which).wait()
+            oc_copy(j, which).wait_recv()
+
+        def add(r):
+            out_own[j, r, width : 2 * width] = (
+                out_own[j, r, width : 2 * width].astype(wide)
+                + core_in[j, r, width : 2 * width].astype(wide)
+            ).astype(low)
+            out_own[j, r, 0:width] = (
+                out_own[j, r, 0:width].astype(wide) + core_in[j, r, 0:width].astype(wide)
+            ).astype(low)
+
+        tiles(rows, 64, add)
+
+    out_core(3)
+    t_copy(1).start()
+    t_copy(0).start()
+    ox_copy(3).start()
+
+    def oz_copy(j):
+        return remote(
+            out_own.at[j, :, cols(0)], z_in.at[j - 1], oz_send.at[j], oz_recv.at[j], {"dp": z ^ j}
+        )
+
+    def out_far(j):
+        ox_copy(j).wait_recv()
+
+        def add(r):
+            out_own[j, r, 0:width] = (
+                out_own[j, r, 0:width].astype(wide) + x_in[j, r, :].astype(wide)
+            ).astype(low)
+
+        tiles(rows, 64, add)
+
+    def fz_copy(a, j):
+        at = pl.ds(pl.multiple_of(z * hidden, hidden), hidden)
+        return remote(
+            own_f.at[a, j], results[a].at[:, at], fz_send.at[a, j], fz_recv.at[a, j], {"dp": z ^ j}
+        )
+
+    def f_own(a):
+        at = pl.ds(pl.multiple_of(z * hidden, hidden), hidden)
+        return pltpu.make_async_copy(own_f.at[a, 0], results[a].at[:, at], own_sem.at[a, 0])
+
+    def f_row(a, j):
+        own_load(a, j).wait()
+        for k in others:
+            fy_copy(a, j, k).wait_recv()
+        total = own_f[a, j].astype(wide)
+        for k in others:
+            total = total + row_f[a, k - 1, j].astype(wide)
+        own_f[a, j] = total.astype(low)
+
+    out_core(2)
+    f_row(0, 3)
+    ox_copy(2).start()
+    out_core(1)
+    fz_copy(0, 3).start()
+    ox_copy(1).start()
+    t_copy(1).wait_recv()
+    t_copy(2).start()
+    out_core(0)
+    t_copy(0).wait_recv()
+    f_row(0, 2)
+    ox_copy(0).start()
+    loads[0].wait()
+    t_copy(2).wait_recv()
+
+    do[...] = (dot_nn(full[...], wo[...]) * valid_ref[...]).astype(low)
+    fz_copy(0, 2).start()
+    for p in range(4):
+        at = slice(p * width, (p + 1) * width)
+        dw_out[at, :] = contract_rows(full[:, at], mix_ref[...]).astype(low)
+
+    def deltas(r):
+        for h in range(heads):
+            at = slice(h * HEAD_SIZE, (h + 1) * HEAD_SIZE)
+            total = jnp.sum(do[r, at].astype(wide) * mix_ref[r, at].astype(wide), axis=1, keepdims=True)
+            delta[h, r, :] = jnp.broadcast_to(total, (total.shape[0], 128))
+
+    tiles(rows, 64, deltas)
+    dq[...] = jnp.zeros_like(dq)
+    q_tile = 256
+
+    def attend_block(b, slot):
+        dkv[...] = jnp.zeros_like(dkv)
+
+        def tile(i, unused):
+            at = pl.ds(pl.multiple_of(i * q_tile, q_tile), q_tile)
+            query_pos = y * rows + i * q_tile + lax.broadcasted_iota(jnp.int32, (q_tile, rows), 0)
+            key_pos = b * rows + lax.broadcasted_iota(jnp.int32, (q_tile, rows), 1)
+            for h in range(heads):
+                head = slice(h * HEAD_SIZE, (h + 1) * HEAD_SIZE)
+                query, grad = q_ref[h, at, :], do[at, head]
+                keys, values = kv[slot, :, 0:k_cols], kv[slot, :, k_cols : 2 * k_cols]
+                scores = times_transposed(query, keys) * score_scale
+                probs = jnp.where(
+                    key_pos <= query_pos, jnp.exp(scores - lse_ref[h, at, 0:1]), 0.0
+                )
+                grad_probs = times_transposed(grad, values)
+                grad_scores = (probs * (grad_probs - delta[h, at, 0:1]) * score_scale).astype(low)
+                dq[at, head] += dot_nn(grad_scores, keys)
+                dkv[:, 0:k_cols] += contract_rows(grad_scores, query)
+                dkv[:, k_cols : 2 * k_cols] += contract_rows(probs.astype(low), grad)
+            return unused
+
+        lax.fori_loop(0, rows // q_tile, tile, 0)
+
+    def kv_copy(k):
+        return remote(
+            dkv_out, dkv_in.at[k - 1], kv_send.at[k], kv_recv.at[k], {"row": y ^ k}
+        )
+
+    blocks = [*others, 0]
+
+    def when_block(k, body):
+        if k:
+            pl.when((y ^ k) < y)(body)
+        else:
+            body()
+
+    def kv_load(i):
+        return pltpu.make_async_copy(
+            kv_hbm.at[y ^ blocks[i]], kv.at[i % 2], load_sem.at[3 + i % 2]
+        )
+
+    when_block(blocks[0], lambda: kv_load(0).start())
+    for i, k in enumerate(others):
+        when_block(k, lambda i=i: kv_load(i).wait())
+        when_block(blocks[i + 1], lambda i=i: kv_load(i + 1).start())
+        when_block(k, lambda i=i, k=k: attend_block(y ^ k, i % 2))
+        if i:
+            when_block(k - 1, lambda k=k: kv_copy(k - 1).wait_send())
+
+        def keep(r):
+            dkv_out[r, :] = dkv[r, :].astype(low)
+
+        when_block(k, lambda: tiles(rows, 64, keep))
+        if i == 0:
+            f_row(0, 1)
+            f_row(0, 0)
+        when_block(k, lambda k=k: kv_copy(k).start())
+
+    fz_copy(0, 1).start()
+    f_own(0).start()
+    out_far(3)
+    f_row(1, 3)
+    oz_copy(3).start()
+    fz_copy(1, 3).start()
+
+    def wy_copy(j, k):
+        at = pl.ds(pl.multiple_of(((z ^ j ^ col) * row_size + (y ^ k)) * local, local), local)
+        return remote(
+            dw_out.at[at], row_o.at[k - 1, j], wy_send.at[k, j], wy_recv.at[k, j], {"row": y ^ k}
+        )
+
+    for j in far_first:
+        for k in others:
+            wy_copy(j, k).start()
+    for j in far_first:
+        for k in others:
+            fy_copy(2, j, k).start()
+    kv_load(len(others)).wait()
+    attend_block(y, len(others) % 2)
+
+    def back(r, first, second, at):
+        c, s = cos_ref[r, :], sin_ref[r, :]
+        graw[r, at : at + half] = (first * c + second * s).astype(low)
+        graw[r, at + half : at + 2 * half] = (second * c - first * s).astype(low)
+
+    def queries(r):
+        for h in range(heads):
+            at = h * HEAD_SIZE
+            back(r, dq[r, at : at + half], dq[r, at + half : at + 2 * half], at)
+
+    tiles(rows, 64, queries)
+    for k in others:
+
+        @pl.when((y ^ k) > y)
+        def _():
+            kv_copy(k).wait_recv()
+
+            def add(r):
+                dkv[r, :] = dkv[r, :] + dkv_in[k - 1, r, :].astype(wide)
+
+            tiles(rows, 64, add)
+
+    def keys_back(r):
+        back(r, dkv[r, 0:half], dkv[r, half : 2 * half], q_cols)
+        graw[r, q_cols + k_cols : all_cols] = dkv[r, k_cols : 2 * k_cols].astype(low)
+
+    tiles(rows, 64, keys_back)
+    loads[1].wait()
+    loads[2].wait()
+    f_row(1, 2)
+
+    def ay_copy(j, k):
+        at = pl.ds(pl.multiple_of(((z ^ j ^ col) * row_size + (y ^ k)) * local, local), local)
+        return remote(
+            dw_attn.at[at], row_a.at[k - 1, j], ay_send.at[k, j], ay_recv.at[k, j], {"row": y ^ k}
+        )
+
+    for p in range(4):
+        at = slice(p * width, (p + 1) * width)
+        for n in range(0, all_cols, 512):
+            dw_attn[at, n : n + 512] = contract_rows(xn[:, at], graw[:, n : n + 512]).astype(low)
+    fz_copy(1, 2).start()
+    for which in range(3):
+        t_copy(which).wait_send()
+    part = full
+    part_copy = remote(part.at[:, pl.ds(2 * width, 2 * width)], pcore_in, p_send, p_recv, core)
+    for q, p in ((2, 1), (3, 3)):
+        part[:, q * width : (q + 1) * width] = times_transposed(
+            graw[...], aw[p * width : (p + 1) * width, :]
+        ).astype(low)
+    for j in far_first:
+        for k in others:
+            ay_copy(j, k).start()
+    for q, p in ((0, 0), (1, 2)):
+        part[:, q * width : (q + 1) * width] = times_transposed(
+            graw[...], aw[p * width : (p + 1) * width, :]
+        ).astype(low)
+    part_copy.start()
+    f_row(1, 1)
+    f_row(1, 0)
+    part_copy.wait()
+    fz_copy(1, 1).start()
+    f_own(1).start()
+
+    def add_core(r):
+        px_out[r, :] = (
+            part[r, width : 2 * width].astype(wide) + pcore_in[r, width : 2 * width].astype(wide)
+        ).astype(low)
+
+    tiles(rows, 64, add_core)
+    out_far(2)
+    r_copy = remote(px_out, px_in, r_send, r_recv, far)
+    r_copy.start()
+    oz_copy(2).start()
+    out_far(1)
+
+    def wz_copy(j):
+        return remote(z_o.at[j - 1], in_o.at[j - 1], wz_send.at[j], wz_recv.at[j], {"dp": z ^ j})
+
+    def o_row(j):
+        for k in others:
+            wy_copy(j, k).wait_recv()
+        at = pl.ds(pl.multiple_of(((z ^ j ^ col) * row_size + y) * local, local), local)
+        total = dw_out[at, :].astype(wide)
+        for k in others:
+            total = total + row_o[k - 1, j].astype(wide)
+        if j:
+            z_o[j - 1] = total.astype(low)
+        else:
+            dwo_ref[...] = total
+
+    o_row(3)
+    oz_copy(1).start()
+    out_far(0)
+    o_row(2)
+    wz_copy(3).start()
+    o_row(1)
+    wz_copy(2).start()
+    o_row(0)
+    wz_copy(1).start()
+    r_copy.wait()
+
+    def dxn(r):
+        return (
+            part[r, 0:width].astype(wide) + pcore_in[r, 0:width].astype(wide) + px_in[r, :].astype(wide)
+        )
+
+    def inner_one(i, total):
+        r = pl.ds(pl.multiple_of(i * 64, 64), 64)
+        grad, tokens = dxn(r), tok_ref[r, :].astype(wide)
+        lanes[1, r, :] = lane_sums(gain_one * grad * tokens).astype(low)
+        return total + jnp.sum(grad * tokens * factor_one_ref[r, 0:1], axis=0, keepdims=True)
+
+    gain_one_grad = lax.fori_loop(0, rows // 64, inner_one, jnp.zeros((1, width), wide))
+    for i in range(row_size):
+        at = slice(i * local, (i + 1) * local)
+        gvec[i, 0:1, :] = gain_one_grad[:, at]
+        gvec[i, 1:2, :] = gain_two_grad[:, at]
+        gvec[i, 2:8, :] = jnp.zeros((6, local), wide)
+    f_row(2, 3)
+    for m in (2, 3, 1):
+        l_copy(1, m).start()
+    mine = z == col
+
+    def g_copy(k):
+        return remote(
+            gvec.at[y ^ k],
+            g_in.at[z * row_size + y],
+            g_send.at[k],
+            g_recv.at[z, k],
+            {"dp": col, "row": y ^ k},
+        )
+
+    for k in range(row_size):
+        if k:
+            g_copy(k).start()
+        else:
+
+            @pl.when(jnp.logical_not(mine))
+            def _():
+                g_copy(0).start()
+
+            @pl.when(mine)
+            def _():
+                g_in[z * row_size + y] = gvec[y]
+
+    fz_copy(2, 3).start()
+    f_row(2, 2)
+    f_row(2, 1)
+    fz_copy(2, 2).start()
+    f_row(2, 0)
+    fz_copy(2, 1).start()
+    f_own(2).start()
+    for m in (1, 2, 3):
+        l_copy(1, m).wait_recv()
+
+    def grad_tokens(r):
+        factor = factor_one_ref[r, 0:1]
+        dtok_ref[r, :] = (
+            dtok_ref[r, :].astype(wide)
+            + factor * gain_one * dxn(r)
+            - tok_ref[r, :].astype(wide) * factor * factor * factor * inner(1, r)
+        ).astype(low)
+
+    tiles(rows, 64, grad_tokens)
+
+    def az_copy(j):
+        return remote(z_a.at[j - 1], in_a.at[j - 1], az_send.at[j], az_recv.at[j], {"dp": z ^ j})
+
+    def a_row(j):
+        for k in others:
+            ay_copy(j, k).wait_recv()
+        at = pl.ds(pl.multiple_of(((z ^ j ^ col) * row_size + y) * local, local), local)
+        total = dw_attn[at, :].astype(wide)
+        for k in others:
+            total = total + row_a[k - 1, j].astype(wide)
+        if j:
+            z_a[j - 1] = total.astype(low)
+        else:
+            dattn_ref[...] = total
+
+    a_row(3)
+    a_row(2)
+    az_copy(3).start()
+    a_row(1)
+    az_copy(2).start()
+    a_row(0)
+    az_copy(1).start()
+
+    def gc_copy(m):
+        return remote(
+            gains_ref, gains_ref, gc_send.at[m - 1], gc_recv, {"col": col ^ m}
+        )
+
+    @pl.when(mine)
+    def _():
+        for j in range(4):
+            for k in range(row_size):
+                if j + k:
+                    block = g_in.at[(z ^ j) * row_size + (y ^ k)]
+                    remote(
+                        block, block, g_send.at[k], g_recv.at[z ^ j, k], {"dp": z ^ j, "row": y ^ k}
+                    ).wait_recv()
+        total = g_in[0]
+        for i in range(1, 4 * row_size):
+            total = total + g_in[i]
+        gains_ref[...] = total
+
+    for j in (1, 2, 3):
+        oz_copy(j).wait_recv()
+
+    @pl.when(mine)
+    def _():
+        for m in (1, 2, 3):
+            gc_copy(m).start()
+
+    def layer_out(r):
+        total = h_ref[r, :] + out_own[0, r, 0:width].astype(wide)
+        for j in (1, 2, 3):
+            total = total + z_in[j - 1, r, :].astype(wide)
+        layer_ref[r, :] = total.astype(low)
+
+    tiles(rows, 64, layer_out)
+    for j in (1, 2, 3):
+        wz_copy(j).wait_recv()
+        dwo_ref[...] = dwo_ref[...] + in_o[j - 1].astype(wide)
+    for a in range(3):
+        f_own(a).wait()
+        for j in (1, 2, 3):
+            at = pl.ds(pl.multiple_of((z ^ j) * hidden, hidden), hidden)
+            block = results[a].at[:, at]
+            remote(block, block, fz_send.at[a, j], fz_recv.at[a, j], {"dp": z ^ j}).wait_recv()
+    for j in (1, 2, 3):
+        az_copy(j).wait_recv()
+        dattn_ref[...] = dattn_ref[...] + in_a[j - 1].astype(wide)
+
+    @pl.when(jnp.logical_not(mine))
+    def _():
+        gc_copy(1).wait_recv()
+
+    @pl.when(mine)
+    def _():
+        for m in (1, 2, 3):
+            gc_copy(m).wait_send()
+
+    for k in range(row_size):
+        if k:
+            g_copy(k).wait_send()
+        else:
+
+            @pl.when(jnp.logical_not(mine))
+            def _():
+                g_copy(0).wait_send()
+
+    for n in (0, 1):
+        for m in (1, 2, 3):
+            l_copy(n, m).wait_send()
+    for j in range(4):
+        ox_copy(j).wait_send()
+        for which in (0, 1):
+            oc_copy(j, which).wait_send()
+        if j:
+            oz_copy(j).wait_send()
+            wz_copy(j).wait_send()
+            az_copy(j).wait_send()
+            for a in range(3):
+                fz_copy(a, j).wait_send()
+        for k in others:
+            wy_copy(j, k).wait_send()
+            ay_copy(j, k).wait_send()
+            for a in range(3):
+                fy_copy(a, j, k).wait_send()
+    when_block(row_size - 1, lambda: kv_copy(row_size - 1).wait_send())
+
+
+def attn_bwd_call(
+    dhn,
+    factor_two,
+    h,
+    dout,
+    gains,
+    tokens,
+    factor_one,
+    cos,
+    sin,
+    valid,
+    q,
+    lse,
+    mix,
+    xn,
+    kv,
+    aw,
+    wo,
+    out_part,
+    dwg,
+    dwu,
+    dwd,
+):
+    rows, width = tokens.shape
+    model, hidden = dwg.shape
+    low, wide = jnp.bfloat16, jnp.float32
+    row_size = lax.axis_size("row")
+    local = model // (4 * row_size)
+    all_cols, q_cols = aw.shape[1], wo.shape[1]
+    heads = q_cols // HEAD_SIZE
+    kv_cols = kv.shape[2]
+    vmem = pl.BlockSpec(memory_space=pltpu.VMEM)
+    hbm = pl.BlockSpec(memory_space=pl.ANY)
+    dma = pltpu.SemaphoreType.DMA
+    shape = jax.ShapeDtypeStruct
+    blocks = [part.reshape(4, row_size, local, hidden) for part in (dwg, dwu, dwd)]
+    return pl.pallas_call(
+        attn_bwd_kernel,
+        out_shape=(
+            shape((rows, width), low),
+            shape((rows, width), low),
+            shape((8, local), wide),
+            shape((local, all_cols), wide),
+            shape((local, q_cols), wide),
+            shape((local, 4 * hidden), low),
+            shape((local, 4 * hidden), low),
+            shape((local, 4 * hidden), low),
+        ),
+        in_specs=[vmem] * 13 + [hbm] * 8,
+        out_specs=(vmem,) * 5 + (hbm,) * 3,
+        scratch_shapes=[
+            pltpu.VMEM((rows, model), low),
+            pltpu.VMEM((rows, model), low),
+            pltpu.VMEM((2, rows, kv_cols), low),
+            pltpu.VMEM((model, all_cols), low),
+            pltpu.VMEM((model, q_cols), low),
+            pltpu.VMEM((2, rows, 128), low),
+            pltpu.VMEM((2, 3, rows, 128), low),
+            pltpu.VMEM((rows, q_cols), low),
+            pltpu.VMEM((heads, rows, 128), wide),
+            pltpu.VMEM((rows, q_cols), wide),
+            pltpu.VMEM((rows, kv_cols), wide),
+            pltpu.VMEM((rows, kv_cols), low),
+            pltpu.VMEM((row_size - 1, rows, kv_cols), low),
+            pltpu.VMEM((rows, all_cols), low),
+            pltpu.VMEM((model, all_cols), low),
+            pltpu.VMEM((model, q_cols), low),
+            pltpu.VMEM((3, 4, local, hidden), low),
+            pltpu.VMEM((3, row_size - 1, 4, local, hidden), low),
+            pltpu.VMEM((row_size - 1, 4, local, all_cols), low),
+            pltpu.VMEM((row_size - 1, 4, local, q_cols), low),
+            pltpu.VMEM((3, local, all_cols), low),
+            pltpu.VMEM((3, local, q_cols), low),
+            pltpu.VMEM((3, local, all_cols), low),
+            pltpu.VMEM((3, local, q_cols), low),
+            pltpu.VMEM((4, rows, 2 * width), low),
+            pltpu.VMEM((4, rows, 2 * width), low),
+            pltpu.VMEM((4, rows, width), low),
+            pltpu.VMEM((3, rows, width), low),
+            pltpu.VMEM((rows, 2 * width), low),
+            pltpu.VMEM((rows, width), low),
+            pltpu.VMEM((rows, width), low),
+            pltpu.VMEM((row_size, 8, local), wide),
+            pltpu.VMEM((4 * row_size, 8, local), wide),
+            dma((5,)),
+            dma((2, 3)),
+            dma((2, 3)),
+            dma((3,)),
+            dma((3,)),
+            dma((3, row_size, 4)),
+            dma((3, row_size, 4)),
+            dma((3, 4)),
+            dma((3, 4)),
+            dma((3, 4)),
+            dma((2, 4)),
+            dma((2, 4)),
+            dma((2, 4)),
+            dma((4,)),
+            dma((4,)),
+            dma((4,)),
+            dma((4,)),
+            dma((row_size,)),
+            dma((row_size,)),
+            dma((row_size, 4)),
+            dma((row_size, 4)),
+            dma((4,)),
+            dma((4,)),
+            dma((row_size, 4)),
+            dma((row_size, 4)),
+            dma((4,)),
+            dma((4,)),
+            dma(()),
+            dma(()),
+            dma(()),
+            dma(()),
+            dma((row_size,)),
+            dma((4, row_size)),
+            dma((3,)),
+            dma(()),
+        ],
+        compiler_params=pltpu.CompilerParams(
+            collective_id=3, has_side_effects=True, vmem_limit_bytes=66_000_000
+        ),
+        cost_estimate=pl.CostEstimate(
+            flops=14_000_000_000, bytes_accessed=40_000_000, transcendentals=2_000_000
+        ),
+    )(
+        dhn,
+        factor_two,
+        h,
+        dout,
+        gains,
+        tokens,
+        factor_one,
+        cos,
+        sin,
+        valid,
+        q,
+        lse,
+        mix,
+        xn,
+        kv,
+        aw,
+        wo,
+        out_part,
+        *blocks,
+    )
+
+
 def per_device(
     tokens,
     w_query,
@@ -1323,14 +1907,8 @@
 ):
     low = jnp.bfloat16
     wide = jnp.float32
-    row_count, col_width = tokens.shape
-    model_width = col_width * 4
-    slot_size = row_count * lax.axis_size("row")
-    key_block = min(512, slot_size)
-    query_group = QUERY_HEADS // KEY_VALUE_HEADS
-    score_scale = 1.0 / math.sqrt(HEAD_SIZE)
-    me_dp, me_row, me_col = (lax.axis_index(name) for name in ("dp", "row", "col"))
-    shift = me_dp ^ me_col
+    row_count = tokens.shape[0]
+    me_row = lax.axis_index("row")
     query_pos = me_row * row_count + jnp.arange(row_count, dtype=jnp.int32)
     valid = (query_pos < lengths[0]).astype(wide)[:, None]
     cosine_table, sine_table = rope_tables(query_pos.astype(wide))
@@ -1338,7 +1916,6 @@
     gains = jnp.zeros((8, gain_attn.shape[0]), wide)
     gains = gains.at[0].set(gain_attn.astype(wide)).at[1].set(gain_ffn.astype(wide))
     q_cols, k_cols = w_query.shape[1], key_matrix.shape[1]
-    kv_heads = k_cols // HEAD_SIZE
     grad_out = (cotangent.astype(wide) * valid).astype(low)
     (
         normed,
@@ -1370,106 +1947,42 @@
         w_up,
         w_down.T,
     )
-    factor_one = factor_one[:, :1]
-    gain_one, gain_two = gains[0], gains[1]
-    query_rows = query_rows.reshape(kv_heads, query_group, row_count, HEAD_SIZE)
-    log_total = log_total[:, :, 0].reshape(kv_heads, query_group, row_count)
-    attended = (
-        mixed_heads.astype(wide)
-        .reshape(row_count, kv_heads, query_group, HEAD_SIZE)
-        .transpose(1, 2, 0, 3)
-    )
-    keys_all = kv_all[:, :, :k_cols].reshape(slot_size, kv_heads, HEAD_SIZE)
-    values_all = kv_all[:, :, k_cols:].reshape(slot_size, kv_heads, HEAD_SIZE)
-    seen = (jnp.arange(slot_size) < (me_row + 1) * row_count)[:, None, None]
-    keys_all = jnp.where(seen, keys_all, 0)
-    values_all = jnp.where(seen, values_all, 0)
-
     residual_low = residual.astype(low)
     grad_normed_two, factor_two, out_part, grad_gate_part, grad_up_part, grad_down_part = ffn_call(
         residual_low, gains[1:2], grad_out_full, gate_weight, up_weight, down_weight
     )
-    layer_out = (residual + scatter_tokens(out_part.reshape(-1, model_width))).astype(low)
-    own_gain_two = gain_two[:col_width]
-    own_factor_two = factor_two[:, :1]
-    own_residual = residual_low.astype(wide)
-    scaled = own_gain_two * grad_normed_two
-    inner = col_sum(jnp.sum(scaled * own_residual, axis=1)[:, None]) / model_width
-    grad_residual = (
-        grad_out.astype(wide)
-        + own_factor_two * scaled
-        - own_residual * own_factor_two * own_factor_two * own_factor_two * inner
-    ).astype(low)
-    gain_two_grad = jnp.sum(grad_normed_two * own_residual * own_factor_two, axis=0)
-
-    grad_residual_full = gather_col(grad_residual)
-    grad_output_part = contract_rows(grad_residual_full, mixed_heads)
-    grad_mixed = (
-        jnp.dot(grad_residual_full, out_weight, preferred_element_type=wide) * valid
-    ).astype(low)
-    grad_heads = grad_mixed.reshape(row_count, kv_heads, query_group, HEAD_SIZE).transpose(
-        1, 2, 0, 3
+    (
+        layer_out,
+        grad_tokens,
+        gain_grads,
+        grad_attn,
+        grad_output,
+        grad_gate,
+        grad_up,
+        grad_down,
+    ) = attn_bwd_call(
+        grad_normed_two,
+        factor_two,
+        residual,
+        grad_out,
+        gains,
+        tokens,
+        factor_one,
+        cosine_table,
+        sine_table,
+        valid,
+        query_rows,
+        log_total,
+        mixed_heads,
+        normed,
+        kv_all,
+        attn_weight,
+        out_weight,
+        out_part,
+        grad_gate_part,
+        grad_up_part,
+        grad_down_part,
     )
-    delta = jnp.sum(grad_heads.astype(wide) * attended, axis=-1)
-    grad_query_rot, grad_keys_all, grad_values_all = attend_back(
-        query_rows,
-        keys_all,
-        values_all,
-        query_pos,
-        key_block,
-        score_scale,
-        log_total,
-        delta,
-        grad_heads,
-    )
-    grad_kv = scatter_row(
-        jnp.concatenate([grad_keys_all, grad_values_all], axis=1).reshape(
-            slot_size // row_count, row_count, 2 * k_cols
-        ),
-        0,
-    )
-    grad_query_raw = (
-        rotate_back(
-            grad_query_rot.transpose(2, 0, 1, 3).reshape(
-                row_count, kv_heads * query_group, HEAD_SIZE
-            ),
-            cosine_table,
-            sine_table,
-        )
-        .reshape(row_count, q_cols)
-        .astype(low)
-    )
-    grad_key_raw = (
-        rotate_back(
-            grad_kv[:, :k_cols].reshape(row_count, kv_heads, HEAD_SIZE), cosine_table, sine_table
-        )
-        .reshape(row_count, k_cols)
-        .astype(low)
-    )
-    grad_raw = jnp.concatenate([grad_query_raw, grad_key_raw, grad_kv[:, k_cols:].astype(low)], axis=1)
-    grad_attn_part = contract_rows(normed, grad_raw)
-    grad_normed = scatter_col(times_transposed(grad_raw, attn_weight))
-    own_gain_one = gain_one[:col_width]
-    own_tokens = tokens.astype(wide)
-    scaled = own_gain_one * grad_normed
-    inner = col_sum(jnp.sum(scaled * own_tokens, axis=1)[:, None]) / model_width
-    grad_tokens = (
-        grad_residual.astype(wide)
-        + factor_one * scaled
-        - own_tokens * factor_one * factor_one * factor_one * inner
-    ).astype(low)
-    gain_one_grad = jnp.sum(grad_normed * own_tokens * factor_one, axis=0)
-
-    gain_grads = jnp.zeros((2, model_width), wide)
-    gain_grads = lax.dynamic_update_slice(
-        gain_grads, jnp.stack([gain_one_grad, gain_two_grad]), (0, me_col * col_width)
-    )
-    gain_grads = lax.psum(gain_grads, ("dp", "row", "col"))
-    own = gain_attn.shape[0]
-    gain_grads = lax.dynamic_slice_in_dim(
-        gain_grads, (me_dp * lax.axis_size("row") + me_row) * own, own, 1
-    )
-    grad_attn = sum_weight(grad_attn_part, shift)
     return (
         layer_out,
         grad_tokens,
@@ -1478,10 +1991,10 @@
         grad_attn[:, :q_cols],
         grad_attn[:, q_cols : q_cols + k_cols],
         grad_attn[:, q_cols + k_cols :],
-        sum_weight(grad_output_part, shift).T,
-        return_weight(grad_gate_part, shift),
-        return_weight(grad_up_part, shift),
-        return_weight(grad_down_part, shift).T,
+        grad_output.T,
+        grad_gate.astype(wide),
+        grad_up.astype(wide),
+        grad_down.T.astype(wide),
     )
 
 

time: 759 us -> 565 us (0.74); the launches traced: 748 us -> 564 us
  Pallas kernels: 329 us -> 537 us
  waiting for transfers between devices: 158 us -> 0 us
  blocking collectives: 69.8 us -> 0 us
  other arithmetic: 57.9 us -> 10.6 us
  local copies, waits for them, and re-layouts: 59.3 us -> 15 us
  starting transfers between devices: 43.3 us -> 0 us
  matrix products: 26.3 us -> 0 us
    pallas_call x0 -> x1, Pallas kernels: none -> 208 us  [attn_bwd_call(): pl.pallas_call(attn_bwd_kernel, out_shape=(shape((rows, width), low), sha...]
    ppermute x34 -> x0, waiting for transfers between devices: 158 us -> none  [swap(): return lax.ppermute(value, axis, [(i, i ^ bit) for i in range(size)])]
    psum x1 -> x0, blocking collectives: 69.8 us -> none  [per_device(): gain_grads = lax.psum(gain_grads, ('dp', 'row', 'col'))]
    ppermute x34 -> x0, starting transfers between devices: 43.3 us -> none  [swap(): return lax.ppermute(value, axis, [(i, i ^ bit) for i in range(size)])]
    dot_general x14 -> x0, matrix products: 26.3 us -> none  [the longest x2 5.43 us: step(): jnp.einsum('hgqk,khd->hgqd', grad_scores, key_part, preferred_element_typ...]
    convert_element_type x14 -> x3, other arithmetic: 22.2 us -> 3.35 us  [the longest x1 1.56 us: per_device(): grad_gate.astype(wide)]
    dynamic_slice x9 -> x0, local copies, waits for them, and re-layouts: 17.6 us -> none  [the longest x4 9.41 us: scatter_row(): mine = lax.dynamic_index_in_dim(value, me, axis, keepdims=False)]
    unnamed x83 -> x22, local copies, waits for them, and re-layouts: 23.4 us -> 8.68 us
  transfers between devices with their start and end apart: 34 -> 0, of which waited for: 14 -> 0; matrix products, arithmetic and copies ran while one was open for 16% -> 0% of each run, Pallas kernels for 0% -> 0%
where the time goes in v4:
time: 565 us; the launch traced here: 564 us
  Pallas kernels  537 us (95%)
  local copies, waits for them, and re-layouts  15 us (3%)
  other arithmetic  10.6 us (2%)
    pallas_call x1, Pallas kernels, attn_bwd_call(): pl.pallas_call(attn_bwd_kernel, out_shape=(shape((rows, width), low), sha...  208 us
    pallas_call x1, Pallas kernels, attn_fwd_call(): pl.pallas_call(attn_fwd_kernel, out_shape=(shape((rows, model), low), sha...  183 us
    pallas_call x1, Pallas kernels, ffn_call(): pl.pallas_call(ffn_kernel, out_shape=(jax.ShapeDtypeStruct((rows, width),...  146 us

profile of v4, /device:TPU:0, one launch (start us, length us, event | category | flops | bytes accessed | tf_op | source)
XLA Modules:
  0.0 564.0 jit_solution(10391428200880939780)
XLA Ops:
  0.6 0.0 copy-start.3
  1.4 0.7 reshape.108
  2.1 0.7 convert.8
  2.8 0.0 copy-start.7
  2.8 0.7 fusion.valid_ref
  3.5 1.8 copy.23
  5.3 1.8 multiply_sine_fusion
  7.1 2.0 multiply_convert_fusion.cot_ref.dout_ref
  9.1 0.0 copy-done.3
  9.1 1.4 copy.24
  10.6 0.0 copy-done.7
  10.6 183.2 %shard_map.203 = (bf16[512,2048]{1,0:T(8,128)(2,1)}, f32[512,128]{1,0:T(8,128)}, bf16[2,512,256]{2,1,0:T(8,128)(2,1)}, bf16[2,512,512]{2,1,0:T(8,128)(2,1)}, f32...) custom-call(bf16[512,512]{1,0:T(8,128)(2,1)} %tok_ref.3, ...), custom_call_target="tpu_custom_call" | custom-call | flops 10000000000 | bytes 40000000 | tf_op jit(solution)/shard_map/pallas_call | solution.py:998
  193.7 1.4 slice.47.gain_ref
  195.2 2.1 convert_element_type.48.h_ref
  197.3 146.0 %shard_map.204 = (f32[512,512]{1,0:T(8,128)}, f32[512,128]{1,0:T(8,128)}, bf16[4,512,2048]{2,1,0:T(8,128)(2,1)}, bf16[2048,512]{1,0:T(8,128)(2,1)}, bf16[2048,51...) custom-call(bf16[512,512]{1,0:T(8,128)(2,1)} %convert_element_type.48.h_ref, f32[1,2048]{1,0:T(1,128)} %slice.47.gain_ref, ...), custom_call_target="tpu_custom_call" | custom-call | flops 38654705664 | bytes 40000000 | tf_op jit(solution)/shard_map/pallas_call | solution.py:419
  343.3 207.8 %shard_map.205 = (bf16[512,512]{1,0:T(8,128)(2,1)}, bf16[512,512]{1,0:T(8,128)(2,1)}, f32[8,256]{1,0:T(8,128)}, f32[256,1024]{1,0:T(8,128)}, f32[256,512]{1,0:T(...) custom-call(f32[512,512]{1,0:T(8,128)} %get-tuple-element.69.dhn_ref, ...), custom_call_target="tpu_custom_call" | custom-call | flops 14000000000 | bytes 40000000 | tf_op jit(solution)/shard_map/pallas_call | solution.py:1781
  551.0 0.0 copy-start.4
  551.1 0.0 copy-start.2
  551.1 1.4 fusion.5
  552.5 2.0 copy.25
  554.5 1.9 slice.50
  556.4 0.0 copy-done.4
  556.4 0.0 copy-start.1
  556.4 0.8 fusion.4
  557.2 0.0 copy-done.2
  557.2 1.6 convert_element_type.49
  558.8 0.0 copy-done.1
  558.8 0.0 copy-start
  558.8 1.6 convert_element_type.50
  560.4 0.0 copy-done
  560.4 0.2 convert_bitcast_fusion
  560.6 0.0 copy-start.6
  560.6 0.0 copy-start.5
  560.6 1.8 copy.26
  562.4 0.0 copy-done.6
  562.4 0.8 copy.31
  563.2 0.0 copy-done.5
  563.2 0.8 copy.32
  (5 shorter events, 0.1 us)
Async XLA Ops:
  0.6 8.5 %copy-start.3 = (bf16[2048,256]{1,0:T(8,128)(2,1)S(1)}, bf16[2048,256]{1,0:T(8,128)(2,1)}, u32[]{:S(2)}) copy-start(bf16[2048,256]{1,0:T(8,128)(2,1)} %param.23) | copy-start | bytes 3145732
  2.8 7.8 %copy-start.7 = (f32[8,256]{1,0:T(8,128)}, f32[8,256]{1,0:T(8,128)S(1)}, u32[]{:S(2)}) copy-start(f32[8,256]{1,0:T(8,128)S(1)} %scatter.14.gains_ref) | copy-start | bytes 24580
  551.0 5.4 copy-start.4
  551.1 6.2 %copy-start.2 = (bf16[256,2048]{1,0:T(8,128)(2,1)S(1)}, bf16[256,2048]{1,0:T(8,128)(2,1)}, u32[]{:S(2)}) copy-start(bf16[256,2048]{1,0:T(8,128)(2,1)} %get-tuple-element.88) | copy-start | bytes 3145732
  556.4 2.4 copy-start.1
  558.8 1.6 copy-start
  560.6 1.8 copy-start.6
  560.6 2.6 copy-start.5

commit v5 on v4

--- a/solution.py
+++ b/solution.py
@@ -1060,6 +1060,52 @@
             flops=10_000_000_000, bytes_accessed=40_000_000, transcendentals=2_000_000
         ),
     )(tokens, cot, gains, cos, sin, valid, wq, wk, wv, wo, wg, wu, wd)
+
+
+class Reduce:
+    def __init__(self, z, mid, block, inbox, send, recv):
+        self.z, self.mid, self.block, self.inbox = z, mid, block, inbox
+        self.send, self.recv = send, recv
+
+    def copy(self, j):
+        owner = self.z ^ j
+        above = owner > self.z
+        target = jnp.where(above, self.z + 1, self.z - 1)
+        slot = jnp.where(target == owner, jnp.where(above, 3, 4), (target ^ owner) - 1)
+        return remote(
+            self.block(j), self.inbox.at[slot], self.send.at[j], self.recv.at[slot], {"dp": target}
+        )
+
+    def arrived(self, slot):
+        block = self.inbox.at[slot]
+        remote(block, block, self.send.at[0], self.recv.at[slot], {"dp": self.z ^ 1}).wait_recv()
+
+    def first(self, j):
+        @pl.when(jnp.logical_not(self.mid))
+        def _():
+            self.copy(j).start()
+
+    def relay(self, j, add):
+        @pl.when(self.mid)
+        def _():
+            self.arrived(j - 1)
+            add(j)
+            self.copy(j).start()
+
+    def finish(self, add):
+        @pl.when(self.z > 0)
+        def _():
+            self.arrived(3)
+            add(3)
+
+        @pl.when(self.z < 3)
+        def _():
+            self.arrived(4)
+            add(4)
+
+    def drain(self):
+        for j in (1, 2, 3):
+            self.copy(j).wait_send()
 
 
 def lane_sums(value):
@@ -1183,6 +1229,10 @@
     z, y, col = (lax.axis_index(name) for name in ("dp", "row", "col"))
     core, far = {"col": col ^ 1}, {"col": col ^ 2}
     others = range(1, row_size)
+    mid = jnp.logical_and(z > 0, z < 3)
+    third = jnp.where(mid, 2, 3)
+    second = jnp.where(mid, 3, 2)
+    by_distance = (third, second, 1, 0)
     partials = (dwg_hbm, dwu_hbm, dwd_hbm)
     results = (gg_ref, gu_ref, gd_ref)
 
@@ -1244,7 +1294,7 @@
         lanes[0, r, :] = lane_sums(gain_two * dhn_ref[r, :] * residual(r)).astype(low)
 
     tiles(rows, 64, inner_two)
-    for j in far_first:
+    for j in by_distance:
         for which in (0, 1):
             oc_copy(j, which).start()
             oo_copy(j, which).start()
@@ -1316,15 +1366,20 @@
 
         tiles(rows, 64, add)
 
-    out_core(3)
+    out_core(third)
     t_copy(1).start()
     t_copy(0).start()
-    ox_copy(3).start()
-
-    def oz_copy(j):
-        return remote(
-            out_own.at[j, :, cols(0)], z_in.at[j - 1], oz_send.at[j], oz_recv.at[j], {"dp": z ^ j}
-        )
+    ox_copy(third).start()
+
+    outs = Reduce(z, mid, lambda j: out_own.at[j, :, cols(0)], z_in, oz_send, oz_recv)
+
+    def out_add(j):
+        def add(r):
+            out_own[j, r, 0:width] = (
+                out_own[j, r, 0:width].astype(wide) + z_in[j - 1, r, :].astype(wide)
+            ).astype(low)
+
+        tiles(rows, 64, add)
 
     def out_far(j):
         ox_copy(j).wait_recv()
@@ -1355,9 +1410,9 @@
             total = total + row_f[a, k - 1, j].astype(wide)
         own_f[a, j] = total.astype(low)
 
-    out_core(2)
+    out_core(second)
     f_row(0, 3)
-    ox_copy(2).start()
+    ox_copy(second).start()
     out_core(1)
     fz_copy(0, 3).start()
     ox_copy(1).start()
@@ -1447,9 +1502,9 @@
 
     fz_copy(0, 1).start()
     f_own(0).start()
-    out_far(3)
+    out_far(third)
     f_row(1, 3)
-    oz_copy(3).start()
+    outs.first(third)
     fz_copy(1, 3).start()
 
     def wy_copy(j, k):
@@ -1458,13 +1513,16 @@
             dw_out.at[at], row_o.at[k - 1, j], wy_send.at[k, j], wy_recv.at[k, j], {"row": y ^ k}
         )
 
-    for j in far_first:
+    for j in by_distance:
         for k in others:
             wy_copy(j, k).start()
     for j in far_first:
         for k in others:
             fy_copy(2, j, k).start()
     kv_load(len(others)).wait()
+    out_far(second)
+    outs.first(second)
+    outs.relay(third, out_add)
     attend_block(y, len(others) % 2)
 
     def back(r, first, second, at):
@@ -1517,7 +1575,7 @@
         part[:, q * width : (q + 1) * width] = times_transposed(
             graw[...], aw[p * width : (p + 1) * width, :]
         ).astype(low)
-    for j in far_first:
+    for j in by_distance:
         for k in others:
             ay_copy(j, k).start()
     for q, p in ((0, 0), (1, 2)):
@@ -1537,14 +1595,21 @@
         ).astype(low)
 
     tiles(rows, 64, add_core)
-    out_far(2)
+    out_far(1)
     r_copy = remote(px_out, px_in, r_send, r_recv, far)
     r_copy.start()
-    oz_copy(2).start()
-    out_far(1)
-
-    def wz_copy(j):
-        return remote(z_o.at[j - 1], in_o.at[j - 1], wz_send.at[j], wz_recv.at[j], {"dp": z ^ j})
+    outs.first(1)
+    outs.relay(second, out_add)
+
+    outw = Reduce(z, mid, lambda j: z_o.at[j - 1], in_o, wz_send, wz_recv)
+
+    def o_add(j):
+        def add(r):
+            z_o[j - 1, r, :] = (
+                z_o[j - 1, r, :].astype(wide) + in_o[j - 1, r, :].astype(wide)
+            ).astype(low)
+
+        tiles(local, 32, add)
 
     def o_row(j):
         for k in others:
@@ -1553,20 +1618,20 @@
         total = dw_out[at, :].astype(wide)
         for k in others:
             total = total + row_o[k - 1, j].astype(wide)
-        if j:
+        if isinstance(j, int) and j == 0:
+            dwo_ref[...] = total
+        else:
             z_o[j - 1] = total.astype(low)
-        else:
-            dwo_ref[...] = total
-
-    o_row(3)
-    oz_copy(1).start()
+
+    o_row(third)
     out_far(0)
-    o_row(2)
-    wz_copy(3).start()
+    outw.first(third)
+    outs.relay(1, out_add)
+    o_row(second)
     o_row(1)
-    wz_copy(2).start()
+    outw.first(second)
     o_row(0)
-    wz_copy(1).start()
+    outw.first(1)
     r_copy.wait()
 
     def dxn(r):
@@ -1614,12 +1679,15 @@
                 g_in[z * row_size + y] = gvec[y]
 
     fz_copy(2, 3).start()
+    outw.relay(third, o_add)
     f_row(2, 2)
     f_row(2, 1)
     fz_copy(2, 2).start()
+    outw.relay(second, o_add)
     f_row(2, 0)
     fz_copy(2, 1).start()
     f_own(2).start()
+    outw.relay(1, o_add)
     for m in (1, 2, 3):
         l_copy(1, m).wait_recv()
 
@@ -1633,8 +1701,15 @@
 
     tiles(rows, 64, grad_tokens)
 
-    def az_copy(j):
-        return remote(z_a.at[j - 1], in_a.at[j - 1], az_send.at[j], az_recv.at[j], {"dp": z ^ j})
+    attn = Reduce(z, mid, lambda j: z_a.at[j - 1], in_a, az_send, az_recv)
+
+    def a_add(j):
+        def add(r):
+            z_a[j - 1, r, :] = (
+                z_a[j - 1, r, :].astype(wide) + in_a[j - 1, r, :].astype(wide)
+            ).astype(low)
+
+        tiles(local, 32, add)
 
     def a_row(j):
         for k in others:
@@ -1643,18 +1718,21 @@
         total = dw_attn[at, :].astype(wide)
         for k in others:
             total = total + row_a[k - 1, j].astype(wide)
-        if j:
+        if isinstance(j, int) and j == 0:
+            dattn_ref[...] = total
+        else:
             z_a[j - 1] = total.astype(low)
-        else:
-            dattn_ref[...] = total
-
-    a_row(3)
-    a_row(2)
-    az_copy(3).start()
+
+    a_row(third)
+    a_row(second)
+    attn.first(third)
     a_row(1)
-    az_copy(2).start()
+    attn.first(second)
     a_row(0)
-    az_copy(1).start()
+    attn.first(1)
+    attn.relay(third, a_add)
+    attn.relay(second, a_add)
+    attn.relay(1, a_add)
 
     def gc_copy(m):
         return remote(
@@ -1675,33 +1753,44 @@
             total = total + g_in[i]
         gains_ref[...] = total
 
-    for j in (1, 2, 3):
-        oz_copy(j).wait_recv()
-
     @pl.when(mine)
     def _():
         for m in (1, 2, 3):
             gc_copy(m).start()
 
+    for slot in (3, 4):
+
+        @pl.when((z > 0) if slot == 3 else (z < 3))
+        def _():
+            outs.arrived(slot)
+
+        @pl.when((z == 0) if slot == 3 else (z == 3))
+        def _():
+            z_in[slot] = jnp.zeros((rows, width), low)
+
     def layer_out(r):
         total = h_ref[r, :] + out_own[0, r, 0:width].astype(wide)
-        for j in (1, 2, 3):
-            total = total + z_in[j - 1, r, :].astype(wide)
+        for slot in (3, 4):
+            total = total + z_in[slot, r, :].astype(wide)
         layer_ref[r, :] = total.astype(low)
 
     tiles(rows, 64, layer_out)
-    for j in (1, 2, 3):
-        wz_copy(j).wait_recv()
-        dwo_ref[...] = dwo_ref[...] + in_o[j - 1].astype(wide)
+
+    def o_last(slot):
+        dwo_ref[...] = dwo_ref[...] + in_o[slot].astype(wide)
+
+    outw.finish(o_last)
     for a in range(3):
         f_own(a).wait()
         for j in (1, 2, 3):
             at = pl.ds(pl.multiple_of((z ^ j) * hidden, hidden), hidden)
             block = results[a].at[:, at]
             remote(block, block, fz_send.at[a, j], fz_recv.at[a, j], {"dp": z ^ j}).wait_recv()
-    for j in (1, 2, 3):
-        az_copy(j).wait_recv()
-        dattn_ref[...] = dattn_ref[...] + in_a[j - 1].astype(wide)
+
+    def a_last(slot):
+        dattn_ref[...] = dattn_ref[...] + in_a[slot].astype(wide)
+
+    attn.finish(a_last)
 
     @pl.when(jnp.logical_not(mine))
     def _():
@@ -1724,14 +1813,13 @@
     for n in (0, 1):
         for m in (1, 2, 3):
             l_copy(n, m).wait_send()
+    for summed in (outs, outw, attn):
+        summed.drain()
     for j in range(4):
         ox_copy(j).wait_send()
         for which in (0, 1):
             oc_copy(j, which).wait_send()
         if j:
-            oz_copy(j).wait_send()
-            wz_copy(j).wait_send()
-            az_copy(j).wait_send()
             for a in range(3):
                 fz_copy(a, j).wait_send()
         for k in others:
@@ -1815,12 +1903,12 @@
             pltpu.VMEM((row_size - 1, 4, local, q_cols), low),
             pltpu.VMEM((3, local, all_cols), low),
             pltpu.VMEM((3, local, q_cols), low),
-            pltpu.VMEM((3, local, all_cols), low),
-            pltpu.VMEM((3, local, q_cols), low),
+            pltpu.VMEM((5, local, all_cols), low),
+            pltpu.VMEM((5, local, q_cols), low),
             pltpu.VMEM((4, rows, 2 * width), low),
             pltpu.VMEM((4, rows, 2 * width), low),
             pltpu.VMEM((4, rows, width), low),
-            pltpu.VMEM((3, rows, width), low),
+            pltpu.VMEM((5, rows, width), low),
             pltpu.VMEM((rows, 2 * width), low),
             pltpu.VMEM((rows, width), low),
             pltpu.VMEM((rows, width), low),
@@ -1842,17 +1930,17 @@
             dma((4,)),
             dma((4,)),
             dma((4,)),
-            dma((4,)),
+            dma((5,)),
             dma((row_size,)),
             dma((row_size,)),
             dma((row_size, 4)),
             dma((row_size, 4)),
             dma((4,)),
-            dma((4,)),
+            dma((5,)),
             dma((row_size, 4)),
             dma((row_size, 4)),
             dma((4,)),
-            dma((4,)),
+            dma((5,)),
             dma(()),
             dma(()),
             dma(()),

time: 565 us -> 538 us (0.952)
  Pallas kernels: 537 us -> 511 us
    pallas_call x1, Pallas kernels: 208 us -> 182 us  [attn_bwd_call(): pl.pallas_call(attn_bwd_kernel, out_shape=(shape((rows, width), low), sha...]
where the time goes in v5:
time: 538 us
  Pallas kernels  511 us (95%)
  local copies, waits for them, and re-layouts  15 us (3%)
  other arithmetic  10.6 us (2%)
    pallas_call x1, Pallas kernels, attn_fwd_call(): pl.pallas_call(attn_fwd_kernel, out_shape=(shape((rows, model), low), sha...  183 us
    pallas_call x1, Pallas kernels, attn_bwd_call(): pl.pallas_call(attn_bwd_kernel, out_shape=(shape((rows, width), low), sha...  182 us
    pallas_call x1, Pallas kernels, ffn_call(): pl.pallas_call(ffn_kernel, out_shape=(jax.ShapeDtypeStruct((rows, width),...  146 us

profile of v5, /device:TPU:0, one launch (start us, length us, event | category | flops | bytes accessed | tf_op | source)
XLA Modules:
  0.0 537.9 jit_solution(2142489805553368026)
XLA Ops:
  0.6 0.0 copy-start.3
  1.4 0.7 reshape.108
  2.1 0.7 convert.8
  2.8 0.0 copy-start.7
  2.8 0.7 fusion.valid_ref
  3.5 1.8 copy.23
  5.3 1.8 multiply_sine_fusion
  7.1 2.0 multiply_convert_fusion.cot_ref.dout_ref
  9.1 0.0 copy-done.3
  9.1 1.4 copy.24
  10.6 0.0 copy-done.7
  10.6 183.2 %shard_map.203 = (bf16[512,2048]{1,0:T(8,128)(2,1)}, f32[512,128]{1,0:T(8,128)}, bf16[2,512,256]{2,1,0:T(8,128)(2,1)}, bf16[2,512,512]{2,1,0:T(8,128)(2,1)}, f32...) custom-call(bf16[512,512]{1,0:T(8,128)(2,1)} %tok_ref.3, ...), custom_call_target="tpu_custom_call" | custom-call | flops 10000000000 | bytes 40000000 | tf_op jit(solution)/shard_map/pallas_call | solution.py:998
  193.7 1.4 slice.47.gain_ref
  195.2 2.1 convert_element_type.48.h_ref
  197.3 146.0 %shard_map.204 = (f32[512,512]{1,0:T(8,128)}, f32[512,128]{1,0:T(8,128)}, bf16[4,512,2048]{2,1,0:T(8,128)(2,1)}, bf16[2048,512]{1,0:T(8,128)(2,1)}, bf16[2048,51...) custom-call(bf16[512,512]{1,0:T(8,128)(2,1)} %convert_element_type.48.h_ref, f32[1,2048]{1,0:T(1,128)} %slice.47.gain_ref, ...), custom_call_target="tpu_custom_call" | custom-call | flops 38654705664 | bytes 40000000 | tf_op jit(solution)/shard_map/pallas_call | solution.py:419
  343.3 181.6 %shard_map.205 = (bf16[512,512]{1,0:T(8,128)(2,1)}, bf16[512,512]{1,0:T(8,128)(2,1)}, f32[8,256]{1,0:T(8,128)}, f32[256,1024]{1,0:T(8,128)}, f32[256,512]{1,0:T(...) custom-call(f32[512,512]{1,0:T(8,128)} %get-tuple-element.69.dhn_ref, ...), custom_call_target="tpu_custom_call" | custom-call | flops 14000000000 | bytes 40000000 | tf_op jit(solution)/shard_map/pallas_call | solution.py:1869
  524.9 0.0 copy-start.4
  524.9 0.0 copy-start.2
  524.9 1.4 fusion.5
  526.3 2.0 copy.25
  528.4 1.9 slice.50
  530.2 0.0 copy-done.4
  530.2 0.0 copy-start.1
  530.2 0.8 fusion.4
  531.1 0.0 copy-done.2
  531.1 1.6 convert_element_type.49
  532.6 0.0 copy-done.1
  532.6 0.0 copy-start
  532.6 1.6 convert_element_type.50
  534.2 0.0 copy-done
  534.2 0.2 convert_bitcast_fusion
  534.4 0.0 copy-start.6
  534.4 0.0 copy-start.5
  534.5 1.8 copy.26
  536.3 0.0 copy-done.6
  536.3 0.8 copy.31
  537.1 0.0 copy-done.5
  537.1 0.8 copy.32
  (5 shorter events, 0.1 us)
Async XLA Ops:
  0.6 8.5 %copy-start.3 = (bf16[2048,256]{1,0:T(8,128)(2,1)S(1)}, bf16[2048,256]{1,0:T(8,128)(2,1)}, u32[]{:S(2)}) copy-start(bf16[2048,256]{1,0:T(8,128)(2,1)} %param.23) | copy-start | bytes 3145732
  2.8 7.8 %copy-start.7 = (f32[8,256]{1,0:T(8,128)}, f32[8,256]{1,0:T(8,128)S(1)}, u32[]{:S(2)}) copy-start(f32[8,256]{1,0:T(8,128)S(1)} %scatter.14.gains_ref) | copy-start | bytes 24580
  524.9 5.4 copy-start.4
  524.9 6.2 %copy-start.2 = (bf16[256,2048]{1,0:T(8,128)(2,1)S(1)}, bf16[256,2048]{1,0:T(8,128)(2,1)}, u32[]{:S(2)}) copy-start(bf16[256,2048]{1,0:T(8,128)(2,1)} %get-tuple-element.88) | copy-start | bytes 3145732
  530.2 2.4 copy-start.1
  532.6 1.6 copy-start
  534.4 1.8 copy-start.6
  534.4 2.6 copy-start.5

commit v6 on v5

--- a/solution.py
+++ b/solution.py
@@ -280,7 +280,7 @@
         def norm(r):
             x = full[j, r, :].astype(wide)
             factor = lax.rsqrt(jnp.sum(x * x, axis=1, keepdims=True) * (1.0 / model) + EPSILON)
-            full[j, r, :] = (x * factor * gain_ref[...]).astype(low)
+            full[j, r, :] = (x * factor * gain_ref[1:2, :]).astype(low)
 
             @pl.when(s == 0)
             def _():
@@ -528,7 +528,7 @@
 
 def attn_fwd_kernel(
     tok_ref,
-    cot_ref,
+    cot_in_ref,
     gains_ref,
     cos_ref,
     sin_ref,
@@ -540,20 +540,26 @@
     wg_hbm,
     wu_hbm,
     wd_hbm,
-    xn_ref,
     factor_ref,
     q_ref,
     kv_ref,
     lse_ref,
     mix_ref,
     h_ref,
-    aw_ref,
-    wo_ref,
+    hlow_ref,
     gain_ref,
+    xn_hbm,
+    aw_hbm,
+    woo_hbm,
     fg_hbm,
     fu_hbm,
     fd_hbm,
     do_hbm,
+    xn_ref,
+    aw_ref,
+    wo_ref,
+    cot_ref,
+    out_sem,
     full,
     qkv,
     gain_in,
@@ -692,6 +698,7 @@
         piece.start()
 
     full[:, 0:width] = tok_ref[...]
+    cot_ref[...] = (cot_in_ref[...].astype(wide) * valid_ref[...]).astype(low)
     t_copy(1).wait_recv()
     t_copy(2).start()
     attn.arrive(z ^ 1)
@@ -763,6 +770,12 @@
     for o in range(4):
         for k in others:
             row_wait(aw_ref, o, k, ay_send, ay_recv)
+    outs = [
+        pltpu.make_async_copy(src, dst, out_sem.at[i])
+        for i, (src, dst) in enumerate(((xn_ref, xn_hbm), (aw_ref, aw_hbm), (wo_ref, woo_hbm)))
+    ]
+    outs[0].start()
+    outs[1].start()
     for n in range(0, q_cols + 2 * k_cols, 512):
         qkv[:, n : n + 512] = dot_nn(xn_ref[...], aw_ref[:, n : n + 512])
 
@@ -879,6 +892,7 @@
     for o in range(4):
         for k in others:
             row_wait(wo_ref, o, k, oy_send, oy_recv)
+    outs[2].start()
     part_copy = remote(part.at[:, pl.ds(2 * width, 2 * width)], core_in, p_send, p_recv, core)
     for at, p in ((2, 1), (3, 3), (0, 0)):
         part[:, at * width : (at + 1) * width] = times_transposed(
@@ -914,7 +928,9 @@
     r_copy.wait()
 
     def add_far(r):
-        h_ref[r, :] = h_ref[r, :] + x_in[r, :].astype(wide)
+        total = h_ref[r, :] + x_in[r, :].astype(wide)
+        h_ref[r, :] = total
+        hlow_ref[r, :] = total.astype(low)
 
     tiles(rows, 64, add_far)
     for a in (1, 2):
@@ -956,6 +972,8 @@
             if j:
                 f_copy(a, j).wait_send()
     do_own.wait()
+    for out in outs:
+        out.wait()
     for j in range(4):
         dx_copy(j).wait_send()
         dc_copy(j, 0).wait()
@@ -998,24 +1016,30 @@
     return pl.pallas_call(
         attn_fwd_kernel,
         out_shape=(
-            shape((rows, model), low),
             shape((rows, 128), wide),
             shape((heads, rows, HEAD_SIZE), low),
             shape((row_size, rows, 2 * k_cols), low),
             shape((heads, rows, 128), wide),
             shape((rows, q_cols), low),
             shape((rows, width), wide),
+            shape((rows, width), low),
+            shape((8, model), wide),
+            shape((rows, model), low),
             shape((model, q_cols + 2 * k_cols), low),
             shape((model, q_cols), low),
-            shape((8, model), wide),
             shape((model, hidden), low),
             shape((model, hidden), low),
             shape((model, hidden), low),
             shape((4, rows, model), low),
         ),
         in_specs=[vmem] * 6 + [hbm] * 7,
-        out_specs=(vmem,) * 10 + (hbm,) * 4,
+        out_specs=(vmem,) * 8 + (hbm,) * 7,
         scratch_shapes=[
+            pltpu.VMEM((rows, model), low),
+            pltpu.VMEM((model, q_cols + 2 * k_cols), low),
+            pltpu.VMEM((model, q_cols), low),
+            pltpu.VMEM((rows, width), low),
+            dma((3,)),
             pltpu.VMEM((rows, model), low),
             pltpu.VMEM((rows, q_cols + 2 * k_cols), wide),
             pltpu.VMEM((4 * row_size, 8, local), wide),
@@ -1331,7 +1355,7 @@
     def grad_residual(r):
         factor = factor_two_ref[r, 0:1]
         grad = (
-            dout_ref[r, :].astype(wide)
+            dout_ref[r, :].astype(wide) * valid_ref[r, :]
             + factor * gain_two * dhn_ref[r, :]
             - residual(r) * factor * factor * factor * inner(0, r)
         ).astype(low)
@@ -2004,25 +2028,25 @@
     gains = jnp.zeros((8, gain_attn.shape[0]), wide)
     gains = gains.at[0].set(gain_attn.astype(wide)).at[1].set(gain_ffn.astype(wide))
     q_cols, k_cols = w_query.shape[1], key_matrix.shape[1]
-    grad_out = (cotangent.astype(wide) * valid).astype(low)
     (
-        normed,
         factor_one,
         query_rows,
         kv_all,
         log_total,
         mixed_heads,
         residual,
+        residual_low,
+        gains,
+        normed,
         attn_weight,
         out_weight,
-        gains,
         gate_weight,
         up_weight,
         down_weight,
         grad_out_full,
     ) = attn_fwd_call(
         tokens,
-        grad_out,
+        cotangent,
         gains,
         cosine_table,
         sine_table,
@@ -2035,9 +2059,8 @@
         w_up,
         w_down.T,
     )
-    residual_low = residual.astype(low)
     grad_normed_two, factor_two, out_part, grad_gate_part, grad_up_part, grad_down_part = ffn_call(
-        residual_low, gains[1:2], grad_out_full, gate_weight, up_weight, down_weight
+        residual_low, gains, grad_out_full, gate_weight, up_weight, down_weight
     )
     (
         layer_out,
@@ -2052,7 +2075,7 @@
         grad_normed_two,
         factor_two,
         residual,
-        grad_out,
+        cotangent,
         gains,
         tokens,
         factor_one,

time: 538 us -> 531 us (0.987)
  no operation moved by 1% of the time
where the time goes in v6:
time: 531 us
  Pallas kernels  508 us (96%)
  local copies, waits for them, and re-layouts  14.4 us (3%)
  other arithmetic  6.56 us (1%)
    pallas_call x1, Pallas kernels, attn_bwd_call(): pl.pallas_call(attn_bwd_kernel, out_shape=(shape((rows, width), low), sha...  182 us
    pallas_call x1, Pallas kernels, attn_fwd_call(): pl.pallas_call(attn_fwd_kernel, out_shape=(shape((rows, 128), wide), shap...  181 us
    pallas_call x1, Pallas kernels, ffn_call(): pl.pallas_call(ffn_kernel, out_shape=(jax.ShapeDtypeStruct((rows, width),...  146 us

profile of v6, /device:TPU:0, one launch (start us, length us, event | category | flops | bytes accessed | tf_op | source)
XLA Modules:
  0.0 530.8 jit_solution(10420583967090205521)
XLA Ops:
  1.3 0.7 reshape.107
  2.0 0.7 convert.8
  2.7 0.0 copy-start.6
  2.7 0.7 fusion.valid_ref
  3.4 1.8 copy.23
  5.2 1.8 multiply_sine_fusion
  7.0 2.3 copy.24
  9.3 0.0 copy-done.6
  9.3 180.9 %shard_map.203 = (f32[512,128]{1,0:T(8,128)}, bf16[2,512,256]{2,1,0:T(8,128)(2,1)}, bf16[2,512,512]{2,1,0:T(8,128)(2,1)}, f32[2,512,128]{2,1,0:T(8,128)}, bf16[5...) custom-call(bf16[512,512]{1,0:T(8,128)(2,1)} %tok_ref.3, ...), custom_call_target="tpu_custom_call" | custom-call | flops 10000000000 | bytes 40000000 | tf_op jit(solution)/shard_map/pallas_call | solution.py:1016
  190.2 146.0 %shard_map.204 = (f32[512,512]{1,0:T(8,128)}, f32[512,128]{1,0:T(8,128)}, bf16[4,512,2048]{2,1,0:T(8,128)(2,1)}, bf16[2048,512]{1,0:T(8,128)(2,1)}, bf16[2048,51...) custom-call(bf16[512,512]{1,0:T(8,128)(2,1)} %get-tuple-element.64.h_ref, f32[8,2048]{1,0:T(8,128)} %get-tuple-element.65.gain_ref, ...), custom_call_target="tpu_custom_call" | custom-call | flops 38654705664 | bytes 40000000 | tf_op jit(solution)/shard_map/pallas_call | solution.py:419
  336.2 181.6 %shard_map.205 = (bf16[512,512]{1,0:T(8,128)(2,1)}, bf16[512,512]{1,0:T(8,128)(2,1)}, f32[8,256]{1,0:T(8,128)}, f32[256,1024]{1,0:T(8,128)}, f32[256,512]{1,0:T(...) custom-call(f32[512,512]{1,0:T(8,128)} %get-tuple-element.70.dhn_ref, ...), custom_call_target="tpu_custom_call" | custom-call | flops 14000000000 | bytes 40000000 | tf_op jit(solution)/shard_map/pallas_call | solution.py:1893
  517.8 0.0 copy-start.3
  517.8 0.0 copy-start.2
  517.8 1.4 fusion.2
  519.2 2.0 copy.25
  521.3 1.9 slice.46
  523.1 0.0 copy-done.3
  523.1 0.0 copy-start.1
  523.1 0.8 fusion.1
  524.0 0.0 copy-done.2
  524.0 1.6 convert_element_type.33
  525.5 0.0 copy-done.1
  525.5 0.0 copy-start
  525.5 1.6 convert_element_type.34
  527.1 0.0 copy-done
  527.1 0.2 convert_bitcast_fusion
  527.3 0.0 copy-start.5
  527.4 0.0 copy-start.4
  527.4 1.8 copy.26
  529.2 0.0 copy-done.5
  529.2 0.8 copy.31
  530.0 0.0 copy-done.4
  530.0 0.8 copy.32
  (4 shorter events, 0.1 us)
Async XLA Ops:
  2.7 6.6 %copy-start.6 = (f32[8,256]{1,0:T(8,128)}, f32[8,256]{1,0:T(8,128)S(1)}, u32[]{:S(2)}) copy-start(f32[8,256]{1,0:T(8,128)S(1)} %scatter.14.gains_ref) | copy-start | bytes 24580
  517.8 5.4 %copy-start.3 = (f32[256,1024]{1,0:T(8,128)S(1)}, f32[256,1024]{1,0:T(8,128)}, u32[]{:S(2)}) copy-start(f32[256,1024]{1,0:T(8,128)} %get-tuple-element.88) | copy-start | bytes 3145732
  517.8 6.2 %copy-start.2 = (bf16[256,2048]{1,0:T(8,128)(2,1)S(1)}, bf16[256,2048]{1,0:T(8,128)(2,1)}, u32[]{:S(2)}) copy-start(bf16[256,2048]{1,0:T(8,128)(2,1)} %get-tuple-element.90) | copy-start | bytes 3145732
  523.1 2.4 copy-start.1
  525.5 1.6 copy-start
  527.3 1.8 copy-start.5
  527.4 2.6 copy-start.4
